TPU v7x, 32 devices: a whole 2x2x4 slice. The times are simulated.
32 devices in a mesh: blk: 16 (over z, y, x), fsdp: 2 (over core).
Axes of the slice: x: 2, y: 2, z: 4, core: 2. Of those that a mesh axis runs over, the one named last changes fastest.
Arguments:
- hidden_in: bfloat16 [2, 8192, 2048], P('fsdp', 'blk'), may hold values from -6 to 6
- w_query: bfloat16 [2048, 128], P('fsdp'), may hold values from -0.125 to 0.125
- query_gain: float32 [128], replicated, may hold values from 0.1 to 1.9
- key_rows: bfloat16 [2, 8192, 128], P('fsdp', 'blk'), may hold values from -4 to 4
- value_rows: bfloat16 [2, 8192, 128], P('fsdp', 'blk'), may hold values from -6 to 6
- grad_out: bfloat16 [2, 8192, 128], P('fsdp', 'blk'), may hold values from -6 to 6
- logsumexp: float32 [2, 8192], P('fsdp', 'blk'), may hold values from 4 to 8
- row_delta: float32 [2, 8192], P('fsdp', 'blk'), may hold values from -6 to 6
- doc_ids: int32 [2, 8192], P('fsdp', 'blk'), may hold values from 0 to 7, never falling along the last dimension, each value on 1 to 4096 neighbouring positions
Outputs:
- grad_hidden: bfloat16 [2, 8192, 2048], P('fsdp', 'blk')
- grad_keys: bfloat16 [2, 8192, 128], P('fsdp', 'blk')
- grad_values: bfloat16 [2, 8192, 128], P('fsdp', 'blk')
- grad_wquery: float32 [2048, 128], P('fsdp')
Inputs may be any that keep to these rules, and one draw needn't show every extreme that they name: `doc_ids`: along each sequence the document numbers never fall; each document has 1 to 4096 tokens.
All inputs are finite; a program needn't handle non-finite values.
Results may differ from a plain program's by a relative error of at most 0.0097.
Values may be sent and summed in bfloat16 or wider, within the bound.
No kernel may reach another device: no remote copies, remote signals or barrier semaphores. Data moves between devices by JAX's collectives and lax.ppermute only.
A program may use at most 64 MiB of HBM per device.

v0:
```python
import jax
import jax.numpy as jnp
from jax import lax
from jax.sharding import PartitionSpec as P

ROUNDS = 8


def passed_along(value, axis, by):
    size = lax.axis_size(axis)
    pairs = [(i, i + by) for i in range(size) if 0 <= i + by < size]
    return lax.ppermute(value, axis, pairs)


def from_behind(value, axis, by):
    size = lax.axis_size(axis)
    return lax.ppermute(value, axis, [(i, (i + by) % size) for i in range(size)])


def local(
    hidden_in, w_query, query_gain, key_rows, value_rows, grad_out, logsumexp, row_delta, doc_ids
):
    inputs = hidden_in[0]
    own_keys = key_rows[0]
    own_values = value_rows[0]
    outgrad = grad_out[0]
    own_lse = logsumexp[0]
    own_delta = row_delta[0]
    own_docs = doc_ids[0].astype(jnp.float32)
    tokens = own_keys.shape[0]
    width = own_keys.shape[1]
    score_scale = width ** (-0.5)
    position = lax.axis_index("blk")
    lower_tri = jnp.arange(tokens)[:, None] >= jnp.arange(tokens)[None, :]
    projection = lax.all_gather(w_query, "fsdp", axis=0, tiled=True)
    q_pre = jnp.dot(inputs, projection, preferred_element_type=jnp.float32)
    inverse = lax.rsqrt(jnp.mean(q_pre * q_pre, axis=-1, keepdims=True) + 1e-06)
    normed = q_pre * inverse
    query = (normed * query_gain).astype(jnp.bfloat16)
    zeros_rows = jnp.zeros((tokens, width), jnp.float32)
    key_pair = jnp.stack([own_keys, own_values])
    keys_acc, values_acc, docs_far = (zeros_rows, zeros_rows, own_docs)
    query_acc = zeros_rows
    for turn in range(ROUNDS):
        if turn > 0:
            key_pair = passed_along(key_pair, "blk", 1)
            keys_acc, values_acc, docs_far = from_behind((keys_acc, values_acc, docs_far), "blk", 1)
        in_range = position - turn >= 0
        k_block = key_pair[0]
        allowed = (own_docs[:, None] == docs_far[None, :]) & in_range
        if turn == 0:
            allowed = allowed & lower_tri
        scores = (
            lax.dot_general(
                query, k_block, (((1,), (1,)), ((), ())), preferred_element_type=jnp.float32
            )
            * score_scale
        )
        attn_prob = jnp.exp(jnp.where(allowed, scores - own_lse[:, None], -1e30))
        grad_prob = lax.dot_general(
            outgrad, key_pair[1], (((1,), (1,)), ((), ())), preferred_element_type=jnp.float32
        )
        grad_score = attn_prob * (grad_prob - own_delta[:, None])
        prob_half = attn_prob.astype(jnp.bfloat16)
        score_half = grad_score.astype(jnp.bfloat16)
        query_term = jnp.dot(score_half, k_block, preferred_element_type=jnp.float32)
        key_term = lax.dot_general(
            score_half, query, (((0,), (0,)), ((), ())), preferred_element_type=jnp.float32
        )
        value_term = lax.dot_general(
            prob_half, outgrad, (((0,), (0,)), ((), ())), preferred_element_type=jnp.float32
        )
        query_term, key_term, value_term = (query_term, key_term, value_term)
        query_acc = query_acc + query_term
        keys_acc = keys_acc + key_term
        values_acc = values_acc + value_term
    keys_acc, values_acc = from_behind((keys_acc, values_acc), "blk", 1 - ROUNDS)
    grad_query = query_acc * score_scale
    grad_keys = (keys_acc * score_scale).astype(jnp.bfloat16)
    grad_values = values_acc.astype(jnp.bfloat16)
    scaled = grad_query * query_gain
    grad_pre = (
        inverse * (scaled - normed * jnp.mean(scaled * normed, axis=-1, keepdims=True))
    ).astype(jnp.bfloat16)
    grad_hidden = lax.dot_general(
        grad_pre, projection, (((1,), (1,)), ((), ())), preferred_element_type=jnp.float32
    )
    weight_term = lax.dot_general(
        inputs, grad_pre, (((0,), (0,)), ((), ())), preferred_element_type=jnp.float32
    )
    owned_terms = lax.psum_scatter(weight_term, "fsdp", scatter_dimension=0, tiled=True)
    grad_wquery = lax.psum(owned_terms, "blk")
    return (grad_hidden.astype(jnp.bfloat16)[None], grad_keys[None], grad_values[None], grad_wquery)


def solution(mesh):
    return jax.shard_map(
        local,
        mesh=mesh,
        in_specs=(
            P("fsdp", "blk", None),
            P("fsdp", None),
            P(),
            P("fsdp", "blk", None),
            P("fsdp", "blk", None),
            P("fsdp", "blk", None),
            P("fsdp", "blk"),
            P("fsdp", "blk"),
            P("fsdp", "blk"),
        ),
        out_specs=(
            P("fsdp", "blk", None),
            P("fsdp", "blk", None),
            P("fsdp", "blk", None),
            P("fsdp", None),
        ),
        check_vma=False,
    )
```

profile of v0, /device:TPU:0, one launch (start us, length us, event | category | flops | bytes accessed | tf_op | source)
XLA Modules:
  0.0 300.4 jit_solution(11042038270078718164)
XLA Ops:
  8.1 3.0 collective-permute-start
  11.1 2.4 all_gather.3
  16.2 1.5 collective-permute-start.22
  17.7 1.5 collective-permute-start.2
  20.0 4.1 %collective-permute-start.1 = (bf16[2,512,128]{2,1,0:T(8,128)(2,1)}, bf16[2,512,128]{2,1,0:T(8,128)(2,1)}, u32[]{:S(2)}, u32[]{:S(2)}) collective-permute-start(bf16[2,512,128]{2,1,0:T(8,128)(2,1)} %pad_maximum_fusion), channel_id=1, source_target_pairs={{0,2},{2,4},{4,6},{6,8},{8,10},{10,12},{12,14},{14,16},{16,18},{18... | collective-permute-start | bytes 786440 | tf_op jit(solution)/shard_map/ppermute | solution.py:12
  24.1 4.4 %collective-permute-done.2 = f32[512]{0:T(512)S(1)} collective-permute-done((f32[512]{0:T(512)S(1)}, f32[512]{0:T(512)S(1)}, u32[]{:S(2)}, u32[]{:S(2)}) %collective-permute-start.2) | collective-permute-done | bytes 2080 | tf_op jit(solution)/shard_map/ppermute | solution.py:17
  28.8 6.9 %collective-permute-done.4 = f32[512]{0:T(512)S(1)} collective-permute-done((f32[512]{0:T(512)S(1)}, f32[512]{0:T(512)S(1)}, u32[]{:S(2)}, u32[]{:S(2)}) %collective-permute-start.4) | collective-permute-done | bytes 2080 | tf_op jit(solution)/shard_map/ppermute | solution.py:17
  36.8 6.1 %collective-permute-done.6 = f32[512]{0:T(512)S(1)} collective-permute-done((f32[512]{0:T(512)S(1)}, f32[512]{0:T(512)S(1)}, u32[]{:S(2)}, u32[]{:S(2)}) %collective-permute-start.6) | collective-permute-done | bytes 2080 | tf_op jit(solution)/shard_map/ppermute | solution.py:17
  43.5 6.7 %collective-permute-done.8 = f32[512]{0:T(512)} collective-permute-done((f32[512]{0:T(512)S(1)}, f32[512]{0:T(512)}, u32[]{:S(2)}, u32[]{:S(2)}) %collective-permute-start.8) | collective-permute-done | bytes 2080 | tf_op jit(solution)/shard_map/ppermute | solution.py:17
  50.3 7.4 %collective-permute-done.10 = f32[512]{0:T(512)S(1)} collective-permute-done((f32[512]{0:T(512)}, f32[512]{0:T(512)S(1)}, u32[]{:S(2)}, u32[]{:S(2)}) %collective-permute-start.10) | collective-permute-done | bytes 2080 | tf_op jit(solution)/shard_map/ppermute | solution.py:17
  57.6 1.2 fusion.15
  58.9 1.5 convolution_add_fusion
  60.5 1.3 collective-permute-start.3
  61.8 1.4 fusion.35
  63.2 1.3 convolution_add_fusion.1
  64.6 1.2 convolution_add_fusion.8
  65.8 7.1 %collective-permute-done.3 = bf16[2,512,128]{2,1,0:T(8,128)(2,1)S(1)} collective-permute-done((bf16[2,512,128]{2,1,0:T(8,128)(2,1)}, bf16[2,512,128]{2,1,0:T(8,128)(2,1)S(1)}, u32[]{:S(2)}, u32[]{:S(2)}) %collective-permute-start.3) | collective-permute-done | bytes 262176 | tf_op jit(solution)/shard_map/ppermute | solution.py:12
  73.2 1.3 fusion.73
  74.5 2.4 collective-permute-start.24
  76.9 1.9 collective-permute-start.5
  79.7 1.3 collective-permute-start.16
  81.3 8.3 %collective-permute-done.5 = bf16[2,512,128]{2,1,0:T(8,128)(2,1)S(1)} collective-permute-done((bf16[2,512,128]{2,1,0:T(8,128)(2,1)S(1)}, bf16[2,512,128]{2,1,0:T(8,128)(2,1)S(1)}, u32[]{:S(2)}, u32[]{:S(2)}) %collective-permute-start.5) | collective-permute-done | bytes 262176 | tf_op jit(solution)/shard_map/ppermute | solution.py:12
  90.0 4.4 %collective-permute-start.7 = (bf16[2,512,128]{2,1,0:T(8,128)(2,1)S(1)}, bf16[2,512,128]{2,1,0:T(8,128)(2,1)S(1)}, u32[]{:S(2)}, u32[]{:S(2)}) collective-permute-start(bf16[2,512,128]{2,1,0:T(8,128)(2,1)S(1)} %collective-permute-done.5), channel_id=1, source_target_pairs={{0,2},{2,4},{4,6},{6,8},{8,10},{10,12},{12,14},{14,16},{16,18},{18... | collective-permute-start | bytes 786440 | tf_op jit(solution)/shard_map/ppermute | solution.py:12
  96.0 2.5 collective-permute-start.17
  98.8 2.0 collective-permute-done.7
  101.2 4.4 %collective-permute-start.9 = (bf16[2,512,128]{2,1,0:T(8,128)(2,1)S(1)}, bf16[2,512,128]{2,1,0:T(8,128)(2,1)S(1)}, u32[]{:S(2)}, u32[]{:S(2)}) collective-permute-start(bf16[2,512,128]{2,1,0:T(8,128)(2,1)S(1)} %collective-permute-done.7), channel_id=1, source_target_pairs={{0,2},{2,4},{4,6},{6,8},{8,10},{10,12},{12,14},{14,16},{16,18},{18... | collective-permute-start | bytes 786440 | tf_op jit(solution)/shard_map/ppermute | solution.py:12
  106.4 4.8 %collective-permute-done.9 = bf16[2,512,128]{2,1,0:T(8,128)(2,1)S(1)} collective-permute-done((bf16[2,512,128]{2,1,0:T(8,128)(2,1)S(1)}, bf16[2,512,128]{2,1,0:T(8,128)(2,1)S(1)}, u32[]{:S(2)}, u32[]{:S(2)}) %collective-permute-start.9) | collective-permute-done | bytes 262176 | tf_op jit(solution)/shard_map/ppermute | solution.py:12
  111.5 4.4 %collective-permute-start.11 = (bf16[2,512,128]{2,1,0:T(8,128)(2,1)S(1)}, bf16[2,512,128]{2,1,0:T(8,128)(2,1)S(1)}, u32[]{:S(2)}, u32[]{:S(2)}) collective-permute-start(bf16[2,512,128]{2,1,0:T(8,128)(2,1)S(1)} %collective-permute-done.9), channel_id=1, source_target_pairs={{0,2},{2,4},{4,6},{6,8},{8,10},{10,12},{12,14},{14,16},{16,18},{18... | collective-permute-start | bytes 786440 | tf_op jit(solution)/shard_map/ppermute | solution.py:12
  117.4 3.3 %collective-permute-done.11 = bf16[2,512,128]{2,1,0:T(8,128)(2,1)S(1)} collective-permute-done((bf16[2,512,128]{2,1,0:T(8,128)(2,1)S(1)}, bf16[2,512,128]{2,1,0:T(8,128)(2,1)S(1)}, u32[]{:S(2)}, u32[]{:S(2)}) %collective-permute-start.11) | collective-permute-done | bytes 262176 | tf_op jit(solution)/shard_map/ppermute | solution.py:12
  121.0 4.6 %collective-permute-start.13 = (bf16[2,512,128]{2,1,0:T(8,128)(2,1)S(1)}, bf16[2,512,128]{2,1,0:T(8,128)(2,1)S(1)}, u32[]{:S(2)}, u32[]{:S(2)}) collective-permute-start(bf16[2,512,128]{2,1,0:T(8,128)(2,1)S(1)} %collective-permute-done.11), channel_id=1, source_target_pairs={{0,2},{2,4},{4,6},{6,8},{8,10},{10,12},{12,14},{14,16},{16,18},{18... | collective-permute-start | bytes 786440 | tf_op jit(solution)/shard_map/ppermute | solution.py:12
  126.4 5.6 %collective-permute-done.13 = bf16[2,512,128]{2,1,0:T(8,128)(2,1)S(1)} collective-permute-done((bf16[2,512,128]{2,1,0:T(8,128)(2,1)S(1)}, bf16[2,512,128]{2,1,0:T(8,128)(2,1)S(1)}, u32[]{:S(2)}, u32[]{:S(2)}) %collective-permute-start.13) | collective-permute-done | bytes 262176 | tf_op jit(solution)/shard_map/ppermute | solution.py:12
  133.6 1.4 convolution_bitcast_fusion
  135.1 1.9 fusion.68
  137.0 2.5 collective-permute-start.25
  141.0 3.1 %collective-permute-start.18 = (f32[512,128]{1,0:T(8,128)S(1)}, f32[512,128]{1,0:T(8,128)S(1)}, u32[]{:S(2)}, u32[]{:S(2)}) collective-permute-start(f32[512,128]{1,0:T(8,128)S(1)} %add.97), channel_id=1, source_target_pairs={{0,2},{2,4},{4,6},{6,8},{8,10},{10,12},{12,14},{14,16},{16,18},{18... | collective-permute-start | bytes 786440 | tf_op jit(solution)/shard_map/ppermute | solution.py:17
  144.2 8.3 %collective-permute-done.25 = f32[512,128]{1,0:T(8,128)S(1)} collective-permute-done((f32[512,128]{1,0:T(8,128)S(1)}, f32[512,128]{1,0:T(8,128)S(1)}, u32[]{:S(2)}, u32[]{:S(2)}) %collective-permute-start.25) | collective-permute-done | bytes 262176 | tf_op jit(solution)/shard_map/ppermute | solution.py:17
  153.4 2.7 collective-permute-done.18
  156.2 8.7 %collective-permute-done.26 = f32[512,128]{1,0:T(8,128)S(1)} collective-permute-done((f32[512,128]{1,0:T(8,128)S(1)}, f32[512,128]{1,0:T(8,128)S(1)}, u32[]{:S(2)}, u32[]{:S(2)}) %collective-permute-start.26) | collective-permute-done | bytes 262176 | tf_op jit(solution)/shard_map/ppermute | solution.py:17
  166.5 4.1 %collective-permute-done.19 = f32[512,128]{1,0:T(8,128)S(1)} collective-permute-done((f32[512,128]{1,0:T(8,128)S(1)}, f32[512,128]{1,0:T(8,128)S(1)}, u32[]{:S(2)}, u32[]{:S(2)}) %collective-permute-start.19) | collective-permute-done | bytes 262176 | tf_op jit(solution)/shard_map/ppermute | solution.py:17
  170.7 7.5 %collective-permute-done.27 = f32[512,128]{1,0:T(8,128)S(1)} collective-permute-done((f32[512,128]{1,0:T(8,128)S(1)}, f32[512,128]{1,0:T(8,128)S(1)}, u32[]{:S(2)}, u32[]{:S(2)}) %collective-permute-start.27) | collective-permute-done | bytes 262176 | tf_op jit(solution)/shard_map/ppermute | solution.py:17
  179.2 1.8 collective-permute-done.20
  181.2 7.8 %collective-permute-done.28 = f32[512,128]{1,0:T(8,128)} collective-permute-done((f32[512,128]{1,0:T(8,128)S(1)}, f32[512,128]{1,0:T(8,128)}, u32[]{:S(2)}, u32[]{:S(2)}) %collective-permute-start.28) | collective-permute-done | bytes 262176 | tf_op jit(solution)/shard_map/ppermute | solution.py:17
  189.0 1.8 fusion.48
  190.9 2.1 fusion
  193.0 6.2 %collective-permute-done.29 = bf16[512,128]{1,0:T(8,128)(2,1)S(1)} collective-permute-done((bf16[512,128]{1,0:T(8,128)(2,1)S(1)}, bf16[512,128]{1,0:T(8,128)(2,1)S(1)}, u32[]{:S(2)}, u32[]{:S(2)}) %collective-permute-start.29) | collective-permute-done | bytes 131104 | tf_op jit(solution)/shard_map/ppermute | solution.py:17
  199.2 1.6 fusion.107
  200.8 90.0 %all-reduce.2.cloned.1.call-done = f32[1024,128]{0,1:T(8,128)} async-done(((f32[1024,128]{0,1:T(8,128)}), f32[1024,128]{0,1:T(8,128)}) %all-reduce.2.cloned.1.call-update) | async-done | bytes 524304 | tf_op jit(solution)/shard_map/psum | solution.py:92
  290.8 2.0 copy.20
  (150 shorter events, 21.7 us)
Async XLA Ops:
  7.2 174.0 %reduce-scatter.2.cloned.1.call-start = ((), (), s32[]{:S(2)}) async-start(), calls=%async_computation.1 | async-start | bytes 1572864 | tf_op jit(solution)/shard_map/reduce_scatter | solution.py:91
  8.1 9.7 %collective-permute-start = (f32[512]{0:T(512)S(1)}, f32[512]{0:T(512)S(1)}, u32[]{:S(2)}, u32[]{:S(2)}) collective-permute-start(f32[512]{0:T(512)S(1)} %bitcast.198), channel_id=1, source_target_pairs={{0,2},{2,4},{4,6},{6,8},{8,10},{10,12},{12,14},{14,16},{16,18},{18... | collective-permute-start | bytes 6152 | tf_op jit(solution)/shard_map/ppermute | solution.py:17
  14.4 14.1 %copy-start.30 = (f32[1,512]{1,0:T(1,128)S(1)}, f32[1,512]{1,0:T(1,128)}, u32[]{:S(2)}) copy-start(f32[1,512]{1,0:T(1,128)} %param.16) | copy-start | bytes 6148
  16.2 34.0 %copy-start.33 = (f32[128]{0:T(128)S(1)}, f32[128]{0:T(128)}, u32[]{:S(2)}) copy-start(f32[128]{0:T(128)} %param.11) | copy-start | bytes 1540
  16.2 42.6 %collective-permute-start.22 = (f32[512,128]{1,0:T(8,128)}, f32[512,128]{1,0:T(8,128)}, u32[]{:S(2)}, u32[]{:S(2)}) collective-permute-start(f32[512,128]{1,0:T(8,128)} %fusion.77), channel_id=1, source_target_pairs={{0,2},{2,4},{4,6},{6,8},{8,10},{10,12},{12,14},{14,16},{16,18},{18... | collective-permute-start | bytes 786440 | tf_op jit(solution)/shard_map/ppermute | solution.py:17
  17.7 10.8 %collective-permute-start.2 = (f32[512]{0:T(512)S(1)}, f32[512]{0:T(512)S(1)}, u32[]{:S(2)}, u32[]{:S(2)}) collective-permute-start(f32[512]{0:T(512)S(1)} %collective-permute-done), channel_id=1, source_target_pairs={{0,2},{2,4},{4,6},{6,8},{8,10},{10,12},{12,14},{14,16},{16,18},{18... | collective-permute-start | bytes 6152 | tf_op jit(solution)/shard_map/ppermute | solution.py:17
  20.0 37.7 %collective-permute-start.1 = (bf16[2,512,128]{2,1,0:T(8,128)(2,1)}, bf16[2,512,128]{2,1,0:T(8,128)(2,1)}, u32[]{:S(2)}, u32[]{:S(2)}) collective-permute-start(bf16[2,512,128]{2,1,0:T(8,128)(2,1)} %pad_maximum_fusion), channel_id=1, source_target_pairs={{0,2},{2,4},{4,6},{6,8},{8,10},{10,12},{12,14},{14,16},{16,18},{18... | collective-permute-start | bytes 786440 | tf_op jit(solution)/shard_map/ppermute | solution.py:12
  28.5 14.4 %copy-start.27 = (f32[512]{0:T(512)}, f32[512]{0:T(512)S(1)}, u32[]{:S(2)}) copy-start(f32[512]{0:T(512)S(1)} %collective-permute-done.2) | copy-start | bytes 6148
  28.5 7.2 %collective-permute-start.4 = (f32[512]{0:T(512)S(1)}, f32[512]{0:T(512)S(1)}, u32[]{:S(2)}, u32[]{:S(2)}) collective-permute-start(f32[512]{0:T(512)S(1)} %collective-permute-done.2), channel_id=1, source_target_pairs={{0,2},{2,4},{4,6},{6,8},{8,10},{10,12},{12,14},{14,16},{16,18},{18... | collective-permute-start | bytes 6152 | tf_op jit(solution)/shard_map/ppermute | solution.py:17
  35.7 7.2 %collective-permute-start.6 = (f32[512]{0:T(512)S(1)}, f32[512]{0:T(512)S(1)}, u32[]{:S(2)}, u32[]{:S(2)}) collective-permute-start(f32[512]{0:T(512)S(1)} %collective-permute-done.4), channel_id=1, source_target_pairs={{0,2},{2,4},{4,6},{6,8},{8,10},{10,12},{12,14},{14,16},{16,18},{18... | collective-permute-start | bytes 6152 | tf_op jit(solution)/shard_map/ppermute | solution.py:17
  36.8 26.4 %collective-permute-start.14 = (f32[512,128]{1,0:T(8,128)}, f32[512,128]{1,0:T(8,128)}, u32[]{:S(2)}, u32[]{:S(2)}) collective-permute-start(f32[512,128]{1,0:T(8,128)} %fusion.135), channel_id=1, source_target_pairs={{0,2},{2,4},{4,6},{6,8},{8,10},{10,12},{12,14},{14,16},{16,18},{18... | collective-permute-start | bytes 786440 | tf_op jit(solution)/shard_map/ppermute | solution.py:17
  42.9 7.3 %collective-permute-start.8 = (f32[512]{0:T(512)S(1)}, f32[512]{0:T(512)}, u32[]{:S(2)}, u32[]{:S(2)}) collective-permute-start(f32[512]{0:T(512)S(1)} %collective-permute-done.6), channel_id=1, source_target_pairs={{0,2},{2,4},{4,6},{6,8},{8,10},{10,12},{12,14},{14,16},{16,18},{18... | collective-permute-start | bytes 6152 | tf_op jit(solution)/shard_map/ppermute | solution.py:17
  50.2 7.4 %collective-permute-start.10 = (f32[512]{0:T(512)}, f32[512]{0:T(512)S(1)}, u32[]{:S(2)}, u32[]{:S(2)}) collective-permute-start(f32[512]{0:T(512)} %collective-permute-done.8), channel_id=1, source_target_pairs={{0,2},{2,4},{4,6},{6,8},{8,10},{10,12},{12,14},{14,16},{16,18},{18... | collective-permute-start | bytes 6152 | tf_op jit(solution)/shard_map/ppermute | solution.py:17
  57.6 74.7 %collective-permute-start.12 = (f32[512]{0:T(512)S(1)}, f32[512]{0:T(512)S(1)}, u32[]{:S(2)}, u32[]{:S(2)}) collective-permute-start(f32[512]{0:T(512)S(1)} %collective-permute-done.10), channel_id=1, source_target_pairs={{0,2},{2,4},{4,6},{6,8},{8,10},{10,12},{12,14},{14,16},{16,18},{18... | collective-permute-start | bytes 6152 | tf_op jit(solution)/shard_map/ppermute | solution.py:17
  60.4 12.8 %collective-permute-start.23 = (f32[512,128]{1,0:T(8,128)S(1)}, f32[512,128]{1,0:T(8,128)S(1)}, u32[]{:S(2)}, u32[]{:S(2)}) collective-permute-start(f32[512,128]{1,0:T(8,128)S(1)} %convolution_add_fusion), channel_id=1, source_target_pairs={{0,2},{2,4},{4,6},{6,8},{8,10},{10,12},{12,14},{14,16},{16,18},{18... | collective-permute-start | bytes 786440 | tf_op jit(solution)/shard_map/ppermute | solution.py:17
  60.5 12.4 %collective-permute-start.3 = (bf16[2,512,128]{2,1,0:T(8,128)(2,1)}, bf16[2,512,128]{2,1,0:T(8,128)(2,1)S(1)}, u32[]{:S(2)}, u32[]{:S(2)}) collective-permute-start(bf16[2,512,128]{2,1,0:T(8,128)(2,1)} %collective-permute-done.1), channel_id=1, source_target_pairs={{0,2},{2,4},{4,6},{6,8},{8,10},{10,12},{12,14},{14,16},{16,18},{18... | collective-permute-start | bytes 786440 | tf_op jit(solution)/shard_map/ppermute | solution.py:12
  63.2 10.1 %copy-start.28 = (f32[512]{0:T(512)S(1)}, f32[512]{0:T(512)}, u32[]{:S(2)}) copy-start(f32[512]{0:T(512)} %copy-done.27) | copy-start | bytes 6148
  64.5 14.3 %copy-start.31 = (f32[1,512]{1,0:T(1,128)S(1)}, f32[1,512]{1,0:T(1,128)}, u32[]{:S(2)}) copy-start(f32[1,512]{1,0:T(1,128)} %param.16) | copy-start | bytes 6148
  64.5 15.1 %collective-permute-start.15 = (f32[512,128]{1,0:T(8,128)S(1)}, f32[512,128]{1,0:T(8,128)S(1)}, u32[]{:S(2)}, u32[]{:S(2)}) collective-permute-start(f32[512,128]{1,0:T(8,128)S(1)} %convolution_add_fusion.1), channel_id=1, source_target_pairs={{0,2},{2,4},{4,6},{6,8},{8,10},{10,12},{12,14},{14,16},{16,18},{18... | collective-permute-start | bytes 786440 | tf_op jit(solution)/shard_map/ppermute | solution.py:17
  74.5 60.6 %collective-permute-start.24 = (f32[512,128]{1,0:T(8,128)}, f32[512,128]{1,0:T(8,128)}, u32[]{:S(2)}, u32[]{:S(2)}) collective-permute-start(f32[512,128]{1,0:T(8,128)} %fusion.73), channel_id=1, source_target_pairs={{0,2},{2,4},{4,6},{6,8},{8,10},{10,12},{12,14},{14,16},{16,18},{18... | collective-permute-start | bytes 786440 | tf_op jit(solution)/shard_map/ppermute | solution.py:17
  76.9 12.7 %collective-permute-start.5 = (bf16[2,512,128]{2,1,0:T(8,128)(2,1)S(1)}, bf16[2,512,128]{2,1,0:T(8,128)(2,1)S(1)}, u32[]{:S(2)}, u32[]{:S(2)}) collective-permute-start(bf16[2,512,128]{2,1,0:T(8,128)(2,1)S(1)} %collective-permute-done.3), channel_id=1, source_target_pairs={{0,2},{2,4},{4,6},{6,8},{8,10},{10,12},{12,14},{14,16},{16,18},{18... | collective-permute-start | bytes 786440 | tf_op jit(solution)/shard_map/ppermute | solution.py:12
  79.3 15.1 %copy-start.25 = (f32[512]{0:T(512)S(1)}, f32[512]{0:T(512)}, u32[]{:S(2)}) copy-start(f32[512]{0:T(512)} %copy-done.24) | copy-start | bytes 6148
  79.7 15.6 %collective-permute-start.16 = (f32[512,128]{1,0:T(8,128)S(1)}, f32[512,128]{1,0:T(8,128)S(1)}, u32[]{:S(2)}, u32[]{:S(2)}) collective-permute-start(f32[512,128]{1,0:T(8,128)S(1)} %add.95), channel_id=1, source_target_pairs={{0,2},{2,4},{4,6},{6,8},{8,10},{10,12},{12,14},{14,16},{16,18},{18... | collective-permute-start | bytes 786440 | tf_op jit(solution)/shard_map/ppermute | solution.py:17
  90.0 10.8 %collective-permute-start.7 = (bf16[2,512,128]{2,1,0:T(8,128)(2,1)S(1)}, bf16[2,512,128]{2,1,0:T(8,128)(2,1)S(1)}, u32[]{:S(2)}, u32[]{:S(2)}) collective-permute-start(bf16[2,512,128]{2,1,0:T(8,128)(2,1)S(1)} %collective-permute-done.5), channel_id=1, source_target_pairs={{0,2},{2,4},{4,6},{6,8},{8,10},{10,12},{12,14},{14,16},{16,18},{18... | collective-permute-start | bytes 786440 | tf_op jit(solution)/shard_map/ppermute | solution.py:12
  94.8 10.7 %copy-start.22 = (f32[512]{0:T(512)S(1)}, f32[512]{0:T(512)}, u32[]{:S(2)}) copy-start(f32[512]{0:T(512)} %copy-done.21) | copy-start | bytes 6148
  96.0 43.9 %collective-permute-start.17 = (f32[512,128]{1,0:T(8,128)}, f32[512,128]{1,0:T(8,128)}, u32[]{:S(2)}, u32[]{:S(2)}) collective-permute-start(f32[512,128]{1,0:T(8,128)} %add.96), channel_id=1, source_target_pairs={{0,2},{2,4},{4,6},{6,8},{8,10},{10,12},{12,14},{14,16},{16,18},{18... | collective-permute-start | bytes 786440 | tf_op jit(solution)/shard_map/ppermute | solution.py:17
  101.2 10.0 %collective-permute-start.9 = (bf16[2,512,128]{2,1,0:T(8,128)(2,1)S(1)}, bf16[2,512,128]{2,1,0:T(8,128)(2,1)S(1)}, u32[]{:S(2)}, u32[]{:S(2)}) collective-permute-start(bf16[2,512,128]{2,1,0:T(8,128)(2,1)S(1)} %collective-permute-done.7), channel_id=1, source_target_pairs={{0,2},{2,4},{4,6},{6,8},{8,10},{10,12},{12,14},{14,16},{16,18},{18... | collective-permute-start | bytes 786440 | tf_op jit(solution)/shard_map/ppermute | solution.py:12
  111.5 9.1 %collective-permute-start.11 = (bf16[2,512,128]{2,1,0:T(8,128)(2,1)S(1)}, bf16[2,512,128]{2,1,0:T(8,128)(2,1)S(1)}, u32[]{:S(2)}, u32[]{:S(2)}) collective-permute-start(bf16[2,512,128]{2,1,0:T(8,128)(2,1)S(1)} %collective-permute-done.9), channel_id=1, source_target_pairs={{0,2},{2,4},{4,6},{6,8},{8,10},{10,12},{12,14},{14,16},{16,18},{18... | collective-permute-start | bytes 786440 | tf_op jit(solution)/shard_map/ppermute | solution.py:12
  121.0 11.3 %copy-start.2 = (f32[512,512]{1,0:T(8,128)}, f32[512,512]{1,0:T(8,128)S(1)}, u32[]{:S(2)}) copy-start(f32[512,512]{1,0:T(8,128)S(1)} %fusion.25) | copy-start | bytes 3145732
  121.0 11.0 %collective-permute-start.13 = (bf16[2,512,128]{2,1,0:T(8,128)(2,1)S(1)}, bf16[2,512,128]{2,1,0:T(8,128)(2,1)S(1)}, u32[]{:S(2)}, u32[]{:S(2)}) collective-permute-start(bf16[2,512,128]{2,1,0:T(8,128)(2,1)S(1)} %collective-permute-done.11), channel_id=1, source_target_pairs={{0,2},{2,4},{4,6},{6,8},{8,10},{10,12},{12,14},{14,16},{16,18},{18... | collective-permute-start | bytes 786440 | tf_op jit(solution)/shard_map/ppermute | solution.py:12
  135.0 17.4 %copy-start.23 = (f32[512]{0:T(512)S(1)}, f32[512]{0:T(512)}, u32[]{:S(2)}) copy-start(f32[512]{0:T(512)} %copy-done.21) | copy-start | bytes 6148
  135.1 155.8 %all-reduce.2.cloned.1.call-start = ((), (), s32[]{:S(2)}) async-start(), calls=%async_computation.2 | async-start | bytes 1048576 | tf_op jit(solution)/shard_map/psum | solution.py:92
  135.1 17.3 %copy-start.8 = (f32[512,512]{1,0:T(8,128)S(1)}, f32[512,512]{1,0:T(8,128)}, u32[]{:S(2)}) copy-start(f32[512,512]{1,0:T(8,128)} %copy-done.7) | copy-start | bytes 3145732
  137.0 16.0 %copy-start.14 = (bf16[512,512]{1,0:T(8,128)(2,1)S(1)}, bf16[512,512]{1,0:T(8,128)(2,1)}, u32[]{:S(2)}) copy-start(bf16[512,512]{1,0:T(8,128)(2,1)} %copy-done.13) | copy-start | bytes 1572868
  137.0 15.4 %collective-permute-start.25 = (f32[512,128]{1,0:T(8,128)S(1)}, f32[512,128]{1,0:T(8,128)S(1)}, u32[]{:S(2)}, u32[]{:S(2)}) collective-permute-start(f32[512,128]{1,0:T(8,128)S(1)} %fusion.68), channel_id=1, source_target_pairs={{0,2},{2,4},{4,6},{6,8},{8,10},{10,12},{12,14},{14,16},{16,18},{18... | collective-permute-start | bytes 786440 | tf_op jit(solution)/shard_map/ppermute | solution.py:17
  139.9 25.0 %copy-start.5 = (f32[512,512]{1,0:T(8,128)S(1)}, f32[512,512]{1,0:T(8,128)}, u32[]{:S(2)}) copy-start(f32[512,512]{1,0:T(8,128)} %copy-done.4) | copy-start | bytes 3145732
  141.0 15.0 %collective-permute-start.18 = (f32[512,128]{1,0:T(8,128)S(1)}, f32[512,128]{1,0:T(8,128)S(1)}, u32[]{:S(2)}, u32[]{:S(2)}) collective-permute-start(f32[512,128]{1,0:T(8,128)S(1)} %add.97), channel_id=1, source_target_pairs={{0,2},{2,4},{4,6},{6,8},{8,10},{10,12},{12,14},{14,16},{16,18},{18... | collective-permute-start | bytes 786440 | tf_op jit(solution)/shard_map/ppermute | solution.py:17
  153.0 13.2 %copy-start.12 = (bf16[512,512]{1,0:T(8,128)(2,1)S(1)}, bf16[512,512]{1,0:T(8,128)(2,1)}, u32[]{:S(2)}) copy-start(bf16[512,512]{1,0:T(8,128)(2,1)} %copy-done.11) | copy-start | bytes 1572868
  153.0 11.9 %collective-permute-start.26 = (f32[512,128]{1,0:T(8,128)S(1)}, f32[512,128]{1,0:T(8,128)S(1)}, u32[]{:S(2)}, u32[]{:S(2)}) collective-permute-start(f32[512,128]{1,0:T(8,128)S(1)} %fusion.63), channel_id=1, source_target_pairs={{0,2},{2,4},{4,6},{6,8},{8,10},{10,12},{12,14},{14,16},{16,18},{18... | collective-permute-start | bytes 786440 | tf_op jit(solution)/shard_map/ppermute | solution.py:17
  153.4 24.9 %copy-start.3 = (f32[512,512]{1,0:T(8,128)S(1)}, f32[512,512]{1,0:T(8,128)}, u32[]{:S(2)}) copy-start(f32[512,512]{1,0:T(8,128)} %copy-done.2) | copy-start | bytes 3145732
  156.1 14.5 %collective-permute-start.19 = (f32[512,128]{1,0:T(8,128)S(1)}, f32[512,128]{1,0:T(8,128)S(1)}, u32[]{:S(2)}, u32[]{:S(2)}) collective-permute-start(f32[512,128]{1,0:T(8,128)S(1)} %add.98), channel_id=1, source_target_pairs={{0,2},{2,4},{4,6},{6,8},{8,10},{10,12},{12,14},{14,16},{16,18},{18... | collective-permute-start | bytes 786440 | tf_op jit(solution)/shard_map/ppermute | solution.py:17
  166.1 12.7 %copy-start.10 = (bf16[512,512]{1,0:T(8,128)(2,1)S(1)}, bf16[512,512]{1,0:T(8,128)(2,1)}, u32[]{:S(2)}) copy-start(bf16[512,512]{1,0:T(8,128)(2,1)} %copy-done.9) | copy-start | bytes 1572868
  166.1 12.1 %collective-permute-start.27 = (f32[512,128]{1,0:T(8,128)S(1)}, f32[512,128]{1,0:T(8,128)S(1)}, u32[]{:S(2)}, u32[]{:S(2)}) collective-permute-start(f32[512,128]{1,0:T(8,128)S(1)} %fusion.58), channel_id=1, source_target_pairs={{0,2},{2,4},{4,6},{6,8},{8,10},{10,12},{12,14},{14,16},{16,18},{18... | collective-permute-start | bytes 786440 | tf_op jit(solution)/shard_map/ppermute | solution.py:17
  170.6 18.4 %copy-start.35 = (f32[512]{0:T(512)S(1)}, f32[512]{0:T(512)}, u32[]{:S(2)}) copy-start(f32[512]{0:T(512)} %copy-done.34) | copy-start | bytes 6148
  170.7 10.4 %collective-permute-start.20 = (f32[512,128]{1,0:T(8,128)S(1)}, f32[512,128]{1,0:T(8,128)S(1)}, u32[]{:S(2)}, u32[]{:S(2)}) collective-permute-start(f32[512,128]{1,0:T(8,128)S(1)} %add.99), channel_id=1, source_target_pairs={{0,2},{2,4},{4,6},{6,8},{8,10},{10,12},{12,14},{14,16},{16,18},{18... | collective-permute-start | bytes 786440 | tf_op jit(solution)/shard_map/ppermute | solution.py:17
  178.8 10.2 %collective-permute-start.28 = (f32[512,128]{1,0:T(8,128)S(1)}, f32[512,128]{1,0:T(8,128)}, u32[]{:S(2)}, u32[]{:S(2)}) collective-permute-start(f32[512,128]{1,0:T(8,128)S(1)} %fusion.53), channel_id=1, source_target_pairs={{0,2},{2,4},{4,6},{6,8},{8,10},{10,12},{12,14},{14,16},{16,18},{18... | collective-permute-start | bytes 786440 | tf_op jit(solution)/shard_map/ppermute | solution.py:17
  181.1 18.1 %collective-permute-start.21 = (f32[512,128]{1,0:T(8,128)S(1)}, f32[512,128]{1,0:T(8,128)}, u32[]{:S(2)}, u32[]{:S(2)}) collective-permute-start(f32[512,128]{1,0:T(8,128)S(1)} %add.100), channel_id=1, source_target_pairs={{0,18},{2,20},{4,22},{6,24},{8,26},{10,28},{12,30},{14,0},{16,2},{... | collective-permute-start | bytes 786440 | tf_op jit(solution)/shard_map/ppermute | solution.py:17
  190.8 8.3 %collective-permute-start.29 = (bf16[512,128]{1,0:T(8,128)(2,1)S(1)}, bf16[512,128]{1,0:T(8,128)(2,1)S(1)}, u32[]{:S(2)}, u32[]{:S(2)}) collective-permute-start(bf16[512,128]{1,0:T(8,128)(2,1)S(1)} %fusion.48), channel_id=1, source_target_pairs={{0,18},{2,20},{4,22},{6,24},{8,26},{10,28},{12,30},{14,0},{16,2},{... | collective-permute-start | bytes 393224 | tf_op jit(solution)/shard_map/ppermute | solution.py:17
  (20 other events, 92.7 us)
Sparse Core Ops, SparseCore 0:
  135.2 14.0 reduce-scatter.1
  181.3 109.4 all-reduce.1
where the time goes:
time: 301 us; the launch traced here: 300 us
  waiting for transfers between devices  200 us (66%)
  starting transfers between devices  43.6 us (14%)
  matrix products  30.6 us (10%)
  between operations  14.9 us (5%)
  other arithmetic  5.3 us (2%)
  local copies, waits for them, and re-layouts  3.74 us (1%)
    psum x1, waiting for transfers between devices, local(): grad_wquery = lax.psum(owned_terms, 'blk')  90 us
    ppermute x23, waiting for transfers between devices, from_behind(): lax.ppermute(value, axis, [(i, (i + by) % size) for i in range(size)])  78.7 us
    ppermute x7, waiting for transfers between devices, passed_along(): return lax.ppermute(value, axis, pairs)  31.1 us
    ppermute x7, starting transfers between devices, passed_along(): return lax.ppermute(value, axis, pairs)  25.1 us
    ppermute x23, starting transfers between devices, from_behind(): lax.ppermute(value, axis, [(i, (i + by) % size) for i in range(size)])  18.4 us
    dot_general x8, matrix products, local(): lax.dot_general(prob_half, outgrad, (((0,), (0,)), ((), ())), preferred_e...  9.81 us
  transfers between devices with their start and end apart: 32, of which 21 were waited for; matrix products, arithmetic and copies ran while one was open for 12% of the time, Pallas kernels for 0%

commit v1 on v0

v1 whole, which is shorter than its diff:
```python
import functools
import math

import jax
import jax.numpy as jnp
from jax import lax
from jax.experimental import pallas as pl
from jax.experimental.pallas import tpu as pltpu
from jax.sharding import PartitionSpec as P

ROUNDS = 8
LOG2E = 1.4426950408889634
BF = jnp.bfloat16
F32 = jnp.float32
T_CHUNK = 256


def shifted(value, by):
    size = lax.axis_size("blk")
    pairs = [(i, i + by) for i in range(size) if 0 <= i + by < size]
    return lax.ppermute(value, "blk", pairs)


def turned(value, by, group):
    size = lax.axis_size("blk")
    pairs = [(i, i - i % group + (i + by) % group) for i in range(size)]
    return lax.ppermute(value, "blk", pairs)


def pieces(x):
    hi = lax.reduce_precision(x, 8, 7)
    rest = x - hi
    mid = lax.reduce_precision(rest, 8, 7)
    return [hi.astype(BF), mid.astype(BF), (rest - mid).astype(BF)]


def rows_of(vectors, width, total):
    flat = jnp.concatenate(vectors).reshape(-1, width)
    return jnp.pad(flat, ((0, total - flat.shape[0]), (0, 0)))


def dot_nt(a, b):
    return lax.dot_general(a, b, (((1,), (1,)), ((), ())), preferred_element_type=F32)


def dot_nn(a, b):
    return lax.dot_general(a, b, (((1,), (0,)), ((), ())), preferred_element_type=F32)


def attention_kernel(group, far, tokens, width, r_ref, *refs):
    sizes = [group, group, far + 1]
    q_refs, o_refs, kv_refs = (
        refs[: group],
        refs[group : 2 * group],
        refs[2 * group : sum(sizes)],
    )
    rest = refs[sum(sizes) :]
    dq_refs, dkv_refs = rest[:group], rest[group : group + far + 1]
    kt_sc, docs_sc, dk_acc, dv_acc, k_sc, v_sc = rest[group + far + 1 :]
    r = r_ref[0]
    per = tokens // width
    scale = width ** (-0.5)

    for s in range(far + 1):
        k_sc[s] = kv_refs[s][:tokens]
        v_sc[s] = kv_refs[s][tokens : 2 * tokens]
        kt_sc[s] = kv_refs[s][:tokens].astype(F32).T.astype(BF)
        docs = kv_refs[s][2 * tokens :].astype(F32)
        for j in range(per):
            row = jnp.broadcast_to(docs[j : j + 1, :], (width, width))
            docs_sc[s, j * width : (j + 1) * width, :] = row.T
        dk_acc[s] = jnp.zeros((tokens, width), F32)
        dv_acc[s] = jnp.zeros((tokens, width), F32)

    def row_of(aux, at):
        return jnp.concatenate([aux[at + j : at + j + 1, :] for j in range(per)], axis=1)

    for k in range(group):
        q = q_refs[k][...]
        o = o_refs[k][:tokens]
        aux = o_refs[k][tokens:].astype(F32)
        part = [row_of(aux, i * per) for i in range(7)]
        lse = (part[0] + part[1] + part[2]) * LOG2E
        delta = part[3] + part[4] + part[5]
        docs_q = part[6]
        dqt = jnp.zeros((width, tokens), F32)
        for j in range(far):
            if j > 0:
                s = j
            elif k == 0:
                s = 0
            else:
                s = jnp.where(r >= k, far, 0)
            for c in range(0, tokens, T_CHUNK):
                rows = slice(c, c + T_CHUNK)
                scores = dot_nt(k_sc[s, rows, :], q)
                grad_prob = dot_nt(v_sc[s, rows, :], o)
                allowed = docs_sc[s, rows, :1] == docs_q
                if j == 0 and k == 0:
                    t_at = c + lax.broadcasted_iota(jnp.int32, (T_CHUNK, tokens), 0)
                    i_at = lax.broadcasted_iota(jnp.int32, (T_CHUNK, tokens), 1)
                    allowed = allowed & (t_at <= i_at)
                prob = jnp.where(allowed, jnp.exp2(scores * (scale * LOG2E) - lse), 0.0)
                dscore = (prob * (grad_prob - delta)).astype(BF)
                dv_acc[s, rows, :] += dot_nn(prob.astype(BF), o)
                dk_acc[s, rows, :] += dot_nn(dscore, q)
                dqt += dot_nn(kt_sc[s, :, rows], dscore)
        dq_refs[k][...] = (dqt.T * scale).astype(dq_refs[k].dtype)

    for s in range(far + 1):
        dkv_refs[s][:tokens] = (dk_acc[s] * scale).astype(dkv_refs[s].dtype)
        dkv_refs[s][tokens:] = dv_acc[s].astype(dkv_refs[s].dtype)


def attention(group, far, tokens, width, r, q_list, o_list, kv_list):
    vmem = pl.BlockSpec(memory_space=pltpu.VMEM)
    pairs = group * far
    dq_shapes = [
        jax.ShapeDtypeStruct((tokens, width), F32 if k == 0 else BF) for k in range(group)
    ]
    dkv_shapes = [
        jax.ShapeDtypeStruct((2 * tokens, width), F32 if s == 0 else BF) for s in range(far + 1)
    ]
    out = pl.pallas_call(
        functools.partial(attention_kernel, group, far, tokens, width),
        out_shape=dq_shapes + dkv_shapes,
        in_specs=[pl.BlockSpec(memory_space=pltpu.SMEM)] + [vmem] * (2 * group + far + 1),
        out_specs=[vmem] * (group + far + 1),
        scratch_shapes=[
            pltpu.VMEM((far + 1, width, tokens), BF),
            pltpu.VMEM((far + 1, tokens, width), F32),
            pltpu.VMEM((far + 1, tokens, width), F32),
            pltpu.VMEM((far + 1, tokens, width), F32),
            pltpu.VMEM((far + 1, tokens, width), BF),
            pltpu.VMEM((far + 1, tokens, width), BF),
        ],
        compiler_params=pltpu.CompilerParams(vmem_limit_bytes=48 * 1024 * 1024),
        cost_estimate=pl.CostEstimate(
            flops=pairs * 10 * tokens * tokens * width,
            bytes_accessed=8 * 1024 * 1024,
            transcendentals=pairs * tokens * tokens,
        ),
        name="attention",
    )(r, *q_list, *o_list, *kv_list)
    return out[:group], out[group:]


def local(
    hidden_in, w_query, query_gain, key_rows, value_rows, grad_out, logsumexp, row_delta, doc_ids
):
    inputs = hidden_in[0]
    tokens, width = key_rows.shape[1:]
    blocks = lax.axis_size("blk")
    halves = lax.axis_size("fsdp")
    group = math.gcd(blocks, max(1, ROUNDS // 2))
    far = ROUNDS // group
    r = (lax.axis_index("blk") % group).astype(jnp.int32)[None]

    per = tokens // width
    docs = (doc_ids[0] + 1).astype(BF)
    kv_own = jnp.concatenate(
        [key_rows[0], value_rows[0], rows_of([docs], width, -(-per // 16) * 16)]
    )
    kv_list = [kv_own] + [shifted(kv_own, group * s) for s in range(1, far + 1)]
    aux = rows_of(
        pieces(logsumexp[0]) + pieces(row_delta[0]) + [docs], width, -(-7 * per // 16) * 16
    )
    o_own = jnp.concatenate([grad_out[0], aux])
    o_list = [o_own] + [turned(o_own, k, group) for k in range(1, group)]

    projection = lax.all_gather(w_query, "fsdp", axis=0, tiled=True)
    q_pre = jnp.dot(inputs, projection, preferred_element_type=F32)
    inverse = lax.rsqrt(jnp.mean(q_pre * q_pre, axis=-1, keepdims=True) + 1e-06)
    normed = q_pre * inverse
    query = (normed * query_gain).astype(BF)
    q_list = [query] + [turned(query, k, group) for k in range(1, group)]

    dq_list, dkv_list = attention(group, far, tokens, width, r, q_list, o_list, kv_list)

    grad_query = dq_list[0]
    for k in range(1, group):
        grad_query = grad_query + turned(dq_list[k], -k, group).astype(F32)
    scaled = grad_query * query_gain
    grad_pre = (
        inverse * (scaled - normed * jnp.mean(scaled * normed, axis=-1, keepdims=True))
    ).astype(BF)
    weight_term = lax.dot_general(
        inputs, grad_pre, (((0,), (0,)), ((), ())), preferred_element_type=F32
    ).astype(BF)
    grad_hidden = dot_nt(grad_pre, projection).astype(BF)

    grad_kv = dkv_list[0]
    for s in range(1, far + 1):
        grad_kv = grad_kv + shifted(dkv_list[s], -group * s).astype(F32)
    grad_kv = grad_kv.astype(BF)

    owned = weight_term.shape[0] // halves
    share = -(-owned // blocks)
    terms = weight_term.reshape(halves, owned, width)
    if share * blocks != owned:
        terms = jnp.pad(terms, ((0, 0), (0, share * blocks - owned), (0, 0)))
    terms = terms.reshape(halves * blocks * share, width)
    got = lax.all_to_all(terms, ("fsdp", "blk"), 0, 0, tiled=True)
    mine = jnp.sum(got.reshape(halves * blocks, share, width).astype(F32), axis=0)
    mine = mine.astype(BF)
    everywhere = jnp.broadcast_to(mine[None], (blocks, share, width)).reshape(-1, width)
    total = lax.all_to_all(everywhere, "blk", 0, 0, tiled=True)
    grad_wquery = total[:owned].astype(F32)
    return (grad_hidden[None], grad_kv[None, :tokens], grad_kv[None, tokens:], grad_wquery)


def solution(mesh):
    return jax.shard_map(
        local,
        mesh=mesh,
        in_specs=(
            P("fsdp", "blk", None),
            P("fsdp", None),
            P(),
            P("fsdp", "blk", None),
            P("fsdp", "blk", None),
            P("fsdp", "blk", None),
            P("fsdp", "blk"),
            P("fsdp", "blk"),
            P("fsdp", "blk"),
        ),
        out_specs=(
            P("fsdp", "blk", None),
            P("fsdp", "blk", None),
            P("fsdp", "blk", None),
            P("fsdp", None),
        ),
        check_vma=False,
    )
```

time: 301 us -> 103 us (0.34)
  waiting for transfers between devices: 200 us -> 40.2 us
  matrix products: 30.6 us -> 6.26 us
  between operations: 14.9 us -> 0.87 us
  starting transfers between devices: 43.6 us -> 29.8 us
  Pallas kernels: 0 us -> 7.21 us
  local copies, waits for them, and re-layouts: 3.74 us -> 7.78 us
    psum x1 -> x0, waiting for transfers between devices: 90 us -> none  [local(): grad_wquery = lax.psum(owned_terms, 'blk')]
    ppermute x30 -> x13, waiting for transfers between devices: 110 us -> 23.9 us  [the longest x9 14.6 us: turned(): return lax.ppermute(value, 'blk', pairs)]
    dot_general x42 -> x2, matrix products: 29.1 us -> 4.99 us  [the longest x1 3.07 us: dot_nt(): lax.dot_general(a, b, (((1,), (1,)), ((), ())), preferred_element_type=F32)]
    ppermute x30 -> x13, starting transfers between devices: 43.5 us -> 23 us  [the longest x4 12.1 us: shifted(): return lax.ppermute(value, 'blk', pairs)]
    all_to_all x0 -> x2, waiting for transfers between devices: none -> 16.4 us  [the longest x1 14.7 us: local(): got = lax.all_to_all(terms, ('fsdp', 'blk'), 0, 0, tiled=True)]
    pallas_call x0 -> x1, Pallas kernels: none -> 7.21 us  [attention(): pl.pallas_call(functools.partial(attention_kernel, group, far, tokens, wi...]
    all_to_all x0 -> x2, starting transfers between devices: none -> 6.87 us  [the longest x1 3.53 us: local(): total = lax.all_to_all(everywhere, 'blk', 0, 0, tiled=True)]
  transfers between devices with their start and end apart: 32 -> 15, of which waited for: 21 -> 9; matrix products, arithmetic and copies ran while one was open for 12% -> 10% of each run, Pallas kernels for 0% -> 0%
where the time goes in v1:
time: 103 us
  waiting for transfers between devices  40.2 us (39%)
  starting transfers between devices  29.8 us (29%)
  local copies, waits for them, and re-layouts  7.78 us (8%)
  Pallas kernels  7.21 us (7%)
  other arithmetic  6.5 us (6%)
  matrix products  6.26 us (6%)
  blocking collectives  3.82 us (4%)
    all_to_all x1, waiting for transfers between devices, local(): got = lax.all_to_all(terms, ('fsdp', 'blk'), 0, 0, tiled=True)  14.7 us
    ppermute x9, waiting for transfers between devices, turned(): return lax.ppermute(value, 'blk', pairs)  14.6 us
    ppermute x4, starting transfers between devices, shifted(): return lax.ppermute(value, 'blk', pairs)  12.1 us
    ppermute x9, starting transfers between devices, turned(): return lax.ppermute(value, 'blk', pairs)  10.9 us
    ppermute x4, waiting for transfers between devices, shifted(): return lax.ppermute(value, 'blk', pairs)  9.32 us
    pallas_call x1, Pallas kernels, attention(): pl.pallas_call(functools.partial(attention_kernel, group, far, tokens, wi...  7.21 us
    all_gather x1, blocking collectives, local(): projection = lax.all_gather(w_query, 'fsdp', axis=0, tiled=True)  3.82 us
    all_to_all x1, starting transfers between devices, local(): total = lax.all_to_all(everywhere, 'blk', 0, 0, tiled=True)  3.53 us
  transfers between devices with their start and end apart: 15, of which 9 were waited for; matrix products, arithmetic and copies ran while one was open for 10% of the time, Pallas kernels for 0%

profile of v1, /device:TPU:0, one launch (start us, length us, event | category | flops | bytes accessed | tf_op | source)
XLA Modules:
  0.0 102.5 jit_solution(5385128316533473841)
XLA Ops:
  0.6 0.0 copy-start
  0.6 0.8 convert_reduce_fusion
  1.5 1.0 fusion.7.refs_8_
  2.5 0.0 copy-start.13
  2.5 6.0 %collective-permute-start.7 = (bf16[1040,128]{1,0:T(8,128)(2,1)S(1)}, bf16[1040,128]{1,0:T(8,128)(2,1)S(1)}, u32[]{:S(2)}, u32[]{:S(2)}) collective-permute-start(bf16[1040,128]{1,0:T(8,128)(2,1)S(1)} %fusion.7.refs_8_), channel_id=1, source_target_pairs={{0,16},{2,18},{4,20},{6,22},{8,24},{10,26},{12,28},{14,30},{1,17},... | collective-permute-start | bytes 798728 | tf_op jit(solution)/shard_map/ppermute | solution.py:21
  8.5 3.5 %collective-permute-start.6 = (bf16[1040,128]{1,0:T(8,128)(2,1)S(1)}, bf16[1040,128]{1,0:T(8,128)(2,1)S(1)}, u32[]{:S(2)}, u32[]{:S(2)}) collective-permute-start(bf16[1040,128]{1,0:T(8,128)(2,1)S(1)} %fusion.7.refs_8_), channel_id=1, source_target_pairs={{0,8},{2,10},{4,12},{6,14},{8,16},{10,18},{12,20},{14,22},{16,24},... | collective-permute-start | bytes 798728 | tf_op jit(solution)/shard_map/ppermute | solution.py:21
  12.0 3.8 %all_gather.3 = bf16[2048,128]{1,0:T(8,128)(2,1)} all-gather(bf16[1024,128]{1,0:T(8,128)(2,1)} %param.10), channel_id=1, replica_groups=mesh['blk'=16,'fsdp'=2] {'fsdp'}, dimensions={0}, use_global_device_ids=true | all-gather | bytes 786432 | tf_op jit(solution)/shard_map/all_gather | solution.py:171
  15.8 1.9 %multiply_reduce_fusion.1 = (f32[512]{0:T(512)S(1)}, f32[512,128]{0,1:T(8,128)S(1)}) fusion(bf16[2048,128]{1,0:T(8,128)(2,1)} %all_gather.3, bf16[1,512,2048]{2,1,0:T(8,128)(2,1)S(1)} %copy-done), kind=kOutput, calls=%fused_computation.18 | convolution fusion | flops 268566016 | bytes 2885632 | tf_op jit(solution)/shard_map/dot_general | solution.py:172
  17.8 0.8 copy.14
  18.6 1.1 %multiply_convert_fusion.1.refs_0_ = bf16[512,128]{1,0:T(8,128)(2,1)S(1)} fusion(f32[512,128]{1,0:T(8,128)} %copy.14, f32[128]{0:T(128)S(1)} %copy-done.13, f32[512]{0:T(512)S(1)} %add_rsqrt_fusion), kind=kLoop, calls=%fused_computation.17 | loop fusion | flops 196608 | bytes 395776 | tf_op jit(solution)/shard_map/convert_element_type | solution.py:175
  19.7 2.5 %collective-permute-start.2 = (bf16[512,128]{1,0:T(8,128)(2,1)S(1)}, bf16[512,128]{1,0:T(8,128)(2,1)S(1)}, u32[]{:S(2)}, u32[]{:S(2)}) collective-permute-start(bf16[512,128]{1,0:T(8,128)(2,1)S(1)} %multiply_convert_fusion.1.refs_0_), channel_id=1, source_target_pairs={{0,6},{2,0},{4,2},{6,4},{8,14},{10,8},{12,10},{14,12},{16,22},{18,... | collective-permute-start | bytes 393224 | tf_op jit(solution)/shard_map/ppermute | solution.py:27
  22.2 0.5 collective-permute-start.1
  22.7 0.6 collective-permute-start
  23.3 0.1 concatenate.10
  23.5 2.7 %collective-permute-done.2.refs_3_ = bf16[512,128]{1,0:T(8,128)(2,1)S(1)} collective-permute-done((bf16[512,128]{1,0:T(8,128)(2,1)S(1)}, bf16[512,128]{1,0:T(8,128)(2,1)S(1)}, u32[]{:S(2)}, u32[]{:S(2)}) %collective-permute-start.2) | collective-permute-done | bytes 131104 | tf_op jit(solution)/shard_map/ppermute | solution.py:27
  26.1 3.4 %collective-permute-start.5 = (bf16[544,128]{1,0:T(8,128)(2,1)S(1)}, bf16[544,128]{1,0:T(8,128)(2,1)S(1)}, u32[]{:S(2)}, u32[]{:S(2)}) collective-permute-start(bf16[544,128]{1,0:T(8,128)(2,1)S(1)} %fusion.8.refs_4_), channel_id=1, source_target_pairs={{0,6},{2,0},{4,2},{6,4},{8,14},{10,8},{12,10},{14,12},{16,22},{18,... | collective-permute-start | bytes 417800 | tf_op jit(solution)/shard_map/ppermute | solution.py:27
  29.5 1.1 %collective-permute-done.1.refs_2_ = bf16[512,128]{1,0:T(8,128)(2,1)} collective-permute-done((bf16[512,128]{1,0:T(8,128)(2,1)S(1)}, bf16[512,128]{1,0:T(8,128)(2,1)}, u32[]{:S(2)}, u32[]{:S(2)}) %collective-permute-start.1) | collective-permute-done | bytes 131104 | tf_op jit(solution)/shard_map/ppermute | solution.py:27
  30.6 0.5 collective-permute-start.4
  31.1 0.6 collective-permute-start.3
  31.7 1.6 %collective-permute-done.5.refs_7_ = bf16[544,128]{1,0:T(8,128)(2,1)S(1)} collective-permute-done((bf16[544,128]{1,0:T(8,128)(2,1)S(1)}, bf16[544,128]{1,0:T(8,128)(2,1)S(1)}, u32[]{:S(2)}, u32[]{:S(2)}) %collective-permute-start.5) | collective-permute-done | bytes 139296 | tf_op jit(solution)/shard_map/ppermute | solution.py:27
  33.3 0.6 copy-done.7
  33.9 4.6 %collective-permute-done.4.refs_6_ = bf16[544,128]{1,0:T(8,128)(2,1)} collective-permute-done((bf16[544,128]{1,0:T(8,128)(2,1)S(1)}, bf16[544,128]{1,0:T(8,128)(2,1)}, u32[]{:S(2)}, u32[]{:S(2)}) %collective-permute-start.4) | collective-permute-done | bytes 139296 | tf_op jit(solution)/shard_map/ppermute | solution.py:27
  38.6 0.7 copy-done.1
  39.3 0.9 copy-done.2
  40.2 0.9 copy-done.8
  41.1 7.2 %attention.1 = (f32[512,128]{1,0:T(8,128)S(1)}, bf16[512,128]{1,0:T(8,128)(2,1)S(1)}, bf16[512,128]{1,0:T(8,128)(2,1)S(1)}, bf16[512,128]{1,0:T(8,128)(2,1)S(1)}...) custom-call(s32[1]{0:T(128)} %bitcast.1.r_ref, ...), custom_call_target="tpu_custom_call" | custom-call | flops 2684354560 | bytes 8388608 | tf_op jit(solution)/shard_map/attention/pallas_call | solution.py:124
  48.4 0.1 collective-permute-start.8
  48.4 0.8 collective-permute-start.9
  49.2 1.9 %collective-permute-start.10 = (bf16[512,128]{1,0:T(8,128)(2,1)S(1)}, bf16[512,128]{1,0:T(8,128)(2,1)S(1)}, u32[]{:S(2)}, u32[]{:S(2)}) collective-permute-start(bf16[512,128]{1,0:T(8,128)(2,1)S(1)} %get-tuple-element.14), channel_id=1, source_target_pairs={{0,2},{2,4},{4,6},{6,0},{8,10},{10,12},{12,14},{14,8},{16,18},{18,... | collective-permute-start | bytes 393224 | tf_op jit(solution)/shard_map/ppermute | solution.py:27
  51.2 3.1 %collective-permute-done.8 = bf16[512,128]{1,0:T(8,128)(2,1)S(1)} collective-permute-done((bf16[512,128]{1,0:T(8,128)(2,1)S(1)}, bf16[512,128]{1,0:T(8,128)(2,1)S(1)}, u32[]{:S(2)}, u32[]{:S(2)}) %collective-permute-start.8) | collective-permute-done | bytes 131104 | tf_op jit(solution)/shard_map/ppermute | solution.py:27
  54.3 1.5 %collective-permute-done.9 = bf16[512,128]{1,0:T(8,128)(2,1)S(1)} collective-permute-done((bf16[512,128]{1,0:T(8,128)(2,1)S(1)}, bf16[512,128]{1,0:T(8,128)(2,1)S(1)}, u32[]{:S(2)}, u32[]{:S(2)}) %collective-permute-start.9) | collective-permute-done | bytes 131104 | tf_op jit(solution)/shard_map/ppermute | solution.py:27
  55.8 0.2 multiply_reduce_fusion
  56.1 0.2 multiply_convert_fusion
  56.3 1.3 %fusion.1 = bf16[2048,128]{0,1:T(8,128)(2,1)} fusion(bf16[512,128]{1,0:T(8,128)(2,1)S(1)} %multiply_convert_fusion, bf16[1,512,2048]{2,1,0:T(8,128)(2,1)S(1)} %copy-done), kind=kOutput, calls=%fused_computation.3 | convolution fusion | flops 268697600 | bytes 2752512 | tf_op jit(solution)/shard_map/dot_general | solution.py:187
  57.6 2.1 %copy.15 = bf16[2048,128]{1,0:T(8,128)(2,1)} copy(bf16[2048,128]{0,1:T(8,128)(2,1)} %fusion.1) | data formatting | bytes 1048576 | tf_op jit(solution)/shard_map/convert_element_type | solution.py:189
  59.7 3.3 %all-to-all-start = ((bf16[32,64,128]{2,1,0:T(8,128)(2,1)}), bf16[32,64,128]{2,1,0:T(8,128)(2,1)}, u32[]{:S(2)}, u32[]{:S(2)}) async-start(bf16[32,64,128]{2,1,0:T(8,128)(2,1)} %bitcast.30), calls=%async_computation | async-start | bytes 1048576 | tf_op jit(solution)/shard_map/all_to_all | solution.py:203
  63.1 1.3 %collective-permute-start.11 = (bf16[1024,128]{1,0:T(8,128)(2,1)S(1)}, bf16[1024,128]{1,0:T(8,128)(2,1)}, u32[]{:S(2)}, u32[]{:S(2)}) collective-permute-start(bf16[1024,128]{1,0:T(8,128)(2,1)S(1)} %copy-done.6), channel_id=1, source_target_pairs={{8,0},{10,2},{12,4},{14,6},{16,8},{18,10},{20,12},{22,14},{24,16},... | collective-permute-start | bytes 786440 | tf_op jit(solution)/shard_map/ppermute | solution.py:21
  64.4 1.3 %collective-permute-start.12 = (bf16[1024,128]{1,0:T(8,128)(2,1)S(1)}, bf16[1024,128]{1,0:T(8,128)(2,1)}, u32[]{:S(2)}, u32[]{:S(2)}) collective-permute-start(bf16[1024,128]{1,0:T(8,128)(2,1)S(1)} %copy-done.4), channel_id=1, source_target_pairs={{16,0},{18,2},{20,4},{22,6},{24,8},{26,10},{28,12},{30,14},{17,1},... | collective-permute-start | bytes 786440 | tf_op jit(solution)/shard_map/ppermute | solution.py:21
  65.7 14.7 %all-to-all-done = bf16[32,64,128]{2,1,0:T(8,128)(2,1)} async-done(((bf16[32,64,128]{2,1,0:T(8,128)(2,1)}), bf16[32,64,128]{2,1,0:T(8,128)(2,1)}, u32[]{:S(2)}, u32[]{:S(2)}) %all-to-all-start) | async-done | bytes 524320 | tf_op jit(solution)/shard_map/all_to_all | solution.py:203
  80.4 1.1 %reduce_sum.32 = bf16[64,128]{1,0:T(8,128)(2,1)S(1)} reduce(bf16[32,64,128]{2,1,0:T(8,128)(2,1)} %all-to-all-done, bf16[]{:T(256)} %constant.32.clone.1), dimensions={0}, to_apply=%region_2.3 | reduce | flops 253952 | bytes 540674 | tf_op jit(solution)/shard_map/reduce_sum | solution.py:204
  81.5 0.8 broadcast_in_dim.26
  82.3 3.5 %all-to-all-start.1 = ((bf16[16,64,128]{2,1,0:T(8,128)(2,1)}), bf16[16,64,128]{2,1,0:T(8,128)(2,1)S(1)}, u32[]{:S(2)}, u32[]{:S(2)}) async-start(bf16[16,64,128]{2,1,0:T(8,128)(2,1)} %broadcast_in_dim.26), calls=%async_computation.1 | async-start | bytes 524288 | tf_op jit(solution)/shard_map/all_to_all | solution.py:207
  85.8 3.1 %fusion = bf16[1,512,2048]{2,1,0:T(8,128)(2,1)} fusion(bf16[512,128]{1,0:T(8,128)(2,1)S(1)} %multiply_convert_fusion, bf16[2048,128]{1,0:T(8,128)(2,1)} %all_gather.3), kind=kOutput, calls=%fused_computation.1 | convolution fusion | flops 269484032 | bytes 2752512 | tf_op jit(solution)/shard_map/dot_general | solution.py:43
  88.9 9.3 %collective-permute-done.12 = bf16[1024,128]{1,0:T(8,128)(2,1)} collective-permute-done((bf16[1024,128]{1,0:T(8,128)(2,1)S(1)}, bf16[1024,128]{1,0:T(8,128)(2,1)}, u32[]{:S(2)}, u32[]{:S(2)}) %collective-permute-start.12) | collective-permute-done | bytes 262176 | tf_op jit(solution)/shard_map/ppermute | solution.py:21
  98.2 1.1 %add_convert_fusion = bf16[1024,128]{1,0:T(8,128)(2,1)S(1)} fusion(bf16[1024,128]{1,0:T(8,128)(2,1)} %collective-permute-done.12, f32[1024,128]{1,0:T(8,128)S(1)} %get-tuple-element.15, bf16[1024,128]{1,0:T(8,128)(2,1)} %collective-permute-done.11), kind=kLoop, calls=%fused_computation.9 | loop fusion | flops 655360 | bytes 1310720 | tf_op jit(solution)/shard_map/convert_element_type | solution.py:195
  99.3 0.7 slice_bitcast_fusion
  100.0 1.6 %all-to-all-done.1 = bf16[16,64,128]{2,1,0:T(8,128)(2,1)S(1)} async-done(((bf16[16,64,128]{2,1,0:T(8,128)(2,1)}), bf16[16,64,128]{2,1,0:T(8,128)(2,1)S(1)}, u32[]{:S(2)}, u32[]{:S(2)}) %all-to-all-start.1) | async-done | bytes 262176 | tf_op jit(solution)/shard_map/all_to_all | solution.py:207
  101.7 0.8 bitcast_convert_fusion
  (38 shorter events, 0.1 us)
Async XLA Ops:
  0.6 15.2 %copy-start = (bf16[1,512,2048]{2,1,0:T(8,128)(2,1)S(1)}, bf16[1,512,2048]{2,1,0:T(8,128)(2,1)}, u32[]{:S(2)}) copy-start(bf16[1,512,2048]{2,1,0:T(8,128)(2,1)} %param.9) | copy-start | bytes 6291460
  2.5 16.1 %copy-start.13 = (f32[128]{0:T(128)S(1)}, f32[128]{0:T(128)}, u32[]{:S(2)}) copy-start(f32[128]{0:T(128)} %param.11) | copy-start | bytes 1540
  2.5 36.0 %collective-permute-start.7 = (bf16[1040,128]{1,0:T(8,128)(2,1)S(1)}, bf16[1040,128]{1,0:T(8,128)(2,1)S(1)}, u32[]{:S(2)}, u32[]{:S(2)}) collective-permute-start(bf16[1040,128]{1,0:T(8,128)(2,1)S(1)} %fusion.7.refs_8_), channel_id=1, source_target_pairs={{0,16},{2,18},{4,20},{6,22},{8,24},{10,26},{12,28},{14,30},{1,17},... | collective-permute-start | bytes 798728 | tf_op jit(solution)/shard_map/ppermute | solution.py:21
  8.5 30.1 %collective-permute-start.6 = (bf16[1040,128]{1,0:T(8,128)(2,1)S(1)}, bf16[1040,128]{1,0:T(8,128)(2,1)S(1)}, u32[]{:S(2)}, u32[]{:S(2)}) collective-permute-start(bf16[1040,128]{1,0:T(8,128)(2,1)S(1)} %fusion.7.refs_8_), channel_id=1, source_target_pairs={{0,8},{2,10},{4,12},{6,14},{8,16},{10,18},{12,20},{14,22},{16,24},... | collective-permute-start | bytes 798728 | tf_op jit(solution)/shard_map/ppermute | solution.py:21
  15.8 7.5 %copy-start.15 = (f32[1,512]{1,0:T(1,128)S(1)}, f32[1,512]{1,0:T(1,128)}, u32[]{:S(2)}) copy-start(f32[1,512]{1,0:T(1,128)} %param.15) | copy-start | bytes 6148
  15.8 7.5 %copy-start.16 = (f32[1,512]{1,0:T(1,128)S(1)}, f32[1,512]{1,0:T(1,128)}, u32[]{:S(2)}) copy-start(f32[1,512]{1,0:T(1,128)} %param.16) | copy-start | bytes 6148
  15.8 7.6 %copy-start.10 = (bf16[1,512,128]{2,1,0:T(8,128)(2,1)S(1)}, bf16[1,512,128]{2,1,0:T(8,128)(2,1)}, u32[]{:S(2)}) copy-start(bf16[1,512,128]{2,1,0:T(8,128)(2,1)} %param.14) | copy-start | bytes 393220
  17.8 5.7 %copy-start.11 = (f32[512]{0:T(512)}, f32[512]{0:T(512)S(1)}, u32[]{:S(2)}) copy-start(f32[512]{0:T(512)S(1)} %add_rsqrt_fusion) | copy-start | bytes 6148
  19.7 6.4 %collective-permute-start.2 = (bf16[512,128]{1,0:T(8,128)(2,1)S(1)}, bf16[512,128]{1,0:T(8,128)(2,1)S(1)}, u32[]{:S(2)}, u32[]{:S(2)}) collective-permute-start(bf16[512,128]{1,0:T(8,128)(2,1)S(1)} %multiply_convert_fusion.1.refs_0_), channel_id=1, source_target_pairs={{0,6},{2,0},{4,2},{6,4},{8,14},{10,8},{12,10},{14,12},{16,22},{18,... | collective-permute-start | bytes 393224 | tf_op jit(solution)/shard_map/ppermute | solution.py:27
  22.2 8.4 %collective-permute-start.1 = (bf16[512,128]{1,0:T(8,128)(2,1)S(1)}, bf16[512,128]{1,0:T(8,128)(2,1)}, u32[]{:S(2)}, u32[]{:S(2)}) collective-permute-start(bf16[512,128]{1,0:T(8,128)(2,1)S(1)} %multiply_convert_fusion.1.refs_0_), channel_id=1, source_target_pairs={{0,4},{2,6},{4,0},{6,2},{8,12},{10,14},{12,8},{14,10},{16,20},{18,... | collective-permute-start | bytes 393224 | tf_op jit(solution)/shard_map/ppermute | solution.py:27
  22.7 8.4 %collective-permute-start = (bf16[512,128]{1,0:T(8,128)(2,1)S(1)}, bf16[512,128]{1,0:T(8,128)(2,1)}, u32[]{:S(2)}, u32[]{:S(2)}) collective-permute-start(bf16[512,128]{1,0:T(8,128)(2,1)S(1)} %multiply_convert_fusion.1.refs_0_), channel_id=1, source_target_pairs={{0,2},{2,4},{4,6},{6,0},{8,10},{10,12},{12,14},{14,8},{16,18},{18,... | collective-permute-start | bytes 393224 | tf_op jit(solution)/shard_map/ppermute | solution.py:27
  26.1 7.1 %collective-permute-start.5 = (bf16[544,128]{1,0:T(8,128)(2,1)S(1)}, bf16[544,128]{1,0:T(8,128)(2,1)S(1)}, u32[]{:S(2)}, u32[]{:S(2)}) collective-permute-start(bf16[544,128]{1,0:T(8,128)(2,1)S(1)} %fusion.8.refs_4_), channel_id=1, source_target_pairs={{0,6},{2,0},{4,2},{6,4},{8,14},{10,8},{12,10},{14,12},{16,22},{18,... | collective-permute-start | bytes 417800 | tf_op jit(solution)/shard_map/ppermute | solution.py:27
  30.6 7.9 %collective-permute-start.4 = (bf16[544,128]{1,0:T(8,128)(2,1)S(1)}, bf16[544,128]{1,0:T(8,128)(2,1)}, u32[]{:S(2)}, u32[]{:S(2)}) collective-permute-start(bf16[544,128]{1,0:T(8,128)(2,1)S(1)} %fusion.8.refs_4_), channel_id=1, source_target_pairs={{0,4},{2,6},{4,0},{6,2},{8,12},{10,14},{12,8},{14,10},{16,20},{18,... | collective-permute-start | bytes 417800 | tf_op jit(solution)/shard_map/ppermute | solution.py:27
  31.1 7.4 %collective-permute-start.3 = (bf16[544,128]{1,0:T(8,128)(2,1)S(1)}, bf16[544,128]{1,0:T(8,128)(2,1)}, u32[]{:S(2)}, u32[]{:S(2)}) collective-permute-start(bf16[544,128]{1,0:T(8,128)(2,1)S(1)} %fusion.8.refs_4_), channel_id=1, source_target_pairs={{0,2},{2,4},{4,6},{6,0},{8,10},{10,12},{12,14},{14,8},{16,18},{18,... | collective-permute-start | bytes 417800 | tf_op jit(solution)/shard_map/ppermute | solution.py:27
  33.3 0.6 copy-start.7
  38.5 0.7 copy-start.1
  39.3 1.0 copy-start.2
  40.2 0.9 copy-start.8
  41.1 14.7 %copy-start.9 = (f32[512,128]{1,0:T(8,128)S(1)}, f32[512,128]{1,0:T(8,128)}, u32[]{:S(2)}) copy-start(f32[512,128]{1,0:T(8,128)} %copy.14) | copy-start | bytes 786436
  41.1 14.7 %copy-start.12 = (f32[512]{0:T(512)S(1)}, f32[512]{0:T(512)}, u32[]{:S(2)}) copy-start(f32[512]{0:T(512)} %copy-done.11) | copy-start | bytes 6148
  41.1 14.7 %copy-start.14 = (f32[128]{0:T(128)S(1)}, f32[128]{0:T(128)}, u32[]{:S(2)}) copy-start(f32[128]{0:T(128)} %param.11) | copy-start | bytes 1540
  48.3 8.0 %copy-start.3 = (bf16[1024,128]{1,0:T(8,128)(2,1)}, bf16[1024,128]{1,0:T(8,128)(2,1)S(1)}, u32[]{:S(2)}) copy-start(bf16[1024,128]{1,0:T(8,128)(2,1)S(1)} %get-tuple-element.17) | copy-start | bytes 786436
  48.3 8.0 %copy-start.5 = (bf16[1024,128]{1,0:T(8,128)(2,1)}, bf16[1024,128]{1,0:T(8,128)(2,1)S(1)}, u32[]{:S(2)}) copy-start(bf16[1024,128]{1,0:T(8,128)(2,1)S(1)} %get-tuple-element.16) | copy-start | bytes 786436
  48.4 6.0 %collective-permute-start.8 = (bf16[512,128]{1,0:T(8,128)(2,1)S(1)}, bf16[512,128]{1,0:T(8,128)(2,1)S(1)}, u32[]{:S(2)}, u32[]{:S(2)}) collective-permute-start(bf16[512,128]{1,0:T(8,128)(2,1)S(1)} %get-tuple-element.12), channel_id=1, source_target_pairs={{0,6},{2,0},{4,2},{6,4},{8,14},{10,8},{12,10},{14,12},{16,22},{18,... | collective-permute-start | bytes 393224 | tf_op jit(solution)/shard_map/ppermute | solution.py:27
  48.4 7.4 %collective-permute-start.9 = (bf16[512,128]{1,0:T(8,128)(2,1)S(1)}, bf16[512,128]{1,0:T(8,128)(2,1)S(1)}, u32[]{:S(2)}, u32[]{:S(2)}) collective-permute-start(bf16[512,128]{1,0:T(8,128)(2,1)S(1)} %get-tuple-element.13), channel_id=1, source_target_pairs={{0,4},{2,6},{4,0},{6,2},{8,12},{10,14},{12,8},{14,10},{16,20},{18,... | collective-permute-start | bytes 393224 | tf_op jit(solution)/shard_map/ppermute | solution.py:27
  49.2 6.6 %collective-permute-start.10 = (bf16[512,128]{1,0:T(8,128)(2,1)S(1)}, bf16[512,128]{1,0:T(8,128)(2,1)S(1)}, u32[]{:S(2)}, u32[]{:S(2)}) collective-permute-start(bf16[512,128]{1,0:T(8,128)(2,1)S(1)} %get-tuple-element.14), channel_id=1, source_target_pairs={{0,2},{2,4},{4,6},{6,0},{8,10},{10,12},{12,14},{14,8},{16,18},{18,... | collective-permute-start | bytes 393224 | tf_op jit(solution)/shard_map/ppermute | solution.py:27
  57.6 5.4 %copy-start.6 = (bf16[1024,128]{1,0:T(8,128)(2,1)S(1)}, bf16[1024,128]{1,0:T(8,128)(2,1)}, u32[]{:S(2)}) copy-start(bf16[1024,128]{1,0:T(8,128)(2,1)} %copy-done.5) | copy-start | bytes 786436
  57.6 6.8 %copy-start.4 = (bf16[1024,128]{1,0:T(8,128)(2,1)S(1)}, bf16[1024,128]{1,0:T(8,128)(2,1)}, u32[]{:S(2)}) copy-start(bf16[1024,128]{1,0:T(8,128)(2,1)} %copy-done.3) | copy-start | bytes 786436
  59.7 20.7 %all-to-all-start = ((bf16[32,64,128]{2,1,0:T(8,128)(2,1)}), bf16[32,64,128]{2,1,0:T(8,128)(2,1)}, u32[]{:S(2)}, u32[]{:S(2)}) async-start(bf16[32,64,128]{2,1,0:T(8,128)(2,1)} %bitcast.30), calls=%async_computation | async-start | bytes 1048576 | tf_op jit(solution)/shard_map/all_to_all | solution.py:203
  63.1 25.8 %collective-permute-start.11 = (bf16[1024,128]{1,0:T(8,128)(2,1)S(1)}, bf16[1024,128]{1,0:T(8,128)(2,1)}, u32[]{:S(2)}, u32[]{:S(2)}) collective-permute-start(bf16[1024,128]{1,0:T(8,128)(2,1)S(1)} %copy-done.6), channel_id=1, source_target_pairs={{8,0},{10,2},{12,4},{14,6},{16,8},{18,10},{20,12},{22,14},{24,16},... | collective-permute-start | bytes 786440 | tf_op jit(solution)/shard_map/ppermute | solution.py:21
  64.4 33.8 %collective-permute-start.12 = (bf16[1024,128]{1,0:T(8,128)(2,1)S(1)}, bf16[1024,128]{1,0:T(8,128)(2,1)}, u32[]{:S(2)}, u32[]{:S(2)}) collective-permute-start(bf16[1024,128]{1,0:T(8,128)(2,1)S(1)} %copy-done.4), channel_id=1, source_target_pairs={{16,0},{18,2},{20,4},{22,6},{24,8},{26,10},{28,12},{30,14},{17,1},... | collective-permute-start | bytes 786440 | tf_op jit(solution)/shard_map/ppermute | solution.py:21
  82.3 19.4 %all-to-all-start.1 = ((bf16[16,64,128]{2,1,0:T(8,128)(2,1)}), bf16[16,64,128]{2,1,0:T(8,128)(2,1)S(1)}, u32[]{:S(2)}, u32[]{:S(2)}) async-start(bf16[16,64,128]{2,1,0:T(8,128)(2,1)} %broadcast_in_dim.26), calls=%async_computation.1 | async-start | bytes 524288 | tf_op jit(solution)/shard_map/all_to_all | solution.py:207

commit v2 on v0

v2 whole, which is shorter than its diff:
```python
import functools
import math

import jax
import jax.numpy as jnp
from jax import lax
from jax.experimental import pallas as pl
from jax.experimental.pallas import tpu as pltpu
from jax.sharding import PartitionSpec as P


ROUNDS = 8
LOG2E = 1.4426950408889634
BF = jnp.bfloat16
F32 = jnp.float32
T_CHUNK = 256
PACK_MIB = 63.4
ATTENTION_MIB = 16


def shifted(value, by):
    size = lax.axis_size("blk")
    pairs = [(i, i + by) for i in range(size) if 0 <= i + by < size]
    return lax.ppermute(value, "blk", pairs)


def turned(value, by, group):
    size = lax.axis_size("blk")
    pairs = [(i, i - i % group + (i + by) % group) for i in range(size)]
    return lax.ppermute(value, "blk", pairs)


def vmem_specs(count):
    return [pl.BlockSpec(memory_space=pltpu.VMEM)] * count


def params(mib):
    return pltpu.CompilerParams(vmem_limit_bytes=int(mib * 1024 * 1024))


def dot_nt(a, b):
    return lax.dot_general(a, b, (((1,), (1,)), ((), ())), preferred_element_type=F32)


def dot_nn(a, b):
    return lax.dot_general(a, b, (((1,), (0,)), ((), ())), preferred_element_type=F32)


def hbm_specs(count):
    return [pl.BlockSpec(memory_space=pltpu.HBM)] * count


def whole_specs(arrays):
    return [pl.BlockSpec(x.shape, lambda n=len(x.shape): (0,) * n) for x in arrays]


def fetched(pairs, sems):
    copies = [pltpu.make_async_copy(a, b, sems.at[i]) for i, (a, b) in enumerate(pairs)]
    for copy in copies:
        copy.start()
    return copies


def pack_kernel(
    k_ref, v_ref, o_ref, lse_ref, delta_ref, docs_ref, kv_out, o_out,
    lse_sc, delta_sc, docs_sc, sems,
):
    tokens, width = k_ref.shape
    copies = fetched(
        [
            (docs_ref, docs_sc),
            (lse_ref, lse_sc),
            (delta_ref, delta_sc),
            (k_ref, kv_out.at[:tokens]),
            (v_ref, kv_out.at[tokens : 2 * tokens]),
            (o_ref, o_out.at[:tokens]),
        ],
        sems,
    )
    for copy in copies[:3]:
        copy.wait()
    docs = (docs_sc[...] + 1).astype(F32)
    spare = kv_out.shape[0] - 2 * tokens - docs.shape[0]
    kv_out[2 * tokens :] = jnp.concatenate(
        [docs] + [jnp.zeros((spare, width), F32)] * (spare > 0)
    ).astype(BF)
    rows = []
    for ref in (lse_sc, delta_sc):
        rest = ref[...]
        for _ in range(3):
            piece = rest.astype(BF).astype(F32)
            rows.append(piece)
            rest = rest - piece
    rows.append(docs)
    spare = o_out.shape[0] - tokens - 7 * docs.shape[0]
    o_out[tokens:] = jnp.concatenate(
        rows + [jnp.zeros((spare, width), F32)] * (spare > 0)
    ).astype(BF)
    for copy in copies[3:]:
        copy.wait()


def query_kernel(h_ref, w_ref, gain_ref, query_out, q_pre_out):
    q_pre = dot_nn(h_ref[...], w_ref[...])
    inverse = lax.rsqrt(jnp.mean(q_pre * q_pre, axis=-1, keepdims=True) + 1e-06)
    q_pre_out[...] = q_pre
    query_out[...] = (q_pre * inverse * gain_ref[...]).astype(BF)


def row_data(o_ref, tokens, per):
    aux = o_ref[tokens:].astype(F32)
    part = []
    for at in range(0, 7 * per, per):
        part.append(
            jnp.concatenate([aux[at + j : at + j + 1, :] for j in range(per)], axis=1)
        )
    lse = (part[0] + part[1] + part[2]) * LOG2E
    return lse, part[3] + part[4] + part[5], part[6]


def stage_keys(kv_ref, s, tokens, width, k_sc, v_sc, kt_sc, docs_sc, with_kt):
    k_sc[s] = kv_ref[:tokens]
    v_sc[s] = kv_ref[tokens : 2 * tokens]
    if with_kt:
        kt_sc[s] = kv_ref[:tokens].astype(F32).T.astype(BF)
    docs = kv_ref[2 * tokens :].astype(F32)
    for j in range(tokens // width):
        row = jnp.broadcast_to(docs[j : j + 1, :], (width, width))
        docs_sc[s, j * width : (j + 1) * width, :] = row.T


def probabilities(s, rows, c, q, o, lse, delta, docs_q, diagonal, scale, k_sc, v_sc, docs_sc):
    scores = dot_nt(k_sc[s, rows, :], q)
    grad_prob = dot_nt(v_sc[s, rows, :], o)
    allowed = docs_sc[s, rows, :1] == docs_q
    if diagonal:
        t_at = c + lax.broadcasted_iota(jnp.int32, scores.shape, 0)
        i_at = lax.broadcasted_iota(jnp.int32, scores.shape, 1)
        allowed = allowed & (t_at <= i_at)
    prob = jnp.where(allowed, jnp.exp2(scores * (scale * LOG2E) - lse), 0.0)
    return prob, (prob * (grad_prob - delta)).astype(BF)


def slot(r, k, j, far):
    if j > 0:
        return j
    return 0 if k == 0 else jnp.where(r >= k, far, 0)


def others_kernel(group, far, tokens, width, r_ref, q_ref, *refs):
    o_refs, kv_refs = refs[: group - 1], refs[group - 1 : group + far]
    outs = refs[group + far :]
    dq_refs, dkv_ref, acc = outs[: group - 1], outs[group - 1], outs[group]
    kt_sc, docs_sc, k_sc, v_sc = outs[group + 1 :]
    r = r_ref[0]
    scale = width ** (-0.5)
    for s in range(far + 1):
        stage_keys(kv_refs[s], s, tokens, width, k_sc, v_sc, kt_sc, docs_sc, True)
        acc[s] = jnp.zeros((2 * tokens, width), F32)
    for k in range(1, group):
        q = q_ref[(r - k + group) % group]
        o = o_refs[k - 1][:tokens]
        lse, delta, docs_q = row_data(o_refs[k - 1], tokens, tokens // width)
        dqt = jnp.zeros((width, tokens), F32)
        for j in range(far):
            s = slot(r, k, j, far)
            for c in range(0, tokens, T_CHUNK):
                rows = slice(c, c + T_CHUNK)
                below = slice(tokens + c, tokens + c + T_CHUNK)
                prob, dscore = probabilities(
                    s, rows, c, q, o, lse, delta, docs_q, False, scale, k_sc, v_sc, docs_sc
                )
                acc[s, below, :] += dot_nn(prob.astype(BF), o)
                acc[s, rows, :] += dot_nn(dscore, q)
                dqt += dot_nn(kt_sc[s, :, rows], dscore)
        dq_refs[k - 1][...] = (dqt.T * scale).astype(BF)
    dkv_ref[:tokens] = (acc[far, :tokens] * scale).astype(BF)
    dkv_ref[tokens:] = acc[far, tokens:].astype(BF)


def own_kernel(far, tokens, width, q_ref, o_ref, acc, *refs):
    kv_refs, dq_ref, dkv_refs = refs[:far], refs[far], refs[far + 1 : 2 * far + 1]
    kt_sc, docs_sc, k_sc, v_sc = refs[2 * far + 1 :]
    scale = width ** (-0.5)
    q = q_ref[...]
    o = o_ref[:tokens]
    lse, delta, docs_q = row_data(o_ref, tokens, tokens // width)
    dqt = jnp.zeros((width, tokens), F32)
    for s in range(far):
        stage_keys(kv_refs[s], s, tokens, width, k_sc, v_sc, kt_sc, docs_sc, True)
        for c in range(0, tokens, T_CHUNK):
            rows = slice(c, c + T_CHUNK)
            below = slice(tokens + c, tokens + c + T_CHUNK)
            prob, dscore = probabilities(
                s, rows, c, q, o, lse, delta, docs_q, s == 0, scale, k_sc, v_sc, docs_sc
            )
            dkv_refs[s][below, :] = (acc[s, below, :] + dot_nn(prob.astype(BF), o)).astype(BF)
            dkv_refs[s][rows, :] = ((acc[s, rows, :] + dot_nn(dscore, q)) * scale).astype(BF)
            dqt += dot_nn(kt_sc[s, :, rows], dscore)
    dq_ref[...] = dqt.T * scale


def key_scratch(slots, tokens, width):
    return [
        pltpu.VMEM((slots, width, tokens), BF),
        pltpu.VMEM((slots, tokens, width), F32),
        pltpu.VMEM((slots, tokens, width), BF),
        pltpu.VMEM((slots, tokens, width), BF),
    ]


def cost(pairs, tokens, width):
    return pl.CostEstimate(
        flops=pairs * 10 * tokens * tokens * width,
        bytes_accessed=pairs * 8 * tokens * width,
        transcendentals=pairs * tokens * tokens,
    )


def others(group, far, tokens, width, r, q_all, o_list, kv_list):
    block = jax.ShapeDtypeStruct((tokens, width), BF)
    double = jax.ShapeDtypeStruct((2 * tokens, width), BF)
    sums = jax.ShapeDtypeStruct((far + 1, 2 * tokens, width), F32)
    if group == 1:
        return [], jnp.zeros(double.shape, BF), jnp.zeros(sums.shape, F32)
    out = pl.pallas_call(
        functools.partial(others_kernel, group, far, tokens, width),
        out_shape=[block] * (group - 1) + [double, sums],
        in_specs=[pl.BlockSpec(memory_space=pltpu.SMEM)] + vmem_specs(group + far + 1),
        out_specs=vmem_specs(group + 1),
        scratch_shapes=key_scratch(far + 1, tokens, width),
        compiler_params=params(ATTENTION_MIB),
        cost_estimate=cost((group - 1) * far, tokens, width),
        name="others",
    )(r, q_all, *o_list[1:], *kv_list)
    return out[: group - 1], out[group - 1], out[group]


def own(far, tokens, width, query, o_own, acc, kv_list):
    out = pl.pallas_call(
        functools.partial(own_kernel, far, tokens, width),
        out_shape=[jax.ShapeDtypeStruct((tokens, width), F32)]
        + [jax.ShapeDtypeStruct((2 * tokens, width), BF)] * far,
        in_specs=vmem_specs(far + 3),
        out_specs=vmem_specs(far + 1),
        scratch_shapes=key_scratch(far, tokens, width),
        compiler_params=params(ATTENTION_MIB),
        cost_estimate=cost(far, tokens, width),
        name="own",
    )(query, o_own, acc, *kv_list[:far])
    return out[0], out[1:]


def weight_kernel(parts, h_ref, q_pre_ref, gain_ref, own_ref, *refs):
    grad_query = own_ref[...]
    for ref in refs[:parts]:
        grad_query = grad_query + ref[...].astype(F32)
    pre_out, term_out = refs[parts:]
    q_pre = q_pre_ref[...]
    inverse = lax.rsqrt(jnp.mean(q_pre * q_pre, axis=-1, keepdims=True) + 1e-06)
    normed = q_pre * inverse
    scaled = grad_query * gain_ref[...]
    grad_pre = inverse * (scaled - normed * jnp.mean(scaled * normed, axis=-1, keepdims=True))
    pre_out[...] = grad_pre.astype(BF)
    turned_pre = grad_pre.astype(BF).astype(F32).T.astype(BF)
    columns = h_ref.shape[1]
    step = math.gcd(columns, 512)
    for c in range(0, columns, step):
        term = dot_nn(turned_pre, h_ref[:, c : c + step])
        term_out[c : c + step, :] = term.T.astype(BF)


def sum_kernel(got_ref, out_ref):
    total = got_ref[0].astype(F32)
    for i in range(1, got_ref.shape[0]):
        total = total + got_ref[i].astype(F32)
    total = total.astype(BF)
    for i in range(out_ref.shape[0]):
        out_ref[i] = total


def sum_and_repeat(got, copies):
    share, width = got.shape[1:]
    if share % 16:
        total = jnp.sum(got.astype(F32), axis=0).astype(BF)
        return jnp.broadcast_to(total[None], (copies, share, width))
    return pl.pallas_call(
        sum_kernel,
        out_shape=jax.ShapeDtypeStruct((copies, share, width), BF),
        in_specs=vmem_specs(1),
        out_specs=vmem_specs(1)[0],
        compiler_params=params(8),
        name="sum_and_repeat",
    )(got)


def local(
    hidden_in, w_query, query_gain, key_rows, value_rows, grad_out, logsumexp, row_delta, doc_ids
):
    return step(
        hidden_in[0],
        w_query,
        query_gain[None],
        key_rows[0],
        value_rows[0],
        grad_out[0],
        logsumexp,
        row_delta,
        doc_ids,
    )


def step(inputs, w_query, gain, keys, values, outgrad, logsumexp, row_delta, doc_ids):
    tokens, width = keys.shape
    blocks = lax.axis_size("blk")
    halves = lax.axis_size("fsdp")
    group = math.gcd(blocks, max(1, ROUNDS // 2))
    far = ROUNDS // group
    r = (lax.axis_index("blk") % group).astype(jnp.int32)[None]
    per = tokens // width

    kv_own, o_own = pl.pallas_call(
        pack_kernel,
        out_shape=[
            jax.ShapeDtypeStruct((2 * tokens + -(-per // 16) * 16, width), BF),
            jax.ShapeDtypeStruct((tokens + -(-7 * per // 16) * 16, width), BF),
        ],
        in_specs=hbm_specs(6),
        out_specs=vmem_specs(2),
        scratch_shapes=[
            pltpu.VMEM((per, width), F32),
            pltpu.VMEM((per, width), F32),
            pltpu.VMEM((per, width), jnp.int32),
            pltpu.SemaphoreType.DMA((6,)),
        ],
        compiler_params=params(PACK_MIB),
        name="pack",
    )(
        keys,
        values,
        outgrad,
        logsumexp.reshape(per, width),
        row_delta.reshape(per, width),
        doc_ids.reshape(per, width),
    )
    kv_list = [kv_own] + [shifted(kv_own, group * s) for s in range(far, 0, -1)][::-1]
    o_list = [o_own] + [turned(o_own, k, group) for k in range(1, group)]

    projection = lax.all_gather(w_query, "fsdp", axis=0, tiled=True)
    q_like = jax.ShapeDtypeStruct((tokens, width), F32)
    query, q_pre = pl.pallas_call(
        query_kernel,
        out_shape=[
            jax.ShapeDtypeStruct((tokens, width), BF),
            q_like,
        ],
        in_specs=vmem_specs(1) + whole_specs([projection, gain]),
        out_specs=vmem_specs(1) + whole_specs([q_like]),
        compiler_params=params(8),
        name="query",
    )(inputs, projection, gain)
    groups = [list(range(i, i + group)) for i in range(0, blocks, group)]
    q_all = lax.all_gather(query, "blk", axis_index_groups=groups)

    dq_list, grad_kv, acc = others(group, far, tokens, width, r, q_all, o_list, kv_list)

    dq_back = [turned(dq_list[k - 1], -k, group) for k in range(1, group)]
    back = shifted(grad_kv, -group)
    dq_own, dkv_list = own(far, tokens, width, query, o_own, acc, kv_list)
    grad_pre, weight_term = pl.pallas_call(
        functools.partial(weight_kernel, len(dq_back)),
        out_shape=[
            jax.ShapeDtypeStruct((tokens, width), BF),
            jax.ShapeDtypeStruct((inputs.shape[1], width), BF),
        ],
        in_specs=vmem_specs(1) + whole_specs([q_pre, gain]) + vmem_specs(1 + len(dq_back)),
        out_specs=vmem_specs(2),
        compiler_params=params(16),
        name="weight_term",
    )(inputs, q_pre, gain, dq_own, *dq_back)
    grad_hidden = dot_nt(grad_pre, projection).astype(BF)

    for s in range(far - 1, -1, -1):
        grad_kv = (dkv_list[s].astype(F32) + back.astype(F32)).astype(BF)
        if s > 0:
            back = shifted(grad_kv, -group)

    owned = weight_term.shape[0] // halves
    share = -(-owned // blocks)
    got = lax.all_to_all(weight_term, "fsdp", 0, 0, tiled=True)
    terms = sum_and_repeat(got.reshape(halves, owned, width), 1)[0]
    if share * blocks != owned:
        terms = jnp.pad(terms, ((0, share * blocks - owned), (0, 0)))
    got = lax.all_to_all(terms, "blk", 0, 0, tiled=True)
    everywhere = sum_and_repeat(got.reshape(blocks, share, width), blocks)
    total = lax.all_to_all(everywhere.reshape(-1, width), "blk", 0, 0, tiled=True)
    grad_wquery = total[:owned].astype(F32)
    return (grad_hidden[None], grad_kv[None, :tokens], grad_kv[None, tokens:], grad_wquery)


def solution(mesh):
    return jax.shard_map(
        local,
        mesh=mesh,
        in_specs=(
            P("fsdp", "blk", None),
            P("fsdp", None),
            P(),
            P("fsdp", "blk", None),
            P("fsdp", "blk", None),
            P("fsdp", "blk", None),
            P("fsdp", "blk"),
            P("fsdp", "blk"),
            P("fsdp", "blk"),
        ),
        out_specs=(
            P("fsdp", "blk", None),
            P("fsdp", "blk", None),
            P("fsdp", "blk", None),
            P("fsdp", None),
        ),
        check_vma=False,
    )
```

time: 301 us -> 79.7 us (0.26)
  waiting for transfers between devices: 200 us -> 18.1 us
  matrix products: 30.6 us -> 2.03 us
  starting transfers between devices: 43.6 us -> 25.4 us
  blocking collectives: 2.38 us -> 17.4 us
  between operations: 14.9 us -> 0.83 us
  Pallas kernels: 0 us -> 11.4 us
  other arithmetic: 5.3 us -> 0.99 us
    ppermute x30 -> x10, waiting for transfers between devices: 110 us -> 2.53 us  [the longest x6 2.52 us: turned(): return lax.ppermute(value, 'blk', pairs)]
    psum x1 -> x0, waiting for transfers between devices: 90 us -> none  [local(): grad_wquery = lax.psum(owned_terms, 'blk')]
    dot_general x43 -> x1, matrix products: 30.6 us -> 2.03 us  [dot_nt(): lax.dot_general(a, b, (((1,), (1,)), ((), ())), preferred_element_type=F32)]
    ppermute x30 -> x10, starting transfers between devices: 43.5 us -> 18.4 us  [the longest x4 12.2 us: shifted(): return lax.ppermute(value, 'blk', pairs)]
    all_to_all x0 -> x2, waiting for transfers between devices: none -> 15.6 us  [the longest x1 9.31 us: step(): got = lax.all_to_all(terms, 'blk', 0, 0, tiled=True)]
    pallas_call x0 -> x7, Pallas kernels: none -> 11.4 us  [the longest x1 4.76 us: others(): pl.pallas_call(functools.partial(others_kernel, group, far, tokens, width...]
    all_gather x1 -> x2, blocking collectives: 2.38 us -> 13.3 us  [the longest x1 10.9 us: step(): q_all = lax.all_gather(query, 'blk', axis_index_groups=groups)]
    all_to_all x0 -> x2, starting transfers between devices: none -> 7.07 us  [the longest x1 3.53 us: step(): got = lax.all_to_all(terms, 'blk', 0, 0, tiled=True)]
  transfers between devices with their start and end apart: 32 -> 12, of which waited for: 21 -> 4; matrix products, arithmetic and copies ran while one was open for 12% -> 4% of each run, Pallas kernels for 0% -> 6%
where the time goes in v2:
time: 79.7 us; the launch traced here: 79.2 us
  starting transfers between devices  25.4 us (32%)
  waiting for transfers between devices  18.1 us (23%)
  blocking collectives  17.4 us (22%)
  Pallas kernels  11.4 us (14%)
  local copies, waits for them, and re-layouts  2.99 us (4%)
  matrix products  2.03 us (3%)
  other arithmetic  0.99 us (1%)
  between operations  0.83 us (1%)
    ppermute x4, starting transfers between devices, shifted(): return lax.ppermute(value, 'blk', pairs)  12.2 us
    all_gather x1, blocking collectives, step(): q_all = lax.all_gather(query, 'blk', axis_index_groups=groups)  10.9 us
    all_to_all x1, waiting for transfers between devices, step(): got = lax.all_to_all(terms, 'blk', 0, 0, tiled=True)  9.31 us
    all_to_all x1, waiting for transfers between devices, step(): lax.all_to_all(everywhere.reshape(-1, width), 'blk', 0, 0, tiled=True)  6.28 us
    ppermute x6, starting transfers between devices, turned(): return lax.ppermute(value, 'blk', pairs)  6.17 us
    pallas_call x1, Pallas kernels, others(): pl.pallas_call(functools.partial(others_kernel, group, far, tokens, width...  4.76 us
    all_to_all x1, blocking collectives, step(): got = lax.all_to_all(weight_term, 'fsdp', 0, 0, tiled=True)  4.15 us
    all_to_all x1, starting transfers between devices, step(): got = lax.all_to_all(terms, 'blk', 0, 0, tiled=True)  3.53 us
  transfers between devices with their start and end apart: 12, of which 4 were waited for; matrix products, arithmetic and copies ran while one was open for 4% of the time, Pallas kernels for 6%

profile of v2, /device:TPU:0, one launch (start us, length us, event | category | flops | bytes accessed | tf_op | source)
XLA Modules:
  0.0 79.2 jit_solution(9877628256257489912)
XLA Ops:
  0.6 1.9 %pack.1 = (bf16[1040,128]{1,0:T(8,128)(2,1)}, bf16[544,128]{1,0:T(8,128)(2,1)}) custom-call(bf16[512,128]{1,0:T(8,128)(2,1)} %bitcast.29, bf16[512,128]{1,0:T(8,128)(2,1)} %bitcast.30, bf16[512,128]{1,0:T(8,128)(2,1)} %bitcast.31, f32[4,128]{1,0:T(4,128)} %bitcast.32, f32[4,128]{1,0:T(4,128)} %bitcast.33, s32[4,128]{1,0:T(4,128)} %bitcast.34), custom_call_target="tpu_custom_call" | custom-call | tf_op jit(solution)/shard_map/pack/pallas_call | solution.py:322
  2.5 0.0 copy-start.4
  2.5 6.1 %collective-permute-start.4 = (bf16[1040,128]{1,0:T(8,128)(2,1)}, bf16[1040,128]{1,0:T(8,128)(2,1)S(1)}, u32[]{:S(2)}, u32[]{:S(2)}) collective-permute-start(bf16[1040,128]{1,0:T(8,128)(2,1)} %get-tuple-element.21.refs_3_.refs_0_), channel_id=1, source_target_pairs={{0,16},{2,18},{4,20},{6,22},{8,24},{10,26},{12,28},{14,30},{1,17},... | collective-permute-start | bytes 798728 | tf_op jit(solution)/shard_map/ppermute | solution.py:24
  8.7 3.5 %collective-permute-start.3 = (bf16[1040,128]{1,0:T(8,128)(2,1)}, bf16[1040,128]{1,0:T(8,128)(2,1)S(1)}, u32[]{:S(2)}, u32[]{:S(2)}) collective-permute-start(bf16[1040,128]{1,0:T(8,128)(2,1)} %get-tuple-element.21.refs_3_.refs_0_), channel_id=1, source_target_pairs={{0,8},{2,10},{4,12},{6,14},{8,16},{10,18},{12,20},{14,22},{16,24},... | collective-permute-start | bytes 798728 | tf_op jit(solution)/shard_map/ppermute | solution.py:24
  12.2 2.5 %collective-permute-start.2 = (bf16[544,128]{1,0:T(8,128)(2,1)}, bf16[544,128]{1,0:T(8,128)(2,1)S(1)}, u32[]{:S(2)}, u32[]{:S(2)}) collective-permute-start(bf16[544,128]{1,0:T(8,128)(2,1)} %get-tuple-element.20.o_ref), channel_id=1, source_target_pairs={{0,6},{2,0},{4,2},{6,4},{8,14},{10,8},{12,10},{14,12},{16,22},{18,... | collective-permute-start | bytes 417800 | tf_op jit(solution)/shard_map/ppermute | solution.py:30
  14.7 0.5 collective-permute-start.1
  15.2 0.6 collective-permute-start
  15.8 2.4 %all_gather.9.w_ref = bf16[2048,128]{1,0:T(8,128)(2,1)S(1)} all-gather(bf16[1024,128]{1,0:T(8,128)(2,1)} %param.10), channel_id=1, replica_groups=mesh['blk'=16,'fsdp'=2] {'fsdp'}, dimensions={0}, use_global_device_ids=true | all-gather | bytes 786432 | tf_op jit(solution)/shard_map/all_gather | solution.py:349
  18.1 1.6 %copy-done = bf16[1,512,2048]{2,1,0:T(8,128)(2,1)S(1)} copy-done((bf16[1,512,2048]{2,1,0:T(8,128)(2,1)S(1)}, bf16[1,512,2048]{2,1,0:T(8,128)(2,1)}, u32[]{:S(2)}) %copy-start) | copy-done | bytes 2097176
  19.7 0.7 copy-done.2
  20.4 0.8 %query.1 = (bf16[512,128]{1,0:T(8,128)(2,1)S(1)}, f32[512,128]{1,0:T(8,128)S(1)}) custom-call(bf16[512,2048]{1,0:T(8,128)(2,1)S(1)} %bitcast.23, bf16[2048,128]{1,0:T(8,128)(2,1)S(1)} %all_gather.9.w_ref, f32[1,128]{1,0:T(1,128)S(1)} %bitcast.27), custom_call_target="tpu_custom_call" | custom-call | tf_op jit(solution)/shard_map/query/pallas_call | solution.py:351
  21.2 10.9 %all-gather = bf16[2048,128]{1,0:T(8,128)(2,1)S(1)} all-gather(bf16[512,128]{1,0:T(8,128)(2,1)S(1)} %get-tuple-element.19.q_ref), channel_id=2, replica_groups={{0,2,4,6},{8,10,12,14},{16,18,20,22},{24,26,28,30},{1,3,5,7},{9,11,13,1..., dimensions={0}, use_global_device_ids=true | all-gather | bytes 655360 | tf_op jit(solution)/shard_map/all_gather | solution.py:363
  32.1 0.0 collective-permute-done.2.refs_2_
  32.1 0.0 collective-permute-done.1.refs_1_
  32.1 0.0 collective-permute-done.refs_0_
  32.1 0.0 collective-permute-done.4.refs_5_
  32.1 0.0 collective-permute-done.3.refs_4_.refs_1_
  32.1 0.0 copy-done.4
  32.2 0.0 copy-start.5
  32.2 4.8 %others.1 = (bf16[512,128]{1,0:T(8,128)(2,1)S(1)}, bf16[512,128]{1,0:T(8,128)(2,1)S(1)}, bf16[512,128]{1,0:T(8,128)(2,1)S(1)}, bf16[1024,128]{1,0:T(8,128)(2,1)S(1)}, f32[3,1024,128]{2,1,0:T(8,128)S(1)}) custom-call(s32[1]{0:T(128)} %bitcast.8.r_ref, bf16[4,512,128]{2,1,0:T(8,128)(2,1)S(1)} %bitcast.25, bf16[544,128]{1,0:T(8,128)(2,1)S(1)} %collective-permute-done.refs_0_, ...), custom_call_target="tpu_custom_call" | custom-call | flops 2013265920 | bytes 3145728 | tf_op jit(solution)/shard_map/others/pallas_call | solution.py:226
  36.9 0.0 copy-start.1
  37.0 0.0 copy-start.3
  37.0 1.5 %collective-permute-start.5 = (bf16[512,128]{1,0:T(8,128)(2,1)S(1)}, bf16[512,128]{1,0:T(8,128)(2,1)S(1)}, u32[]{:S(2)}, u32[]{:S(2)}) collective-permute-start(bf16[512,128]{1,0:T(8,128)(2,1)S(1)} %get-tuple-element.24), channel_id=1, source_target_pairs={{0,6},{2,0},{4,2},{6,4},{8,14},{10,8},{12,10},{14,12},{16,22},{18,... | collective-permute-start | bytes 393224 | tf_op jit(solution)/shard_map/ppermute | solution.py:30
  38.5 0.5 collective-permute-start.6
  39.0 0.6 collective-permute-start.7
  39.5 1.3 %collective-permute-start.8 = (bf16[1024,128]{1,0:T(8,128)(2,1)S(1)}, bf16[1024,128]{1,0:T(8,128)(2,1)S(1)}, u32[]{:S(2)}, u32[]{:S(2)}) collective-permute-start(bf16[1024,128]{1,0:T(8,128)(2,1)S(1)} %get-tuple-element.30), channel_id=1, source_target_pairs={{8,0},{10,2},{12,4},{14,6},{16,8},{18,10},{20,12},{22,14},{24,16},... | collective-permute-start | bytes 786440 | tf_op jit(solution)/shard_map/ppermute | solution.py:24
  40.8 0.0 copy-done.5
  40.8 1.7 %own.1 = (f32[512,128]{1,0:T(8,128)S(1)}, bf16[1024,128]{1,0:T(8,128)(2,1)S(1)}, bf16[1024,128]{1,0:T(8,128)(2,1)S(1)}) custom-call(bf16[512,128]{1,0:T(8,128)(2,1)S(1)} %get-tuple-element.19.q_ref, bf16[544,128]{1,0:T(8,128)(2,1)S(1)} %copy-done.5, f32[3,1024,128]{2,1,0:T(8,128)S(1)} %get-tuple-element.22.acc, bf16[1040,128]{1,0:T(8,128)(2,1)S(1)} %copy-done.4, ...), custom_call_target="tpu_custom_call" | custom-call | flops 671088640 | bytes 1048576 | tf_op jit(solution)/shard_map/own/pallas_call | solution.py:240
  42.5 0.4 collective-permute-done.5.refs_0_
  42.9 2.1 %collective-permute-done.6.refs_1_ = bf16[512,128]{1,0:T(8,128)(2,1)S(1)} collective-permute-done((bf16[512,128]{1,0:T(8,128)(2,1)S(1)}, bf16[512,128]{1,0:T(8,128)(2,1)S(1)}, u32[]{:S(2)}, u32[]{:S(2)}) %collective-permute-start.6) | collective-permute-done | bytes 131104 | tf_op jit(solution)/shard_map/ppermute | solution.py:30
  45.0 0.0 collective-permute-done.7.refs_2_
  45.0 0.0 copy-done.1
  45.0 0.7 weight_term.1
  45.8 4.2 %all_to_all.24.got_ref = bf16[2,1024,128]{2,1,0:T(8,128)(2,1)S(1)} all-to-all(bf16[2,1024,128]{2,1,0:T(8,128)(2,1)S(1)} %bitcast.26), channel_id=1, replica_groups=mesh['blk'=16,'fsdp'=2] {'fsdp'}, dimensions={0} | all-to-all | bytes 1048576 | tf_op jit(solution)/shard_map/all_to_all | solution.py:390
  49.9 0.8 sum_and_repeat.2
  50.7 3.5 %all-to-all-start.1 = ((bf16[16,64,128]{2,1,0:T(8,128)(2,1)}), bf16[16,64,128]{2,1,0:T(8,128)(2,1)S(1)}, u32[]{:S(2)}, u32[]{:S(2)}) async-start(bf16[16,64,128]{2,1,0:T(8,128)(2,1)} %bitcast.14), calls=%async_computation.1 | async-start | bytes 524288 | tf_op jit(solution)/shard_map/all_to_all | solution.py:394
  54.2 0.0 collective-permute-done.8
  54.3 0.1 add_convert_fusion.1
  54.3 1.3 %collective-permute-start.9 = (bf16[1024,128]{1,0:T(8,128)(2,1)S(1)}, bf16[1024,128]{1,0:T(8,128)(2,1)S(1)}, u32[]{:S(2)}, u32[]{:S(2)}) collective-permute-start(bf16[1024,128]{1,0:T(8,128)(2,1)S(1)} %add_convert_fusion.1), channel_id=1, source_target_pairs={{8,0},{10,2},{12,4},{14,6},{16,8},{18,10},{20,12},{22,14},{24,16},... | collective-permute-start | bytes 786440 | tf_op jit(solution)/shard_map/ppermute | solution.py:24
  55.6 9.3 %all-to-all-done.1.got_ref = bf16[16,64,128]{2,1,0:T(8,128)(2,1)S(1)} async-done(((bf16[16,64,128]{2,1,0:T(8,128)(2,1)}), bf16[16,64,128]{2,1,0:T(8,128)(2,1)S(1)}, u32[]{:S(2)}, u32[]{:S(2)}) %all-to-all-start.1) | async-done | bytes 262176 | tf_op jit(solution)/shard_map/all_to_all | solution.py:394
  64.9 0.8 sum_and_repeat.3
  65.7 3.5 %all-to-all-start.2 = ((bf16[16,64,128]{2,1,0:T(8,128)(2,1)}), bf16[16,64,128]{2,1,0:T(8,128)(2,1)S(1)}, u32[]{:S(2)}, u32[]{:S(2)}) async-start(bf16[16,64,128]{2,1,0:T(8,128)(2,1)} %sum_and_repeat.3), calls=%async_computation.2 | async-start | bytes 524288 | tf_op jit(solution)/shard_map/all_to_all | solution.py:396
  69.2 2.0 %fusion = bf16[1,512,2048]{2,1,0:T(8,128)(2,1)} fusion(bf16[512,128]{1,0:T(8,128)(2,1)S(1)} %get-tuple-element.27, bf16[2048,128]{1,0:T(8,128)(2,1)S(1)} %all_gather.9.w_ref), kind=kOutput, calls=%fused_computation.1 | convolution fusion | flops 269484032 | bytes 2752512 | tf_op jit(solution)/shard_map/dot_general | solution.py:42
  71.3 0.0 collective-permute-done.9
  71.3 0.1 add_convert_fusion
  71.3 0.7 slice_bitcast_fusion
  72.1 6.3 %all-to-all-done.2 = bf16[16,64,128]{2,1,0:T(8,128)(2,1)S(1)} async-done(((bf16[16,64,128]{2,1,0:T(8,128)(2,1)}), bf16[16,64,128]{2,1,0:T(8,128)(2,1)S(1)}, u32[]{:S(2)}, u32[]{:S(2)}) %all-to-all-start.2) | async-done | bytes 262176 | tf_op jit(solution)/shard_map/all_to_all | solution.py:396
  78.3 0.8 %bitcast_convert_fusion = f32[1024,128]{1,0:T(8,128)} fusion(bf16[16,64,128]{2,1,0:T(8,128)(2,1)S(1)} %all-to-all-done.2), kind=kLoop, calls=%fused_computation.4 | loop fusion | flops 131072 | bytes 786432 | tf_op jit(solution)/shard_map/convert_element_type | solution.py:397
  (3 shorter events, 0.0 us)
Async XLA Ops:
  2.5 29.6 %copy-start.4 = (bf16[1040,128]{1,0:T(8,128)(2,1)S(1)}, bf16[1040,128]{1,0:T(8,128)(2,1)}, u32[]{:S(2)}) copy-start(bf16[1040,128]{1,0:T(8,128)(2,1)} %get-tuple-element.21.refs_3_.refs_0_) | copy-start | bytes 798724
  2.5 29.6 %collective-permute-start.4 = (bf16[1040,128]{1,0:T(8,128)(2,1)}, bf16[1040,128]{1,0:T(8,128)(2,1)S(1)}, u32[]{:S(2)}, u32[]{:S(2)}) collective-permute-start(bf16[1040,128]{1,0:T(8,128)(2,1)} %get-tuple-element.21.refs_3_.refs_0_), channel_id=1, source_target_pairs={{0,16},{2,18},{4,20},{6,22},{8,24},{10,26},{12,28},{14,30},{1,17},... | collective-permute-start | bytes 798728 | tf_op jit(solution)/shard_map/ppermute | solution.py:24
  8.7 23.5 %collective-permute-start.3 = (bf16[1040,128]{1,0:T(8,128)(2,1)}, bf16[1040,128]{1,0:T(8,128)(2,1)S(1)}, u32[]{:S(2)}, u32[]{:S(2)}) collective-permute-start(bf16[1040,128]{1,0:T(8,128)(2,1)} %get-tuple-element.21.refs_3_.refs_0_), channel_id=1, source_target_pairs={{0,8},{2,10},{4,12},{6,14},{8,16},{10,18},{12,20},{14,22},{16,24},... | collective-permute-start | bytes 798728 | tf_op jit(solution)/shard_map/ppermute | solution.py:24
  12.2 19.9 %collective-permute-start.2 = (bf16[544,128]{1,0:T(8,128)(2,1)}, bf16[544,128]{1,0:T(8,128)(2,1)S(1)}, u32[]{:S(2)}, u32[]{:S(2)}) collective-permute-start(bf16[544,128]{1,0:T(8,128)(2,1)} %get-tuple-element.20.o_ref), channel_id=1, source_target_pairs={{0,6},{2,0},{4,2},{6,4},{8,14},{10,8},{12,10},{14,12},{16,22},{18,... | collective-permute-start | bytes 417800 | tf_op jit(solution)/shard_map/ppermute | solution.py:30
  14.7 17.5 %collective-permute-start.1 = (bf16[544,128]{1,0:T(8,128)(2,1)}, bf16[544,128]{1,0:T(8,128)(2,1)S(1)}, u32[]{:S(2)}, u32[]{:S(2)}) collective-permute-start(bf16[544,128]{1,0:T(8,128)(2,1)} %get-tuple-element.20.o_ref), channel_id=1, source_target_pairs={{0,4},{2,6},{4,0},{6,2},{8,12},{10,14},{12,8},{14,10},{16,20},{18,... | collective-permute-start | bytes 417800 | tf_op jit(solution)/shard_map/ppermute | solution.py:30
  15.2 17.0 %collective-permute-start = (bf16[544,128]{1,0:T(8,128)(2,1)}, bf16[544,128]{1,0:T(8,128)(2,1)S(1)}, u32[]{:S(2)}, u32[]{:S(2)}) collective-permute-start(bf16[544,128]{1,0:T(8,128)(2,1)} %get-tuple-element.20.o_ref), channel_id=1, source_target_pairs={{0,2},{2,4},{4,6},{6,0},{8,10},{10,12},{12,14},{14,8},{16,18},{18,... | collective-permute-start | bytes 417800 | tf_op jit(solution)/shard_map/ppermute | solution.py:30
  18.1 1.6 %copy-start = (bf16[1,512,2048]{2,1,0:T(8,128)(2,1)S(1)}, bf16[1,512,2048]{2,1,0:T(8,128)(2,1)}, u32[]{:S(2)}) copy-start(bf16[1,512,2048]{2,1,0:T(8,128)(2,1)} %param.9) | copy-start | bytes 6291460
  19.7 0.7 copy-start.2
  32.2 8.7 %copy-start.5 = (bf16[544,128]{1,0:T(8,128)(2,1)S(1)}, bf16[544,128]{1,0:T(8,128)(2,1)}, u32[]{:S(2)}) copy-start(bf16[544,128]{1,0:T(8,128)(2,1)} %get-tuple-element.20.o_ref) | copy-start | bytes 417796
  36.9 8.1 %copy-start.1 = (bf16[1,512,2048]{2,1,0:T(8,128)(2,1)S(1)}, bf16[1,512,2048]{2,1,0:T(8,128)(2,1)}, u32[]{:S(2)}) copy-start(bf16[1,512,2048]{2,1,0:T(8,128)(2,1)} %param.9) | copy-start | bytes 6291460
  37.0 8.1 %copy-start.3 = (f32[128]{0:T(128)S(1)}, f32[128]{0:T(128)}, u32[]{:S(2)}) copy-start(f32[128]{0:T(128)} %param.11) | copy-start | bytes 1540
  37.0 6.0 %collective-permute-start.5 = (bf16[512,128]{1,0:T(8,128)(2,1)S(1)}, bf16[512,128]{1,0:T(8,128)(2,1)S(1)}, u32[]{:S(2)}, u32[]{:S(2)}) collective-permute-start(bf16[512,128]{1,0:T(8,128)(2,1)S(1)} %get-tuple-element.24), channel_id=1, source_target_pairs={{0,6},{2,0},{4,2},{6,4},{8,14},{10,8},{12,10},{14,12},{16,22},{18,... | collective-permute-start | bytes 393224 | tf_op jit(solution)/shard_map/ppermute | solution.py:30
  38.5 6.5 %collective-permute-start.6 = (bf16[512,128]{1,0:T(8,128)(2,1)S(1)}, bf16[512,128]{1,0:T(8,128)(2,1)S(1)}, u32[]{:S(2)}, u32[]{:S(2)}) collective-permute-start(bf16[512,128]{1,0:T(8,128)(2,1)S(1)} %get-tuple-element.25), channel_id=1, source_target_pairs={{0,4},{2,6},{4,0},{6,2},{8,12},{10,14},{12,8},{14,10},{16,20},{18,... | collective-permute-start | bytes 393224 | tf_op jit(solution)/shard_map/ppermute | solution.py:30
  39.0 6.0 %collective-permute-start.7 = (bf16[512,128]{1,0:T(8,128)(2,1)S(1)}, bf16[512,128]{1,0:T(8,128)(2,1)S(1)}, u32[]{:S(2)}, u32[]{:S(2)}) collective-permute-start(bf16[512,128]{1,0:T(8,128)(2,1)S(1)} %get-tuple-element.26), channel_id=1, source_target_pairs={{0,2},{2,4},{4,6},{6,0},{8,10},{10,12},{12,14},{14,8},{16,18},{18,... | collective-permute-start | bytes 393224 | tf_op jit(solution)/shard_map/ppermute | solution.py:30
  39.5 14.7 %collective-permute-start.8 = (bf16[1024,128]{1,0:T(8,128)(2,1)S(1)}, bf16[1024,128]{1,0:T(8,128)(2,1)S(1)}, u32[]{:S(2)}, u32[]{:S(2)}) collective-permute-start(bf16[1024,128]{1,0:T(8,128)(2,1)S(1)} %get-tuple-element.30), channel_id=1, source_target_pairs={{8,0},{10,2},{12,4},{14,6},{16,8},{18,10},{20,12},{22,14},{24,16},... | collective-permute-start | bytes 786440 | tf_op jit(solution)/shard_map/ppermute | solution.py:24
  50.7 14.2 %all-to-all-start.1 = ((bf16[16,64,128]{2,1,0:T(8,128)(2,1)}), bf16[16,64,128]{2,1,0:T(8,128)(2,1)S(1)}, u32[]{:S(2)}, u32[]{:S(2)}) async-start(bf16[16,64,128]{2,1,0:T(8,128)(2,1)} %bitcast.14), calls=%async_computation.1 | async-start | bytes 524288 | tf_op jit(solution)/shard_map/all_to_all | solution.py:394
  54.3 16.9 %collective-permute-start.9 = (bf16[1024,128]{1,0:T(8,128)(2,1)S(1)}, bf16[1024,128]{1,0:T(8,128)(2,1)S(1)}, u32[]{:S(2)}, u32[]{:S(2)}) collective-permute-start(bf16[1024,128]{1,0:T(8,128)(2,1)S(1)} %add_convert_fusion.1), channel_id=1, source_target_pairs={{8,0},{10,2},{12,4},{14,6},{16,8},{18,10},{20,12},{22,14},{24,16},... | collective-permute-start | bytes 786440 | tf_op jit(solution)/shard_map/ppermute | solution.py:24
  65.7 12.7 %all-to-all-start.2 = ((bf16[16,64,128]{2,1,0:T(8,128)(2,1)}), bf16[16,64,128]{2,1,0:T(8,128)(2,1)S(1)}, u32[]{:S(2)}, u32[]{:S(2)}) async-start(bf16[16,64,128]{2,1,0:T(8,128)(2,1)} %sum_and_repeat.3), calls=%async_computation.2 | async-start | bytes 524288 | tf_op jit(solution)/shard_map/all_to_all | solution.py:396

commit v3 on v2

--- a/solution.py
+++ b/solution.py
@@ -62,7 +62,7 @@
 
 
 def pack_kernel(
-    k_ref, v_ref, o_ref, lse_ref, delta_ref, docs_ref, kv_out, o_out,
+    k_ref, v_ref, o_ref, lse_ref, delta_ref, docs_ref, gain_ref, kv_out, o_out, gain_out,
     lse_sc, delta_sc, docs_sc, sems,
 ):
     tokens, width = k_ref.shape
@@ -74,6 +74,7 @@
             (k_ref, kv_out.at[:tokens]),
             (v_ref, kv_out.at[tokens : 2 * tokens]),
             (o_ref, o_out.at[:tokens]),
+            (gain_ref, gain_out),
         ],
         sems,
     )
@@ -100,8 +101,14 @@
         copy.wait()
 
 
-def query_kernel(h_ref, w_ref, gain_ref, query_out, q_pre_out):
-    q_pre = dot_nn(h_ref[...], w_ref[...])
+def query_kernel(parts, f_ref, h_ref, gain_ref, *refs):
+    w_refs, (query_out, q_pre_out, w_out) = refs[:parts], refs[parts:]
+    rows = w_refs[0].shape[0]
+    q_pre = jnp.zeros(q_pre_out.shape, F32)
+    for k in range(parts):
+        at = pl.multiple_of((f_ref[0] - k + parts) % parts * rows, rows)
+        q_pre += dot_nn(h_ref[:, pl.ds(at, rows)], w_refs[k][...])
+        w_out[pl.ds(at, rows), :] = w_refs[k][...]
     inverse = lax.rsqrt(jnp.mean(q_pre * q_pre, axis=-1, keepdims=True) + 1e-06)
     q_pre_out[...] = q_pre
     query_out[...] = (q_pre * inverse * gain_ref[...]).astype(BF)
@@ -251,23 +258,42 @@
     return out[0], out[1:]
 
 
-def weight_kernel(parts, h_ref, q_pre_ref, gain_ref, own_ref, *refs):
+def pre_kernel(parts, halves, f_ref, h_ref, q_pre_ref, gain_ref, own_ref, *refs):
     grad_query = own_ref[...]
     for ref in refs[:parts]:
         grad_query = grad_query + ref[...].astype(F32)
-    pre_out, term_out = refs[parts:]
+    pre_out, turned_out, give_refs = refs[parts], refs[parts + 1], refs[parts + 2 :]
     q_pre = q_pre_ref[...]
     inverse = lax.rsqrt(jnp.mean(q_pre * q_pre, axis=-1, keepdims=True) + 1e-06)
     normed = q_pre * inverse
     scaled = grad_query * gain_ref[...]
     grad_pre = inverse * (scaled - normed * jnp.mean(scaled * normed, axis=-1, keepdims=True))
-    pre_out[...] = grad_pre.astype(BF)
-    turned_pre = grad_pre.astype(BF).astype(F32).T.astype(BF)
-    columns = h_ref.shape[1]
-    step = math.gcd(columns, 512)
-    for c in range(0, columns, step):
-        term = dot_nn(turned_pre, h_ref[:, c : c + step])
-        term_out[c : c + step, :] = term.T.astype(BF)
+    grad_pre = grad_pre.astype(BF)
+    pre_out[...] = grad_pre
+    turned_pre = grad_pre.astype(F32).T.astype(BF)
+    turned_out[...] = turned_pre
+    for k in range(1, halves):
+        rows_of_term(turned_pre, h_ref, (f_ref[0] + k) % halves, give_refs[k - 1])
+
+
+def keep_kernel(f_ref, h_ref, turned_ref, keep_ref):
+    rows_of_term(turned_ref[...], h_ref, f_ref[0], keep_ref)
+
+
+def rows_of_term(turned_pre, h_ref, owner, out_ref):
+    rows = out_ref.shape[0]
+    chunk = math.gcd(rows, 512)
+    for c in range(0, rows, chunk):
+        at = pl.multiple_of(owner * rows + c, chunk)
+        term = dot_nn(turned_pre, h_ref[:, pl.ds(at, chunk)])
+        out_ref[c : c + chunk, :] = term.T.astype(out_ref.dtype)
+
+
+def add_kernel(keep_ref, *refs):
+    total = keep_ref[...]
+    for ref in refs[:-1]:
+        total = total + ref[...].astype(F32)
+    refs[-1][...] = total.astype(BF)
 
 
 def sum_kernel(got_ref, out_ref):
@@ -319,19 +345,24 @@
     r = (lax.axis_index("blk") % group).astype(jnp.int32)[None]
     per = tokens // width
 
-    kv_own, o_own = pl.pallas_call(
+    w_parts = [w_query] + [
+        lax.ppermute(w_query, "fsdp", [(i, (i + k) % halves) for i in range(halves)])
+        for k in range(1, halves)
+    ]
+    kv_own, o_own, gain = pl.pallas_call(
         pack_kernel,
         out_shape=[
             jax.ShapeDtypeStruct((2 * tokens + -(-per // 16) * 16, width), BF),
             jax.ShapeDtypeStruct((tokens + -(-7 * per // 16) * 16, width), BF),
+            jax.ShapeDtypeStruct(gain.shape, F32),
         ],
-        in_specs=hbm_specs(6),
-        out_specs=vmem_specs(2),
+        in_specs=hbm_specs(7),
+        out_specs=vmem_specs(3),
         scratch_shapes=[
             pltpu.VMEM((per, width), F32),
             pltpu.VMEM((per, width), F32),
             pltpu.VMEM((per, width), jnp.int32),
-            pltpu.SemaphoreType.DMA((6,)),
+            pltpu.SemaphoreType.DMA((7,)),
         ],
         compiler_params=params(PACK_MIB),
         name="pack",
@@ -342,23 +373,26 @@
         logsumexp.reshape(per, width),
         row_delta.reshape(per, width),
         doc_ids.reshape(per, width),
+        gain,
     )
-    kv_list = [kv_own] + [shifted(kv_own, group * s) for s in range(far, 0, -1)][::-1]
+    kv_list = [kv_own]
+    for _ in range(1, far + 1):
+        kv_list.append(shifted(kv_list[-1], group))
     o_list = [o_own] + [turned(o_own, k, group) for k in range(1, group)]
 
-    projection = lax.all_gather(w_query, "fsdp", axis=0, tiled=True)
+    f = lax.axis_index("fsdp").astype(jnp.int32)[None]
     q_like = jax.ShapeDtypeStruct((tokens, width), F32)
-    query, q_pre = pl.pallas_call(
-        query_kernel,
-        out_shape=[
-            jax.ShapeDtypeStruct((tokens, width), BF),
-            q_like,
-        ],
-        in_specs=vmem_specs(1) + whole_specs([projection, gain]),
-        out_specs=vmem_specs(1) + whole_specs([q_like]),
+    w_like = jax.ShapeDtypeStruct((inputs.shape[1], width), BF)
+    query, q_pre, projection = pl.pallas_call(
+        functools.partial(query_kernel, halves),
+        out_shape=[jax.ShapeDtypeStruct((tokens, width), BF), q_like, w_like],
+        in_specs=[pl.BlockSpec(memory_space=pltpu.SMEM)]
+        + vmem_specs(2)
+        + whole_specs(w_parts),
+        out_specs=vmem_specs(1) + whole_specs([q_like, w_like]),
         compiler_params=params(8),
         name="query",
-    )(inputs, projection, gain)
+    )(f, inputs, gain, *w_parts)
     groups = [list(range(i, i + group)) for i in range(0, blocks, group)]
     q_all = lax.all_gather(query, "blk", axis_index_groups=groups)
 
@@ -367,17 +401,45 @@
     dq_back = [turned(dq_list[k - 1], -k, group) for k in range(1, group)]
     back = shifted(grad_kv, -group)
     dq_own, dkv_list = own(far, tokens, width, query, o_own, acc, kv_list)
-    grad_pre, weight_term = pl.pallas_call(
-        functools.partial(weight_kernel, len(dq_back)),
-        out_shape=[
-            jax.ShapeDtypeStruct((tokens, width), BF),
-            jax.ShapeDtypeStruct((inputs.shape[1], width), BF),
-        ],
-        in_specs=vmem_specs(1) + whole_specs([q_pre, gain]) + vmem_specs(1 + len(dq_back)),
-        out_specs=vmem_specs(2),
+    owned = inputs.shape[1] // halves
+    smem = [pl.BlockSpec(memory_space=pltpu.SMEM)]
+    block = jax.ShapeDtypeStruct((tokens, width), BF)
+    turned_block = jax.ShapeDtypeStruct((width, tokens), BF)
+    rows = jax.ShapeDtypeStruct((owned, width), BF)
+    grad_pre, turned_pre, *give = pl.pallas_call(
+        functools.partial(pre_kernel, len(dq_back), halves),
+        out_shape=[block, turned_block] + [rows] * (halves - 1),
+        in_specs=smem
+        + vmem_specs(1)
+        + whole_specs([q_pre, gain])
+        + vmem_specs(1 + len(dq_back)),
+        out_specs=vmem_specs(1 + halves),
         compiler_params=params(16),
-        name="weight_term",
-    )(inputs, q_pre, gain, dq_own, *dq_back)
+        name="give_term",
+    )(f, inputs, q_pre, gain, dq_own, *dq_back)
+    got = [
+        lax.ppermute(give[k - 1], "fsdp", [(i, (i + k) % halves) for i in range(halves)])
+        for k in range(1, halves)
+    ]
+    keep = pl.pallas_call(
+        keep_kernel,
+        out_shape=jax.ShapeDtypeStruct((owned, width), F32),
+        in_specs=smem + vmem_specs(2),
+        out_specs=vmem_specs(1)[0],
+        compiler_params=params(16),
+        cost_estimate=pl.CostEstimate(
+            flops=2 * tokens * owned * width, bytes_accessed=2 * tokens * owned, transcendentals=0
+        ),
+        name="keep_term",
+    )(f, inputs, turned_pre)
+    terms = pl.pallas_call(
+        add_kernel,
+        out_shape=rows,
+        in_specs=vmem_specs(halves),
+        out_specs=vmem_specs(1)[0],
+        compiler_params=params(8),
+        name="add_terms",
+    )(keep, *got)
     grad_hidden = dot_nt(grad_pre, projection).astype(BF)
 
     for s in range(far - 1, -1, -1):
@@ -385,10 +447,7 @@
         if s > 0:
             back = shifted(grad_kv, -group)
 
-    owned = weight_term.shape[0] // halves
     share = -(-owned // blocks)
-    got = lax.all_to_all(weight_term, "fsdp", 0, 0, tiled=True)
-    terms = sum_and_repeat(got.reshape(halves, owned, width), 1)[0]
     if share * blocks != owned:
         terms = jnp.pad(terms, ((0, share * blocks - owned), (0, 0)))
     got = lax.all_to_all(terms, "blk", 0, 0, tiled=True)

time: 79.7 us -> 84.8 us (1.064)
  waiting for transfers between devices: 18.1 us -> 25.1 us
  blocking collectives: 17.4 us -> 11.1 us
  starting transfers between devices: 25.4 us -> 28.7 us
  local copies, waits for them, and re-layouts: 2.99 us -> 3.93 us
    ppermute x4, waiting for transfers between devices: 0.01 us -> 7.44 us  [shifted(): return lax.ppermute(value, 'blk', pairs)]
    all_to_all x1 -> x0, blocking collectives: 4.15 us -> none  [step(): got = lax.all_to_all(weight_term, 'fsdp', 0, 0, tiled=True)]
    all_to_all x1, starting transfers between devices: 3.53 us -> 6.51 us  [step(): got = lax.all_to_all(terms, 'blk', 0, 0, tiled=True)]
    all_gather x1 -> x0, blocking collectives: 2.38 us -> none  [step(): projection = lax.all_gather(w_query, 'fsdp', axis=0, tiled=True)]
    all_to_all x1, waiting for transfers between devices: 9.31 us -> 7.75 us  [step(): got = lax.all_to_all(terms, 'blk', 0, 0, tiled=True)]
    ppermute x6, waiting for transfers between devices: 2.52 us -> 3.65 us  [turned(): return lax.ppermute(value, 'blk', pairs)]
    pallas_call x2 -> x4, Pallas kernels: 1.54 us -> 2.58 us  [the longest x1 0.8 us: step(): pl.pallas_call(functools.partial(query_kernel, halves), out_shape=[jax.Sh...]
    unnamed x12 -> x14, local copies, waits for them, and re-layouts: 2.27 us -> 3.22 us
  transfers between devices with their start and end apart: 12 -> 14, of which waited for: 4 -> 7; matrix products, arithmetic and copies ran while one was open for 4% -> 3% of each run, Pallas kernels for 6% -> 5%
where the time goes in v3:
time: 84.8 us; the launch traced here: 84.3 us
  starting transfers between devices  28.7 us (34%)
  waiting for transfers between devices  25.1 us (30%)
  Pallas kernels  11.6 us (14%)
  blocking collectives  11.1 us (13%)
  local copies, waits for them, and re-layouts  3.93 us (5%)
  matrix products  2.03 us (2%)
  other arithmetic  0.99 us (1%)
    ppermute x4, starting transfers between devices, shifted(): return lax.ppermute(value, 'blk', pairs)  11.8 us
    all_gather x1, blocking collectives, step(): q_all = lax.all_gather(query, 'blk', axis_index_groups=groups)  11.1 us
    all_to_all x1, waiting for transfers between devices, step(): got = lax.all_to_all(terms, 'blk', 0, 0, tiled=True)  7.75 us
    ppermute x4, waiting for transfers between devices, shifted(): return lax.ppermute(value, 'blk', pairs)  7.44 us
    ppermute x6, starting transfers between devices, turned(): return lax.ppermute(value, 'blk', pairs)  6.71 us
    all_to_all x1, starting transfers between devices, step(): got = lax.all_to_all(terms, 'blk', 0, 0, tiled=True)  6.51 us
    all_to_all x1, waiting for transfers between devices, step(): lax.all_to_all(everywhere.reshape(-1, width), 'blk', 0, 0, tiled=True)  6.21 us
    pallas_call x1, Pallas kernels, others(): pl.pallas_call(functools.partial(others_kernel, group, far, tokens, width...  4.76 us
  transfers between devices with their start and end apart: 14, of which 7 were waited for; matrix products, arithmetic and copies ran while one was open for 3% of the time, Pallas kernels for 5%

profile of v3, /device:TPU:0, one launch (start us, length us, event | category | flops | bytes accessed | tf_op | source)
XLA Modules:
  0.0 84.3 jit_solution(4198877009398873734)
XLA Ops:
  0.6 1.9 %pack.1 = (bf16[1040,128]{1,0:T(8,128)(2,1)}, bf16[544,128]{1,0:T(8,128)(2,1)}, f32[1,128]{1,0:T(1,128)}) custom-call(bf16[512,128]{1,0:T(8,128)(2,1)} %bitcast.27, bf16[512,128]{1,0:T(8,128)(2,1)} %bitcast.28, bf16[512,128]{1,0:T(8,128)(2,1)} %bitcast.29, f32[4,128]{1,0:T(4,128)} %bitcast.30, f32[4,128]{1,0:T(4,128)} %bitcast.31, s32[4,128]{1,0:T(4,128)} %bitcast.32, ...), custom_call_target="tpu_custom_call" | custom-call | tf_op jit(solution)/shard_map/pack/pallas_call | solution.py:352
  2.5 5.0 %collective-permute-start.4 = (bf16[1040,128]{1,0:T(8,128)(2,1)}, bf16[1040,128]{1,0:T(8,128)(2,1)S(1)}, u32[]{:S(2)}, u32[]{:S(2)}) collective-permute-start(bf16[1040,128]{1,0:T(8,128)(2,1)} %get-tuple-element.25.refs_3_.refs_0_), channel_id=1, source_target_pairs={{0,8},{2,10},{4,12},{6,14},{8,16},{10,18},{12,20},{14,22},{16,24},... | collective-permute-start | bytes 798728 | tf_op jit(solution)/shard_map/ppermute | solution.py:24
  7.5 0.1 collective-permute-start
  7.6 5.9 %collective-permute-done.4.refs_4_.refs_1_ = bf16[1040,128]{1,0:T(8,128)(2,1)S(1)} collective-permute-done((bf16[1040,128]{1,0:T(8,128)(2,1)}, bf16[1040,128]{1,0:T(8,128)(2,1)S(1)}, u32[]{:S(2)}, u32[]{:S(2)}) %collective-permute-start.4) | collective-permute-done | bytes 266272 | tf_op jit(solution)/shard_map/ppermute | solution.py:24
  13.4 4.3 %collective-permute-start.5 = (bf16[1040,128]{1,0:T(8,128)(2,1)S(1)}, bf16[1040,128]{1,0:T(8,128)(2,1)S(1)}, u32[]{:S(2)}, u32[]{:S(2)}) collective-permute-start(bf16[1040,128]{1,0:T(8,128)(2,1)S(1)} %collective-permute-done.4.refs_4_.refs_1_), channel_id=1, source_target_pairs={{0,8},{2,10},{4,12},{6,14},{8,16},{10,18},{12,20},{14,22},{16,24},... | collective-permute-start | bytes 798728 | tf_op jit(solution)/shard_map/ppermute | solution.py:24
  17.7 2.5 %collective-permute-start.3 = (bf16[544,128]{1,0:T(8,128)(2,1)}, bf16[544,128]{1,0:T(8,128)(2,1)S(1)}, u32[]{:S(2)}, u32[]{:S(2)}) collective-permute-start(bf16[544,128]{1,0:T(8,128)(2,1)} %get-tuple-element.24.o_ref), channel_id=1, source_target_pairs={{0,6},{2,0},{4,2},{6,4},{8,14},{10,8},{12,10},{14,12},{16,22},{18,... | collective-permute-start | bytes 417800 | tf_op jit(solution)/shard_map/ppermute | solution.py:30
  20.2 0.5 collective-permute-start.2
  20.7 0.6 collective-permute-start.1
  21.3 0.0 collective-permute-done.refs_1_
  21.3 1.6 %copy-done = bf16[1,512,2048]{2,1,0:T(8,128)(2,1)S(1)} copy-done((bf16[1,512,2048]{2,1,0:T(8,128)(2,1)S(1)}, bf16[1,512,2048]{2,1,0:T(8,128)(2,1)}, u32[]{:S(2)}) %copy-start) | copy-done | bytes 2097176
  22.9 0.9 %copy-done.2 = bf16[1024,128]{1,0:T(8,128)(2,1)S(1)} copy-done((bf16[1024,128]{1,0:T(8,128)(2,1)S(1)}, bf16[1024,128]{1,0:T(8,128)(2,1)}, u32[]{:S(2)}) %copy-start.2) | copy-done | bytes 262168
  23.9 0.7 copy-done.3
  24.5 0.8 query.1
  25.3 11.1 %all-gather = bf16[2048,128]{1,0:T(8,128)(2,1)S(1)} all-gather(bf16[512,128]{1,0:T(8,128)(2,1)S(1)} %get-tuple-element.23.q_ref), channel_id=2, replica_groups={{0,2,4,6},{8,10,12,14},{16,18,20,22},{24,26,28,30},{1,3,5,7},{9,11,13,1..., dimensions={0}, use_global_device_ids=true | all-gather | bytes 655360 | tf_op jit(solution)/shard_map/all_gather | solution.py:397
  36.4 0.0 collective-permute-done.3.refs_2_
  36.4 0.0 collective-permute-done.2.refs_1_
  36.4 0.0 collective-permute-done.1.refs_0_
  36.5 0.0 collective-permute-done.5.refs_5_
  36.5 0.0 copy-start.6
  36.5 4.8 %others.1 = (bf16[512,128]{1,0:T(8,128)(2,1)S(1)}, bf16[512,128]{1,0:T(8,128)(2,1)S(1)}, bf16[512,128]{1,0:T(8,128)(2,1)S(1)}, bf16[1024,128]{1,0:T(8,128)(2,1)S(1)}, f32[3,1024,128]{2,1,0:T(8,128)S(1)}) custom-call(s32[1]{0:T(128)} %bitcast.9.r_ref, bf16[4,512,128]{2,1,0:T(8,128)(2,1)S(1)} %bitcast.26, bf16[544,128]{1,0:T(8,128)(2,1)S(1)} %collective-permute-done.1.refs_0_, ...), custom_call_target="tpu_custom_call" | custom-call | flops 2013265920 | bytes 3145728 | tf_op jit(solution)/shard_map/others/pallas_call | solution.py:233
  41.3 0.0 copy-start.1
  41.3 0.0 copy-start.4
  41.3 1.6 %collective-permute-start.6 = (bf16[512,128]{1,0:T(8,128)(2,1)S(1)}, bf16[512,128]{1,0:T(8,128)(2,1)S(1)}, u32[]{:S(2)}, u32[]{:S(2)}) collective-permute-start(bf16[512,128]{1,0:T(8,128)(2,1)S(1)} %get-tuple-element.28), channel_id=1, source_target_pairs={{0,6},{2,0},{4,2},{6,4},{8,14},{10,8},{12,10},{14,12},{16,22},{18,... | collective-permute-start | bytes 393224 | tf_op jit(solution)/shard_map/ppermute | solution.py:30
  42.8 1.0 %collective-permute-start.7 = (bf16[512,128]{1,0:T(8,128)(2,1)S(1)}, bf16[512,128]{1,0:T(8,128)(2,1)S(1)}, u32[]{:S(2)}, u32[]{:S(2)}) collective-permute-start(bf16[512,128]{1,0:T(8,128)(2,1)S(1)} %get-tuple-element.29), channel_id=1, source_target_pairs={{0,4},{2,6},{4,0},{6,2},{8,12},{10,14},{12,8},{14,10},{16,20},{18,... | collective-permute-start | bytes 393224 | tf_op jit(solution)/shard_map/ppermute | solution.py:30
  43.8 0.6 collective-permute-start.8
  44.4 1.7 %own.1 = (f32[512,128]{1,0:T(8,128)S(1)}, bf16[1024,128]{1,0:T(8,128)(2,1)S(1)}, bf16[1024,128]{1,0:T(8,128)(2,1)S(1)}) custom-call(bf16[512,128]{1,0:T(8,128)(2,1)S(1)} %get-tuple-element.23.q_ref, bf16[544,128]{1,0:T(8,128)(2,1)S(1)} %copy-done.6, f32[3,1024,128]{2,1,0:T(8,128)S(1)} %get-tuple-element.26.acc, bf16[1040,128]{1,0:T(8,128)(2,1)S(1)} %copy-done.5, ...), custom_call_target="tpu_custom_call" | custom-call | flops 671088640 | bytes 1048576 | tf_op jit(solution)/shard_map/own/pallas_call | solution.py:247
  46.1 0.2 collective-permute-done.6.refs_0_
  46.3 1.5 %collective-permute-done.7.refs_1_ = bf16[512,128]{1,0:T(8,128)(2,1)S(1)} collective-permute-done((bf16[512,128]{1,0:T(8,128)(2,1)S(1)}, bf16[512,128]{1,0:T(8,128)(2,1)S(1)}, u32[]{:S(2)}, u32[]{:S(2)}) %collective-permute-start.7) | collective-permute-done | bytes 131104 | tf_op jit(solution)/shard_map/ppermute | solution.py:30
  47.8 1.9 %collective-permute-done.8.refs_2_ = bf16[512,128]{1,0:T(8,128)(2,1)S(1)} collective-permute-done((bf16[512,128]{1,0:T(8,128)(2,1)S(1)}, bf16[512,128]{1,0:T(8,128)(2,1)S(1)}, u32[]{:S(2)}, u32[]{:S(2)}) %collective-permute-start.8) | collective-permute-done | bytes 131104 | tf_op jit(solution)/shard_map/ppermute | solution.py:30
  49.7 0.6 give_term.1
  50.3 0.1 collective-permute-start.11
  50.4 1.3 %collective-permute-start.9 = (bf16[1024,128]{1,0:T(8,128)(2,1)S(1)}, bf16[1024,128]{1,0:T(8,128)(2,1)S(1)}, u32[]{:S(2)}, u32[]{:S(2)}) collective-permute-start(bf16[1024,128]{1,0:T(8,128)(2,1)S(1)} %get-tuple-element.35), channel_id=1, source_target_pairs={{8,0},{10,2},{12,4},{14,6},{16,8},{18,10},{20,12},{22,14},{24,16},... | collective-permute-start | bytes 786440 | tf_op jit(solution)/shard_map/ppermute | solution.py:24
  51.7 0.4 keep_term.1.keep_ref
  52.1 0.0 collective-permute-done.11.refs_0_
  52.1 0.7 add_terms.1
  52.9 6.5 %all-to-all-start = ((bf16[16,64,128]{2,1,0:T(8,128)(2,1)}), bf16[16,64,128]{2,1,0:T(8,128)(2,1)S(1)}, u32[]{:S(2)}, u32[]{:S(2)}) async-start(bf16[16,64,128]{2,1,0:T(8,128)(2,1)} %bitcast.14), calls=%async_computation | async-start | bytes 524288 | tf_op jit(solution)/shard_map/all_to_all | solution.py:453
  59.4 1.6 %collective-permute-done.9 = bf16[1024,128]{1,0:T(8,128)(2,1)S(1)} collective-permute-done((bf16[1024,128]{1,0:T(8,128)(2,1)S(1)}, bf16[1024,128]{1,0:T(8,128)(2,1)S(1)}, u32[]{:S(2)}, u32[]{:S(2)}) %collective-permute-start.9) | collective-permute-done | bytes 262176 | tf_op jit(solution)/shard_map/ppermute | solution.py:24
  61.0 0.1 add_convert_fusion.1
  61.1 1.3 %collective-permute-start.10 = (bf16[1024,128]{1,0:T(8,128)(2,1)S(1)}, bf16[1024,128]{1,0:T(8,128)(2,1)S(1)}, u32[]{:S(2)}, u32[]{:S(2)}) collective-permute-start(bf16[1024,128]{1,0:T(8,128)(2,1)S(1)} %add_convert_fusion.1), channel_id=1, source_target_pairs={{8,0},{10,2},{12,4},{14,6},{16,8},{18,10},{20,12},{22,14},{24,16},... | collective-permute-start | bytes 786440 | tf_op jit(solution)/shard_map/ppermute | solution.py:24
  62.4 7.8 %all-to-all-done.got_ref = bf16[16,64,128]{2,1,0:T(8,128)(2,1)S(1)} async-done(((bf16[16,64,128]{2,1,0:T(8,128)(2,1)}), bf16[16,64,128]{2,1,0:T(8,128)(2,1)S(1)}, u32[]{:S(2)}, u32[]{:S(2)}) %all-to-all-start) | async-done | bytes 262176 | tf_op jit(solution)/shard_map/all_to_all | solution.py:453
  70.1 0.8 sum_and_repeat.1
  70.9 3.5 %all-to-all-start.1 = ((bf16[16,64,128]{2,1,0:T(8,128)(2,1)}), bf16[16,64,128]{2,1,0:T(8,128)(2,1)S(1)}, u32[]{:S(2)}, u32[]{:S(2)}) async-start(bf16[16,64,128]{2,1,0:T(8,128)(2,1)} %sum_and_repeat.1), calls=%async_computation.1 | async-start | bytes 524288 | tf_op jit(solution)/shard_map/all_to_all | solution.py:455
  74.4 2.0 %fusion = bf16[1,512,2048]{2,1,0:T(8,128)(2,1)} fusion(bf16[512,128]{1,0:T(8,128)(2,1)S(1)} %get-tuple-element.31, bf16[2048,128]{1,0:T(8,128)(2,1)S(1)} %get-tuple-element.32), kind=kOutput, calls=%fused_computation.1 | convolution fusion | flops 269484032 | bytes 2752512 | tf_op jit(solution)/shard_map/dot_general | solution.py:42
  76.5 0.0 collective-permute-done.10
  76.5 0.1 add_convert_fusion
  76.5 0.7 slice_bitcast_fusion
  77.2 6.2 %all-to-all-done.1 = bf16[16,64,128]{2,1,0:T(8,128)(2,1)S(1)} async-done(((bf16[16,64,128]{2,1,0:T(8,128)(2,1)}), bf16[16,64,128]{2,1,0:T(8,128)(2,1)S(1)}, u32[]{:S(2)}, u32[]{:S(2)}) %all-to-all-start.1) | async-done | bytes 262176 | tf_op jit(solution)/shard_map/all_to_all | solution.py:455
  83.5 0.8 %bitcast_convert_fusion = f32[1024,128]{1,0:T(8,128)} fusion(bf16[16,64,128]{2,1,0:T(8,128)(2,1)S(1)} %all-to-all-done.1), kind=kLoop, calls=%fused_computation.4 | loop fusion | flops 131072 | bytes 786432 | tf_op jit(solution)/shard_map/convert_element_type | solution.py:456
  (8 shorter events, 0.0 us)
Async XLA Ops:
  2.5 10.9 %collective-permute-start.4 = (bf16[1040,128]{1,0:T(8,128)(2,1)}, bf16[1040,128]{1,0:T(8,128)(2,1)S(1)}, u32[]{:S(2)}, u32[]{:S(2)}) collective-permute-start(bf16[1040,128]{1,0:T(8,128)(2,1)} %get-tuple-element.25.refs_3_.refs_0_), channel_id=1, source_target_pairs={{0,8},{2,10},{4,12},{6,14},{8,16},{10,18},{12,20},{14,22},{16,24},... | collective-permute-start | bytes 798728 | tf_op jit(solution)/shard_map/ppermute | solution.py:24
  7.5 13.8 %collective-permute-start = (bf16[1024,128]{1,0:T(8,128)(2,1)}, bf16[1024,128]{1,0:T(8,128)(2,1)S(1)}, u32[]{:S(2)}, u32[]{:S(2)}) collective-permute-start(bf16[1024,128]{1,0:T(8,128)(2,1)} %refs_0_.1), channel_id=1, source_target_pairs={{0,1},{1,0},{2,3},{3,2},{4,5},{5,4},{6,7},{7,6},{8,9},{9,8},{10,11... | collective-permute-start | bytes 786440 | tf_op jit(solution)/shard_map/ppermute | solution.py:349
  13.4 23.0 %collective-permute-start.5 = (bf16[1040,128]{1,0:T(8,128)(2,1)S(1)}, bf16[1040,128]{1,0:T(8,128)(2,1)S(1)}, u32[]{:S(2)}, u32[]{:S(2)}) collective-permute-start(bf16[1040,128]{1,0:T(8,128)(2,1)S(1)} %collective-permute-done.4.refs_4_.refs_1_), channel_id=1, source_target_pairs={{0,8},{2,10},{4,12},{6,14},{8,16},{10,18},{12,20},{14,22},{16,24},... | collective-permute-start | bytes 798728 | tf_op jit(solution)/shard_map/ppermute | solution.py:24
  17.7 18.7 %collective-permute-start.3 = (bf16[544,128]{1,0:T(8,128)(2,1)}, bf16[544,128]{1,0:T(8,128)(2,1)S(1)}, u32[]{:S(2)}, u32[]{:S(2)}) collective-permute-start(bf16[544,128]{1,0:T(8,128)(2,1)} %get-tuple-element.24.o_ref), channel_id=1, source_target_pairs={{0,6},{2,0},{4,2},{6,4},{8,14},{10,8},{12,10},{14,12},{16,22},{18,... | collective-permute-start | bytes 417800 | tf_op jit(solution)/shard_map/ppermute | solution.py:30
  20.2 16.2 %collective-permute-start.2 = (bf16[544,128]{1,0:T(8,128)(2,1)}, bf16[544,128]{1,0:T(8,128)(2,1)S(1)}, u32[]{:S(2)}, u32[]{:S(2)}) collective-permute-start(bf16[544,128]{1,0:T(8,128)(2,1)} %get-tuple-element.24.o_ref), channel_id=1, source_target_pairs={{0,4},{2,6},{4,0},{6,2},{8,12},{10,14},{12,8},{14,10},{16,20},{18,... | collective-permute-start | bytes 417800 | tf_op jit(solution)/shard_map/ppermute | solution.py:30
  20.7 15.7 %collective-permute-start.1 = (bf16[544,128]{1,0:T(8,128)(2,1)}, bf16[544,128]{1,0:T(8,128)(2,1)S(1)}, u32[]{:S(2)}, u32[]{:S(2)}) collective-permute-start(bf16[544,128]{1,0:T(8,128)(2,1)} %get-tuple-element.24.o_ref), channel_id=1, source_target_pairs={{0,2},{2,4},{4,6},{6,0},{8,10},{10,12},{12,14},{14,8},{16,18},{18,... | collective-permute-start | bytes 417800 | tf_op jit(solution)/shard_map/ppermute | solution.py:30
  21.3 1.6 %copy-start = (bf16[1,512,2048]{2,1,0:T(8,128)(2,1)S(1)}, bf16[1,512,2048]{2,1,0:T(8,128)(2,1)}, u32[]{:S(2)}) copy-start(bf16[1,512,2048]{2,1,0:T(8,128)(2,1)} %param.9) | copy-start | bytes 6291460
  22.9 0.9 %copy-start.2 = (bf16[1024,128]{1,0:T(8,128)(2,1)S(1)}, bf16[1024,128]{1,0:T(8,128)(2,1)}, u32[]{:S(2)}) copy-start(bf16[1024,128]{1,0:T(8,128)(2,1)} %refs_0_.1) | copy-start | bytes 786436
  23.9 0.7 copy-start.3
  24.5 11.9 %copy-start.5 = (bf16[1040,128]{1,0:T(8,128)(2,1)S(1)}, bf16[1040,128]{1,0:T(8,128)(2,1)}, u32[]{:S(2)}) copy-start(bf16[1040,128]{1,0:T(8,128)(2,1)} %get-tuple-element.25.refs_3_.refs_0_) | copy-start | bytes 798724
  36.5 7.9 %copy-start.6 = (bf16[544,128]{1,0:T(8,128)(2,1)S(1)}, bf16[544,128]{1,0:T(8,128)(2,1)}, u32[]{:S(2)}) copy-start(bf16[544,128]{1,0:T(8,128)(2,1)} %get-tuple-element.24.o_ref) | copy-start | bytes 417796
  41.3 8.4 %copy-start.1 = (bf16[1,512,2048]{2,1,0:T(8,128)(2,1)S(1)}, bf16[1,512,2048]{2,1,0:T(8,128)(2,1)}, u32[]{:S(2)}) copy-start(bf16[1,512,2048]{2,1,0:T(8,128)(2,1)} %param.9) | copy-start | bytes 6291460
  41.3 8.4 %copy-start.4 = (f32[1,128]{1,0:T(1,128)S(1)}, f32[1,128]{1,0:T(1,128)}, u32[]{:S(2)}) copy-start(f32[1,128]{1,0:T(1,128)} %get-tuple-element.21.gain_ref) | copy-start | bytes 1540
  41.3 5.0 %collective-permute-start.6 = (bf16[512,128]{1,0:T(8,128)(2,1)S(1)}, bf16[512,128]{1,0:T(8,128)(2,1)S(1)}, u32[]{:S(2)}, u32[]{:S(2)}) collective-permute-start(bf16[512,128]{1,0:T(8,128)(2,1)S(1)} %get-tuple-element.28), channel_id=1, source_target_pairs={{0,6},{2,0},{4,2},{6,4},{8,14},{10,8},{12,10},{14,12},{16,22},{18,... | collective-permute-start | bytes 393224 | tf_op jit(solution)/shard_map/ppermute | solution.py:30
  42.8 5.0 %collective-permute-start.7 = (bf16[512,128]{1,0:T(8,128)(2,1)S(1)}, bf16[512,128]{1,0:T(8,128)(2,1)S(1)}, u32[]{:S(2)}, u32[]{:S(2)}) collective-permute-start(bf16[512,128]{1,0:T(8,128)(2,1)S(1)} %get-tuple-element.29), channel_id=1, source_target_pairs={{0,4},{2,6},{4,0},{6,2},{8,12},{10,14},{12,8},{14,10},{16,20},{18,... | collective-permute-start | bytes 393224 | tf_op jit(solution)/shard_map/ppermute | solution.py:30
  43.8 5.9 %collective-permute-start.8 = (bf16[512,128]{1,0:T(8,128)(2,1)S(1)}, bf16[512,128]{1,0:T(8,128)(2,1)S(1)}, u32[]{:S(2)}, u32[]{:S(2)}) collective-permute-start(bf16[512,128]{1,0:T(8,128)(2,1)S(1)} %get-tuple-element.30), channel_id=1, source_target_pairs={{0,2},{2,4},{4,6},{6,0},{8,10},{10,12},{12,14},{14,8},{16,18},{18,... | collective-permute-start | bytes 393224 | tf_op jit(solution)/shard_map/ppermute | solution.py:30
  50.3 1.8 %collective-permute-start.11 = (bf16[1024,128]{1,0:T(8,128)(2,1)S(1)}, bf16[1024,128]{1,0:T(8,128)(2,1)S(1)}, u32[]{:S(2)}, u32[]{:S(2)}) collective-permute-start(bf16[1024,128]{1,0:T(8,128)(2,1)S(1)} %get-tuple-element.37), channel_id=1, source_target_pairs={{0,1},{1,0},{2,3},{3,2},{4,5},{5,4},{6,7},{7,6},{8,9},{9,8},{10,11... | collective-permute-start | bytes 786440 | tf_op jit(solution)/shard_map/ppermute | solution.py:421
  50.4 10.6 %collective-permute-start.9 = (bf16[1024,128]{1,0:T(8,128)(2,1)S(1)}, bf16[1024,128]{1,0:T(8,128)(2,1)S(1)}, u32[]{:S(2)}, u32[]{:S(2)}) collective-permute-start(bf16[1024,128]{1,0:T(8,128)(2,1)S(1)} %get-tuple-element.35), channel_id=1, source_target_pairs={{8,0},{10,2},{12,4},{14,6},{16,8},{18,10},{20,12},{22,14},{24,16},... | collective-permute-start | bytes 786440 | tf_op jit(solution)/shard_map/ppermute | solution.py:24
  52.9 17.2 %all-to-all-start = ((bf16[16,64,128]{2,1,0:T(8,128)(2,1)}), bf16[16,64,128]{2,1,0:T(8,128)(2,1)S(1)}, u32[]{:S(2)}, u32[]{:S(2)}) async-start(bf16[16,64,128]{2,1,0:T(8,128)(2,1)} %bitcast.14), calls=%async_computation | async-start | bytes 524288 | tf_op jit(solution)/shard_map/all_to_all | solution.py:453
  61.1 15.4 %collective-permute-start.10 = (bf16[1024,128]{1,0:T(8,128)(2,1)S(1)}, bf16[1024,128]{1,0:T(8,128)(2,1)S(1)}, u32[]{:S(2)}, u32[]{:S(2)}) collective-permute-start(bf16[1024,128]{1,0:T(8,128)(2,1)S(1)} %add_convert_fusion.1), channel_id=1, source_target_pairs={{8,0},{10,2},{12,4},{14,6},{16,8},{18,10},{20,12},{22,14},{24,16},... | collective-permute-start | bytes 786440 | tf_op jit(solution)/shard_map/ppermute | solution.py:24
  70.9 12.6 %all-to-all-start.1 = ((bf16[16,64,128]{2,1,0:T(8,128)(2,1)}), bf16[16,64,128]{2,1,0:T(8,128)(2,1)S(1)}, u32[]{:S(2)}, u32[]{:S(2)}) async-start(bf16[16,64,128]{2,1,0:T(8,128)(2,1)} %sum_and_repeat.1), calls=%async_computation.1 | async-start | bytes 524288 | tf_op jit(solution)/shard_map/all_to_all | solution.py:455

commit v4 on v3

--- a/solution.py
+++ b/solution.py
@@ -154,18 +154,19 @@
     return 0 if k == 0 else jnp.where(r >= k, far, 0)
 
 
-def others_kernel(group, far, tokens, width, r_ref, q_ref, *refs):
-    o_refs, kv_refs = refs[: group - 1], refs[group - 1 : group + far]
-    outs = refs[group + far :]
-    dq_refs, dkv_ref, acc = outs[: group - 1], outs[group - 1], outs[group]
-    kt_sc, docs_sc, k_sc, v_sc = outs[group + 1 :]
+def others_kernel(group, far, tokens, width, r_ref, sums_ref, *refs):
+    q_refs, o_refs = refs[: group - 1], refs[group - 1 : 2 * group - 2]
+    kv_refs = refs[2 * group - 2 : 2 * group + far - 1]
+    outs = refs[2 * group + far - 1 :]
+    dq_refs, dkv_refs = outs[: group - 1], outs[group - 1 : group + far]
+    kt_sc, docs_sc, k_sc, v_sc, acc = outs[group + far :]
     r = r_ref[0]
     scale = width ** (-0.5)
     for s in range(far + 1):
         stage_keys(kv_refs[s], s, tokens, width, k_sc, v_sc, kt_sc, docs_sc, True)
-        acc[s] = jnp.zeros((2 * tokens, width), F32)
+        acc[s] = sums_ref[s] if s < far else jnp.zeros((2 * tokens, width), F32)
     for k in range(1, group):
-        q = q_ref[(r - k + group) % group]
+        q = q_refs[k - 1][...]
         o = o_refs[k - 1][:tokens]
         lse, delta, docs_q = row_data(o_refs[k - 1], tokens, tokens // width)
         dqt = jnp.zeros((width, tokens), F32)
@@ -181,13 +182,14 @@
                 acc[s, rows, :] += dot_nn(dscore, q)
                 dqt += dot_nn(kt_sc[s, :, rows], dscore)
         dq_refs[k - 1][...] = (dqt.T * scale).astype(BF)
-    dkv_ref[:tokens] = (acc[far, :tokens] * scale).astype(BF)
-    dkv_ref[tokens:] = acc[far, tokens:].astype(BF)
-
-
-def own_kernel(far, tokens, width, q_ref, o_ref, acc, *refs):
-    kv_refs, dq_ref, dkv_refs = refs[:far], refs[far], refs[far + 1 : 2 * far + 1]
-    kt_sc, docs_sc, k_sc, v_sc = refs[2 * far + 1 :]
+    for s in range(far + 1):
+        dkv_refs[s][:tokens] = (acc[s, :tokens] * scale).astype(BF)
+        dkv_refs[s][tokens:] = acc[s, tokens:].astype(BF)
+
+
+def own_kernel(far, tokens, width, q_ref, o_ref, *refs):
+    kv_refs, dq_ref, sums_ref = refs[:far], refs[far], refs[far + 1]
+    kt_sc, docs_sc, k_sc, v_sc = refs[far + 2 :]
     scale = width ** (-0.5)
     q = q_ref[...]
     o = o_ref[:tokens]
@@ -201,8 +203,8 @@
             prob, dscore = probabilities(
                 s, rows, c, q, o, lse, delta, docs_q, s == 0, scale, k_sc, v_sc, docs_sc
             )
-            dkv_refs[s][below, :] = (acc[s, below, :] + dot_nn(prob.astype(BF), o)).astype(BF)
-            dkv_refs[s][rows, :] = ((acc[s, rows, :] + dot_nn(dscore, q)) * scale).astype(BF)
+            sums_ref[s, below, :] = dot_nn(prob.astype(BF), o)
+            sums_ref[s, rows, :] = dot_nn(dscore, q)
             dqt += dot_nn(kt_sc[s, :, rows], dscore)
     dq_ref[...] = dqt.T * scale
 
@@ -224,38 +226,37 @@
     )
 
 
-def others(group, far, tokens, width, r, q_all, o_list, kv_list):
+def others(group, far, tokens, width, r, sums, q_list, o_list, kv_list):
     block = jax.ShapeDtypeStruct((tokens, width), BF)
     double = jax.ShapeDtypeStruct((2 * tokens, width), BF)
-    sums = jax.ShapeDtypeStruct((far + 1, 2 * tokens, width), F32)
-    if group == 1:
-        return [], jnp.zeros(double.shape, BF), jnp.zeros(sums.shape, F32)
     out = pl.pallas_call(
         functools.partial(others_kernel, group, far, tokens, width),
-        out_shape=[block] * (group - 1) + [double, sums],
-        in_specs=[pl.BlockSpec(memory_space=pltpu.SMEM)] + vmem_specs(group + far + 1),
-        out_specs=vmem_specs(group + 1),
-        scratch_shapes=key_scratch(far + 1, tokens, width),
+        out_shape=[block] * (group - 1) + [double] * (far + 1),
+        in_specs=[pl.BlockSpec(memory_space=pltpu.SMEM)] + vmem_specs(2 * group + far),
+        out_specs=vmem_specs(group + far),
+        scratch_shapes=key_scratch(far + 1, tokens, width)
+        + [pltpu.VMEM((far + 1, 2 * tokens, width), F32)],
         compiler_params=params(ATTENTION_MIB),
-        cost_estimate=cost((group - 1) * far, tokens, width),
+        cost_estimate=cost(max(1, (group - 1) * far), tokens, width),
         name="others",
-    )(r, q_all, *o_list[1:], *kv_list)
-    return out[: group - 1], out[group - 1], out[group]
-
-
-def own(far, tokens, width, query, o_own, acc, kv_list):
-    out = pl.pallas_call(
+    )(r, sums, *q_list[1:], *o_list[1:], *kv_list)
+    return out[: group - 1], out[group - 1 :]
+
+
+def own(far, tokens, width, query, o_own, kv_list):
+    return pl.pallas_call(
         functools.partial(own_kernel, far, tokens, width),
-        out_shape=[jax.ShapeDtypeStruct((tokens, width), F32)]
-        + [jax.ShapeDtypeStruct((2 * tokens, width), BF)] * far,
-        in_specs=vmem_specs(far + 3),
-        out_specs=vmem_specs(far + 1),
+        out_shape=[
+            jax.ShapeDtypeStruct((tokens, width), F32),
+            jax.ShapeDtypeStruct((far, 2 * tokens, width), F32),
+        ],
+        in_specs=vmem_specs(far + 2),
+        out_specs=vmem_specs(2),
         scratch_shapes=key_scratch(far, tokens, width),
         compiler_params=params(ATTENTION_MIB),
         cost_estimate=cost(far, tokens, width),
         name="own",
-    )(query, o_own, acc, *kv_list[:far])
-    return out[0], out[1:]
+    )(query, o_own, *kv_list[:far])
 
 
 def pre_kernel(parts, halves, f_ref, h_ref, q_pre_ref, gain_ref, own_ref, *refs):
@@ -393,14 +394,14 @@
         compiler_params=params(8),
         name="query",
     )(f, inputs, gain, *w_parts)
-    groups = [list(range(i, i + group)) for i in range(0, blocks, group)]
-    q_all = lax.all_gather(query, "blk", axis_index_groups=groups)
-
-    dq_list, grad_kv, acc = others(group, far, tokens, width, r, q_all, o_list, kv_list)
+    q_list = [query] + [turned(query, k, group) for k in range(1, group)]
+    dq_own, sums = own(far, tokens, width, query, o_own, kv_list)
+    dq_list, dkv_list = others(
+        group, far, tokens, width, r, sums, q_list, o_list, kv_list
+    )
 
     dq_back = [turned(dq_list[k - 1], -k, group) for k in range(1, group)]
-    back = shifted(grad_kv, -group)
-    dq_own, dkv_list = own(far, tokens, width, query, o_own, acc, kv_list)
+    back = shifted(dkv_list[far], -group)
     owned = inputs.shape[1] // halves
     smem = [pl.BlockSpec(memory_space=pltpu.SMEM)]
     block = jax.ShapeDtypeStruct((tokens, width), BF)

time: 84.8 us -> 79.7 us (0.940)
  blocking collectives: 11.1 us -> 0 us
  starting transfers between devices: 28.7 us -> 33.6 us
  waiting for transfers between devices: 25.1 us -> 26 us
    all_gather x1 -> x0, blocking collectives: 11.1 us -> none  [step(): q_all = lax.all_gather(query, 'blk', axis_index_groups=groups)]
    ppermute x6 -> x9, starting transfers between devices: 6.71 us -> 11.2 us  [turned(): return lax.ppermute(value, 'blk', pairs)]
    ppermute x6 -> x9, waiting for transfers between devices: 3.65 us -> 7.65 us  [turned(): return lax.ppermute(value, 'blk', pairs)]
    ppermute x4, waiting for transfers between devices: 7.44 us -> 4.03 us  [shifted(): return lax.ppermute(value, 'blk', pairs)]
  transfers between devices with their start and end apart: 14 -> 17, of which waited for: 7 -> 10; matrix products, arithmetic and copies ran while one was open for 3% -> 4% of each run, Pallas kernels for 5% -> 6%
where the time goes in v4:
time: 79.7 us; the launch traced here: 79.1 us
  starting transfers between devices  33.6 us (42%)
  waiting for transfers between devices  26 us (33%)
  Pallas kernels  11.7 us (15%)
  local copies, waits for them, and re-layouts  3.93 us (5%)
  matrix products  2.03 us (3%)
  other arithmetic  0.99 us (1%)
    ppermute x4, starting transfers between devices, shifted(): return lax.ppermute(value, 'blk', pairs)  11.8 us
    ppermute x9, starting transfers between devices, turned(): return lax.ppermute(value, 'blk', pairs)  11.2 us
    all_to_all x1, waiting for transfers between devices, step(): got = lax.all_to_all(terms, 'blk', 0, 0, tiled=True)  8.16 us
    ppermute x9, waiting for transfers between devices, turned(): return lax.ppermute(value, 'blk', pairs)  7.65 us
    all_to_all x1, starting transfers between devices, step(): got = lax.all_to_all(terms, 'blk', 0, 0, tiled=True)  6.92 us
    all_to_all x1, waiting for transfers between devices, step(): lax.all_to_all(everywhere.reshape(-1, width), 'blk', 0, 0, tiled=True)  6.2 us
    pallas_call x1, Pallas kernels, others(): pl.pallas_call(functools.partial(others_kernel, group, far, tokens, width...  4.86 us
    ppermute x4, waiting for transfers between devices, shifted(): return lax.ppermute(value, 'blk', pairs)  4.03 us
  transfers between devices with their start and end apart: 17, of which 10 were waited for; matrix products, arithmetic and copies ran while one was open for 4% of the time, Pallas kernels for 6%

profile of v4, /device:TPU:0, one launch (start us, length us, event | category | flops | bytes accessed | tf_op | source)
XLA Modules:
  0.0 79.1 jit_solution(17887966511065258415)
XLA Ops:
  0.6 1.9 %pack.1 = (bf16[1040,128]{1,0:T(8,128)(2,1)}, bf16[544,128]{1,0:T(8,128)(2,1)}, f32[1,128]{1,0:T(1,128)}) custom-call(bf16[512,128]{1,0:T(8,128)(2,1)} %bitcast.25, bf16[512,128]{1,0:T(8,128)(2,1)} %bitcast.26, bf16[512,128]{1,0:T(8,128)(2,1)} %bitcast.27, f32[4,128]{1,0:T(4,128)} %bitcast.28, f32[4,128]{1,0:T(4,128)} %bitcast.29, s32[4,128]{1,0:T(4,128)} %bitcast.30, ...), custom_call_target="tpu_custom_call" | custom-call | tf_op jit(solution)/shard_map/pack/pallas_call | solution.py:353
  2.5 5.0 %collective-permute-start.1 = (bf16[1040,128]{1,0:T(8,128)(2,1)}, bf16[1040,128]{1,0:T(8,128)(2,1)S(1)}, u32[]{:S(2)}, u32[]{:S(2)}) collective-permute-start(bf16[1040,128]{1,0:T(8,128)(2,1)} %get-tuple-element.25.refs_0_.refs_6_), channel_id=1, source_target_pairs={{0,8},{2,10},{4,12},{6,14},{8,16},{10,18},{12,20},{14,22},{16,24},... | collective-permute-start | bytes 798728 | tf_op jit(solution)/shard_map/ppermute | solution.py:24
  7.5 0.1 collective-permute-start
  7.6 2.5 %collective-permute-start.7 = (bf16[544,128]{1,0:T(8,128)(2,1)}, bf16[544,128]{1,0:T(8,128)(2,1)S(1)}, u32[]{:S(2)}, u32[]{:S(2)}) collective-permute-start(bf16[544,128]{1,0:T(8,128)(2,1)} %get-tuple-element.24.o_ref), channel_id=1, source_target_pairs={{0,6},{2,0},{4,2},{6,4},{8,14},{10,8},{12,10},{14,12},{16,22},{18,... | collective-permute-start | bytes 417800 | tf_op jit(solution)/shard_map/ppermute | solution.py:30
  10.1 0.5 collective-permute-start.6
  10.6 2.8 %collective-permute-done.1.refs_1_.refs_7_ = bf16[1040,128]{1,0:T(8,128)(2,1)S(1)} collective-permute-done((bf16[1040,128]{1,0:T(8,128)(2,1)}, bf16[1040,128]{1,0:T(8,128)(2,1)S(1)}, u32[]{:S(2)}, u32[]{:S(2)}) %collective-permute-start.1) | collective-permute-done | bytes 266272 | tf_op jit(solution)/shard_map/ppermute | solution.py:24
  13.4 4.3 %collective-permute-start.8 = (bf16[1040,128]{1,0:T(8,128)(2,1)S(1)}, bf16[1040,128]{1,0:T(8,128)(2,1)S(1)}, u32[]{:S(2)}, u32[]{:S(2)}) collective-permute-start(bf16[1040,128]{1,0:T(8,128)(2,1)S(1)} %collective-permute-done.1.refs_1_.refs_7_), channel_id=1, source_target_pairs={{0,8},{2,10},{4,12},{6,14},{8,16},{10,18},{12,20},{14,22},{16,24},... | collective-permute-start | bytes 798728 | tf_op jit(solution)/shard_map/ppermute | solution.py:24
  17.7 1.5 %collective-permute-start.5 = (bf16[544,128]{1,0:T(8,128)(2,1)}, bf16[544,128]{1,0:T(8,128)(2,1)S(1)}, u32[]{:S(2)}, u32[]{:S(2)}) collective-permute-start(bf16[544,128]{1,0:T(8,128)(2,1)} %get-tuple-element.24.o_ref), channel_id=1, source_target_pairs={{0,2},{2,4},{4,6},{6,0},{8,10},{10,12},{12,14},{14,8},{16,18},{18,... | collective-permute-start | bytes 417800 | tf_op jit(solution)/shard_map/ppermute | solution.py:30
  19.3 0.0 collective-permute-done.refs_1_
  19.3 1.6 %copy-done = bf16[1,512,2048]{2,1,0:T(8,128)(2,1)S(1)} copy-done((bf16[1,512,2048]{2,1,0:T(8,128)(2,1)S(1)}, bf16[1,512,2048]{2,1,0:T(8,128)(2,1)}, u32[]{:S(2)}) %copy-start) | copy-done | bytes 2097176
  20.9 0.9 %copy-done.2 = bf16[1024,128]{1,0:T(8,128)(2,1)S(1)} copy-done((bf16[1024,128]{1,0:T(8,128)(2,1)S(1)}, bf16[1024,128]{1,0:T(8,128)(2,1)}, u32[]{:S(2)}) %copy-start.2) | copy-done | bytes 262168
  21.8 0.7 copy-done.3
  22.5 0.8 %query.1 = (bf16[512,128]{1,0:T(8,128)(2,1)S(1)}, f32[512,128]{1,0:T(8,128)S(1)}, bf16[2048,128]{1,0:T(8,128)(2,1)S(1)}) custom-call(s32[1]{0:T(128)} %bitcast.f_ref, bf16[512,2048]{1,0:T(8,128)(2,1)S(1)} %bitcast.22, f32[1,128]{1,0:T(1,128)S(1)} %copy-done.3, bf16[1024,128]{1,0:T(8,128)(2,1)S(1)} %copy-done.2, ...), custom_call_target="tpu_custom_call" | custom-call | tf_op jit(solution)/shard_map/query/pallas_call | solution.py:387
  23.3 1.5 %collective-permute-start.4 = (bf16[512,128]{1,0:T(8,128)(2,1)S(1)}, bf16[512,128]{1,0:T(8,128)(2,1)S(1)}, u32[]{:S(2)}, u32[]{:S(2)}) collective-permute-start(bf16[512,128]{1,0:T(8,128)(2,1)S(1)} %get-tuple-element.23.q_ref), channel_id=1, source_target_pairs={{0,6},{2,0},{4,2},{6,4},{8,14},{10,8},{12,10},{14,12},{16,22},{18,... | collective-permute-start | bytes 393224 | tf_op jit(solution)/shard_map/ppermute | solution.py:30
  24.8 1.5 %collective-permute-start.3 = (bf16[512,128]{1,0:T(8,128)(2,1)S(1)}, bf16[512,128]{1,0:T(8,128)(2,1)S(1)}, u32[]{:S(2)}, u32[]{:S(2)}) collective-permute-start(bf16[512,128]{1,0:T(8,128)(2,1)S(1)} %get-tuple-element.23.q_ref), channel_id=1, source_target_pairs={{0,4},{2,6},{4,0},{6,2},{8,12},{10,14},{12,8},{14,10},{16,20},{18,... | collective-permute-start | bytes 393224 | tf_op jit(solution)/shard_map/ppermute | solution.py:30
  26.3 0.6 collective-permute-start.2
  26.9 1.6 %own.1 = (f32[512,128]{1,0:T(8,128)S(1)}, f32[2,1024,128]{2,1,0:T(8,128)S(1)}) custom-call(bf16[512,128]{1,0:T(8,128)(2,1)S(1)} %get-tuple-element.23.q_ref, bf16[544,128]{1,0:T(8,128)(2,1)S(1)} %copy-done.6, bf16[1040,128]{1,0:T(8,128)(2,1)S(1)} %copy-done.5, bf16[1040,128]{1,0:T(8,128)(2,1)S(1)} %collective-permute-done.1.refs_1_.refs_7_), custom_call_target="tpu_custom_call" | custom-call | flops 671088640 | bytes 1048576 | tf_op jit(solution)/shard_map/own/pallas_call | solution.py:247
  28.6 0.0 collective-permute-done.5.refs_3_
  28.6 0.9 %collective-permute-done.4.refs_2_ = bf16[512,128]{1,0:T(8,128)(2,1)S(1)} collective-permute-done((bf16[512,128]{1,0:T(8,128)(2,1)S(1)}, bf16[512,128]{1,0:T(8,128)(2,1)S(1)}, u32[]{:S(2)}, u32[]{:S(2)}) %collective-permute-start.4) | collective-permute-done | bytes 131104 | tf_op jit(solution)/shard_map/ppermute | solution.py:30
  29.5 1.2 %collective-permute-done.3.refs_1_ = bf16[512,128]{1,0:T(8,128)(2,1)S(1)} collective-permute-done((bf16[512,128]{1,0:T(8,128)(2,1)S(1)}, bf16[512,128]{1,0:T(8,128)(2,1)S(1)}, u32[]{:S(2)}, u32[]{:S(2)}) %collective-permute-start.3) | collective-permute-done | bytes 131104 | tf_op jit(solution)/shard_map/ppermute | solution.py:30
  30.7 1.5 %collective-permute-done.2.refs_0_ = bf16[512,128]{1,0:T(8,128)(2,1)S(1)} collective-permute-done((bf16[512,128]{1,0:T(8,128)(2,1)S(1)}, bf16[512,128]{1,0:T(8,128)(2,1)S(1)}, u32[]{:S(2)}, u32[]{:S(2)}) %collective-permute-start.2) | collective-permute-done | bytes 131104 | tf_op jit(solution)/shard_map/ppermute | solution.py:30
  32.2 0.0 collective-permute-done.8.refs_8_
  32.2 4.9 %others.1 = (bf16[512,128]{1,0:T(8,128)(2,1)S(1)}, bf16[512,128]{1,0:T(8,128)(2,1)S(1)}, bf16[512,128]{1,0:T(8,128)(2,1)S(1)}, bf16[1024,128]{1,0:T(8,128)(2,1)S...) custom-call(s32[1]{0:T(128)} %bitcast.9.r_ref, f32[2,1024,128]{2,1,0:T(8,128)S(1)} %get-tuple-element.27.sums_ref, ...), custom_call_target="tpu_custom_call" | custom-call | flops 2013265920 | bytes 3145728 | tf_op jit(solution)/shard_map/others/pallas_call | solution.py:232
  37.1 0.3 collective-permute-start.9
  37.4 0.9 %collective-permute-start.10 = (bf16[512,128]{1,0:T(8,128)(2,1)S(1)}, bf16[512,128]{1,0:T(8,128)(2,1)S(1)}, u32[]{:S(2)}, u32[]{:S(2)}) collective-permute-start(bf16[512,128]{1,0:T(8,128)(2,1)S(1)} %get-tuple-element.29), channel_id=1, source_target_pairs={{0,4},{2,6},{4,0},{6,2},{8,12},{10,14},{12,8},{14,10},{16,20},{18,... | collective-permute-start | bytes 393224 | tf_op jit(solution)/shard_map/ppermute | solution.py:30
  38.3 1.8 %collective-permute-start.11 = (bf16[512,128]{1,0:T(8,128)(2,1)S(1)}, bf16[512,128]{1,0:T(8,128)(2,1)S(1)}, u32[]{:S(2)}, u32[]{:S(2)}) collective-permute-start(bf16[512,128]{1,0:T(8,128)(2,1)S(1)} %get-tuple-element.30), channel_id=1, source_target_pairs={{0,2},{2,4},{4,6},{6,0},{8,10},{10,12},{12,14},{14,8},{16,18},{18,... | collective-permute-start | bytes 393224 | tf_op jit(solution)/shard_map/ppermute | solution.py:30
  40.1 2.0 %collective-permute-done.9.refs_0_ = bf16[512,128]{1,0:T(8,128)(2,1)S(1)} collective-permute-done((bf16[512,128]{1,0:T(8,128)(2,1)S(1)}, bf16[512,128]{1,0:T(8,128)(2,1)S(1)}, u32[]{:S(2)}, u32[]{:S(2)}) %collective-permute-start.9) | collective-permute-done | bytes 131104 | tf_op jit(solution)/shard_map/ppermute | solution.py:30
  42.1 0.3 collective-permute-done.10.refs_1_
  42.4 1.8 %collective-permute-done.11.refs_2_ = bf16[512,128]{1,0:T(8,128)(2,1)S(1)} collective-permute-done((bf16[512,128]{1,0:T(8,128)(2,1)S(1)}, bf16[512,128]{1,0:T(8,128)(2,1)S(1)}, u32[]{:S(2)}, u32[]{:S(2)}) %collective-permute-start.11) | collective-permute-done | bytes 131104 | tf_op jit(solution)/shard_map/ppermute | solution.py:30
  44.1 0.6 give_term.1
  44.8 0.1 collective-permute-start.14
  44.8 1.3 %collective-permute-start.12 = (bf16[1024,128]{1,0:T(8,128)(2,1)S(1)}, bf16[1024,128]{1,0:T(8,128)(2,1)S(1)}, u32[]{:S(2)}, u32[]{:S(2)}) collective-permute-start(bf16[1024,128]{1,0:T(8,128)(2,1)S(1)} %get-tuple-element.35), channel_id=1, source_target_pairs={{8,0},{10,2},{12,4},{14,6},{16,8},{18,10},{20,12},{22,14},{24,16},... | collective-permute-start | bytes 786440 | tf_op jit(solution)/shard_map/ppermute | solution.py:24
  46.1 0.4 keep_term.1.keep_ref
  46.6 0.0 collective-permute-done.14.refs_0_
  46.6 0.7 add_terms.1
  47.3 6.9 %all-to-all-start = ((bf16[16,64,128]{2,1,0:T(8,128)(2,1)}), bf16[16,64,128]{2,1,0:T(8,128)(2,1)S(1)}, u32[]{:S(2)}, u32[]{:S(2)}) async-start(bf16[16,64,128]{2,1,0:T(8,128)(2,1)} %bitcast.13), calls=%async_computation | async-start | bytes 524288 | tf_op jit(solution)/shard_map/all_to_all | solution.py:454
  54.2 1.2 %collective-permute-done.12 = bf16[1024,128]{1,0:T(8,128)(2,1)S(1)} collective-permute-done((bf16[1024,128]{1,0:T(8,128)(2,1)S(1)}, bf16[1024,128]{1,0:T(8,128)(2,1)S(1)}, u32[]{:S(2)}, u32[]{:S(2)}) %collective-permute-start.12) | collective-permute-done | bytes 262176 | tf_op jit(solution)/shard_map/ppermute | solution.py:24
  55.4 0.1 add_convert_fusion.1
  55.5 1.3 %collective-permute-start.13 = (bf16[1024,128]{1,0:T(8,128)(2,1)S(1)}, bf16[1024,128]{1,0:T(8,128)(2,1)S(1)}, u32[]{:S(2)}, u32[]{:S(2)}) collective-permute-start(bf16[1024,128]{1,0:T(8,128)(2,1)S(1)} %add_convert_fusion.1), channel_id=1, source_target_pairs={{8,0},{10,2},{12,4},{14,6},{16,8},{18,10},{20,12},{22,14},{24,16},... | collective-permute-start | bytes 786440 | tf_op jit(solution)/shard_map/ppermute | solution.py:24
  56.8 8.2 %all-to-all-done.got_ref = bf16[16,64,128]{2,1,0:T(8,128)(2,1)S(1)} async-done(((bf16[16,64,128]{2,1,0:T(8,128)(2,1)}), bf16[16,64,128]{2,1,0:T(8,128)(2,1)S(1)}, u32[]{:S(2)}, u32[]{:S(2)}) %all-to-all-start) | async-done | bytes 262176 | tf_op jit(solution)/shard_map/all_to_all | solution.py:454
  65.0 0.8 sum_and_repeat.1
  65.7 3.5 %all-to-all-start.1 = ((bf16[16,64,128]{2,1,0:T(8,128)(2,1)}), bf16[16,64,128]{2,1,0:T(8,128)(2,1)S(1)}, u32[]{:S(2)}, u32[]{:S(2)}) async-start(bf16[16,64,128]{2,1,0:T(8,128)(2,1)} %sum_and_repeat.1), calls=%async_computation.1 | async-start | bytes 524288 | tf_op jit(solution)/shard_map/all_to_all | solution.py:456
  69.3 2.0 %fusion = bf16[1,512,2048]{2,1,0:T(8,128)(2,1)} fusion(bf16[512,128]{1,0:T(8,128)(2,1)S(1)} %get-tuple-element.31, bf16[2048,128]{1,0:T(8,128)(2,1)S(1)} %get-tuple-element.32), kind=kOutput, calls=%fused_computation.1 | convolution fusion | flops 269484032 | bytes 2752512 | tf_op jit(solution)/shard_map/dot_general | solution.py:42
  71.3 0.0 collective-permute-done.13
  71.3 0.1 add_convert_fusion
  71.4 0.7 slice_bitcast_fusion
  72.1 6.2 %all-to-all-done.1 = bf16[16,64,128]{2,1,0:T(8,128)(2,1)S(1)} async-done(((bf16[16,64,128]{2,1,0:T(8,128)(2,1)}), bf16[16,64,128]{2,1,0:T(8,128)(2,1)S(1)}, u32[]{:S(2)}, u32[]{:S(2)}) %all-to-all-start.1) | async-done | bytes 262176 | tf_op jit(solution)/shard_map/all_to_all | solution.py:456
  78.3 0.8 %bitcast_convert_fusion = f32[1024,128]{1,0:T(8,128)} fusion(bf16[16,64,128]{2,1,0:T(8,128)(2,1)S(1)} %all-to-all-done.1), kind=kLoop, calls=%fused_computation.4 | loop fusion | flops 131072 | bytes 786432 | tf_op jit(solution)/shard_map/convert_element_type | solution.py:457
  (13 shorter events, 0.0 us)
Async XLA Ops:
  2.5 10.9 %collective-permute-start.1 = (bf16[1040,128]{1,0:T(8,128)(2,1)}, bf16[1040,128]{1,0:T(8,128)(2,1)S(1)}, u32[]{:S(2)}, u32[]{:S(2)}) collective-permute-start(bf16[1040,128]{1,0:T(8,128)(2,1)} %get-tuple-element.25.refs_0_.refs_6_), channel_id=1, source_target_pairs={{0,8},{2,10},{4,12},{6,14},{8,16},{10,18},{12,20},{14,22},{16,24},... | collective-permute-start | bytes 798728 | tf_op jit(solution)/shard_map/ppermute | solution.py:24
  7.5 11.8 %collective-permute-start = (bf16[1024,128]{1,0:T(8,128)(2,1)}, bf16[1024,128]{1,0:T(8,128)(2,1)S(1)}, u32[]{:S(2)}, u32[]{:S(2)}) collective-permute-start(bf16[1024,128]{1,0:T(8,128)(2,1)} %refs_0_.1), channel_id=1, source_target_pairs={{0,1},{1,0},{2,3},{3,2},{4,5},{5,4},{6,7},{7,6},{8,9},{9,8},{10,11... | collective-permute-start | bytes 786440 | tf_op jit(solution)/shard_map/ppermute | solution.py:350
  7.6 17.2 %collective-permute-start.7 = (bf16[544,128]{1,0:T(8,128)(2,1)}, bf16[544,128]{1,0:T(8,128)(2,1)S(1)}, u32[]{:S(2)}, u32[]{:S(2)}) collective-permute-start(bf16[544,128]{1,0:T(8,128)(2,1)} %get-tuple-element.24.o_ref), channel_id=1, source_target_pairs={{0,6},{2,0},{4,2},{6,4},{8,14},{10,8},{12,10},{14,12},{16,22},{18,... | collective-permute-start | bytes 417800 | tf_op jit(solution)/shard_map/ppermute | solution.py:30
  10.1 16.2 %collective-permute-start.6 = (bf16[544,128]{1,0:T(8,128)(2,1)}, bf16[544,128]{1,0:T(8,128)(2,1)S(1)}, u32[]{:S(2)}, u32[]{:S(2)}) collective-permute-start(bf16[544,128]{1,0:T(8,128)(2,1)} %get-tuple-element.24.o_ref), channel_id=1, source_target_pairs={{0,4},{2,6},{4,0},{6,2},{8,12},{10,14},{12,8},{14,10},{16,20},{18,... | collective-permute-start | bytes 417800 | tf_op jit(solution)/shard_map/ppermute | solution.py:30
  13.4 18.7 %collective-permute-start.8 = (bf16[1040,128]{1,0:T(8,128)(2,1)S(1)}, bf16[1040,128]{1,0:T(8,128)(2,1)S(1)}, u32[]{:S(2)}, u32[]{:S(2)}) collective-permute-start(bf16[1040,128]{1,0:T(8,128)(2,1)S(1)} %collective-permute-done.1.refs_1_.refs_7_), channel_id=1, source_target_pairs={{0,8},{2,10},{4,12},{6,14},{8,16},{10,18},{12,20},{14,22},{16,24},... | collective-permute-start | bytes 798728 | tf_op jit(solution)/shard_map/ppermute | solution.py:24
  17.7 10.8 %collective-permute-start.5 = (bf16[544,128]{1,0:T(8,128)(2,1)}, bf16[544,128]{1,0:T(8,128)(2,1)S(1)}, u32[]{:S(2)}, u32[]{:S(2)}) collective-permute-start(bf16[544,128]{1,0:T(8,128)(2,1)} %get-tuple-element.24.o_ref), channel_id=1, source_target_pairs={{0,2},{2,4},{4,6},{6,0},{8,10},{10,12},{12,14},{14,8},{16,18},{18,... | collective-permute-start | bytes 417800 | tf_op jit(solution)/shard_map/ppermute | solution.py:30
  19.3 1.6 %copy-start = (bf16[1,512,2048]{2,1,0:T(8,128)(2,1)S(1)}, bf16[1,512,2048]{2,1,0:T(8,128)(2,1)}, u32[]{:S(2)}) copy-start(bf16[1,512,2048]{2,1,0:T(8,128)(2,1)} %param.9) | copy-start | bytes 6291460
  20.9 0.9 %copy-start.2 = (bf16[1024,128]{1,0:T(8,128)(2,1)S(1)}, bf16[1024,128]{1,0:T(8,128)(2,1)}, u32[]{:S(2)}) copy-start(bf16[1024,128]{1,0:T(8,128)(2,1)} %refs_0_.1) | copy-start | bytes 786436
  21.8 0.7 copy-start.3
  22.5 4.4 %copy-start.5 = (bf16[1040,128]{1,0:T(8,128)(2,1)S(1)}, bf16[1040,128]{1,0:T(8,128)(2,1)}, u32[]{:S(2)}) copy-start(bf16[1040,128]{1,0:T(8,128)(2,1)} %get-tuple-element.25.refs_0_.refs_6_) | copy-start | bytes 798724
  22.5 4.4 %copy-start.6 = (bf16[544,128]{1,0:T(8,128)(2,1)S(1)}, bf16[544,128]{1,0:T(8,128)(2,1)}, u32[]{:S(2)}) copy-start(bf16[544,128]{1,0:T(8,128)(2,1)} %get-tuple-element.24.o_ref) | copy-start | bytes 417796
  23.3 6.2 %collective-permute-start.4 = (bf16[512,128]{1,0:T(8,128)(2,1)S(1)}, bf16[512,128]{1,0:T(8,128)(2,1)S(1)}, u32[]{:S(2)}, u32[]{:S(2)}) collective-permute-start(bf16[512,128]{1,0:T(8,128)(2,1)S(1)} %get-tuple-element.23.q_ref), channel_id=1, source_target_pairs={{0,6},{2,0},{4,2},{6,4},{8,14},{10,8},{12,10},{14,12},{16,22},{18,... | collective-permute-start | bytes 393224 | tf_op jit(solution)/shard_map/ppermute | solution.py:30
  24.8 5.9 %collective-permute-start.3 = (bf16[512,128]{1,0:T(8,128)(2,1)S(1)}, bf16[512,128]{1,0:T(8,128)(2,1)S(1)}, u32[]{:S(2)}, u32[]{:S(2)}) collective-permute-start(bf16[512,128]{1,0:T(8,128)(2,1)S(1)} %get-tuple-element.23.q_ref), channel_id=1, source_target_pairs={{0,4},{2,6},{4,0},{6,2},{8,12},{10,14},{12,8},{14,10},{16,20},{18,... | collective-permute-start | bytes 393224 | tf_op jit(solution)/shard_map/ppermute | solution.py:30
  26.3 5.9 %collective-permute-start.2 = (bf16[512,128]{1,0:T(8,128)(2,1)S(1)}, bf16[512,128]{1,0:T(8,128)(2,1)S(1)}, u32[]{:S(2)}, u32[]{:S(2)}) collective-permute-start(bf16[512,128]{1,0:T(8,128)(2,1)S(1)} %get-tuple-element.23.q_ref), channel_id=1, source_target_pairs={{0,2},{2,4},{4,6},{6,0},{8,10},{10,12},{12,14},{14,8},{16,18},{18,... | collective-permute-start | bytes 393224 | tf_op jit(solution)/shard_map/ppermute | solution.py:30
  32.2 12.0 %copy-start.1 = (bf16[1,512,2048]{2,1,0:T(8,128)(2,1)S(1)}, bf16[1,512,2048]{2,1,0:T(8,128)(2,1)}, u32[]{:S(2)}) copy-start(bf16[1,512,2048]{2,1,0:T(8,128)(2,1)} %param.9) | copy-start | bytes 6291460
  32.2 12.0 %copy-start.4 = (f32[1,128]{1,0:T(1,128)S(1)}, f32[1,128]{1,0:T(1,128)}, u32[]{:S(2)}) copy-start(f32[1,128]{1,0:T(1,128)} %get-tuple-element.21.gain_ref) | copy-start | bytes 1540
  37.1 5.0 %collective-permute-start.9 = (bf16[512,128]{1,0:T(8,128)(2,1)S(1)}, bf16[512,128]{1,0:T(8,128)(2,1)S(1)}, u32[]{:S(2)}, u32[]{:S(2)}) collective-permute-start(bf16[512,128]{1,0:T(8,128)(2,1)S(1)} %get-tuple-element.28), channel_id=1, source_target_pairs={{0,6},{2,0},{4,2},{6,4},{8,14},{10,8},{12,10},{14,12},{16,22},{18,... | collective-permute-start | bytes 393224 | tf_op jit(solution)/shard_map/ppermute | solution.py:30
  37.4 5.0 %collective-permute-start.10 = (bf16[512,128]{1,0:T(8,128)(2,1)S(1)}, bf16[512,128]{1,0:T(8,128)(2,1)S(1)}, u32[]{:S(2)}, u32[]{:S(2)}) collective-permute-start(bf16[512,128]{1,0:T(8,128)(2,1)S(1)} %get-tuple-element.29), channel_id=1, source_target_pairs={{0,4},{2,6},{4,0},{6,2},{8,12},{10,14},{12,8},{14,10},{16,20},{18,... | collective-permute-start | bytes 393224 | tf_op jit(solution)/shard_map/ppermute | solution.py:30
  38.3 5.9 %collective-permute-start.11 = (bf16[512,128]{1,0:T(8,128)(2,1)S(1)}, bf16[512,128]{1,0:T(8,128)(2,1)S(1)}, u32[]{:S(2)}, u32[]{:S(2)}) collective-permute-start(bf16[512,128]{1,0:T(8,128)(2,1)S(1)} %get-tuple-element.30), channel_id=1, source_target_pairs={{0,2},{2,4},{4,6},{6,0},{8,10},{10,12},{12,14},{14,8},{16,18},{18,... | collective-permute-start | bytes 393224 | tf_op jit(solution)/shard_map/ppermute | solution.py:30
  44.8 1.8 %collective-permute-start.14 = (bf16[1024,128]{1,0:T(8,128)(2,1)S(1)}, bf16[1024,128]{1,0:T(8,128)(2,1)S(1)}, u32[]{:S(2)}, u32[]{:S(2)}) collective-permute-start(bf16[1024,128]{1,0:T(8,128)(2,1)S(1)} %get-tuple-element.37), channel_id=1, source_target_pairs={{0,1},{1,0},{2,3},{3,2},{4,5},{5,4},{6,7},{7,6},{8,9},{9,8},{10,11... | collective-permute-start | bytes 786440 | tf_op jit(solution)/shard_map/ppermute | solution.py:422
  44.8 10.6 %collective-permute-start.12 = (bf16[1024,128]{1,0:T(8,128)(2,1)S(1)}, bf16[1024,128]{1,0:T(8,128)(2,1)S(1)}, u32[]{:S(2)}, u32[]{:S(2)}) collective-permute-start(bf16[1024,128]{1,0:T(8,128)(2,1)S(1)} %get-tuple-element.35), channel_id=1, source_target_pairs={{8,0},{10,2},{12,4},{14,6},{16,8},{18,10},{20,12},{22,14},{24,16},... | collective-permute-start | bytes 786440 | tf_op jit(solution)/shard_map/ppermute | solution.py:24
  47.3 17.6 %all-to-all-start = ((bf16[16,64,128]{2,1,0:T(8,128)(2,1)}), bf16[16,64,128]{2,1,0:T(8,128)(2,1)S(1)}, u32[]{:S(2)}, u32[]{:S(2)}) async-start(bf16[16,64,128]{2,1,0:T(8,128)(2,1)} %bitcast.13), calls=%async_computation | async-start | bytes 524288 | tf_op jit(solution)/shard_map/all_to_all | solution.py:454
  55.5 15.8 %collective-permute-start.13 = (bf16[1024,128]{1,0:T(8,128)(2,1)S(1)}, bf16[1024,128]{1,0:T(8,128)(2,1)S(1)}, u32[]{:S(2)}, u32[]{:S(2)}) collective-permute-start(bf16[1024,128]{1,0:T(8,128)(2,1)S(1)} %add_convert_fusion.1), channel_id=1, source_target_pairs={{8,0},{10,2},{12,4},{14,6},{16,8},{18,10},{20,12},{22,14},{24,16},... | collective-permute-start | bytes 786440 | tf_op jit(solution)/shard_map/ppermute | solution.py:24
  65.7 12.6 %all-to-all-start.1 = ((bf16[16,64,128]{2,1,0:T(8,128)(2,1)}), bf16[16,64,128]{2,1,0:T(8,128)(2,1)S(1)}, u32[]{:S(2)}, u32[]{:S(2)}) async-start(bf16[16,64,128]{2,1,0:T(8,128)(2,1)} %sum_and_repeat.1), calls=%async_computation.1 | async-start | bytes 524288 | tf_op jit(solution)/shard_map/all_to_all | solution.py:456
